TPU v7x, 128 devices: a whole 4x4x4 slice. The times are simulated.
128 devices in a mesh: expert: 8 (over x, core), tile: 16 (over z, y).
Axes of the slice: x: 4, y: 4, z: 4, core: 2. Of those that a mesh axis runs over, the one named last changes fastest.
Arguments:
- weight: bfloat16 [8, 2048, 8192], P('expert', None, 'tile'), may hold values from -6 to 6
- grad: bfloat16 [8, 2048, 8192], P('expert', None, 'tile'), may hold values from -24 to 24, as said below
- first_moment: float32 [8, 2048, 8192], P('expert', None, 'tile'), may hold values from -6 to 6
- second_moment: float32 [8, 2048, 8192], P('expert', None, 'tile'), may hold values from 0.25 to 4
- left_basis: bfloat16 [8, 1024, 2048], P('expert', None, 'tile'), may hold values from -1 to 1, as said below
- right_basis: bfloat16 [8, 1024, 8192], P('expert', None, 'tile'), may hold values from -1 to 1, as said below
Outputs:
- new_weight: bfloat16 [8, 2048, 8192], P('expert', None, 'tile')
- new_first: float32 [8, 2048, 8192], P('expert', None, 'tile')
- new_second: float32 [8, 2048, 8192], P('expert', None, 'tile')
Inputs may be any that keep to these rules, and one draw needn't show every extreme that they name: `grad`: scaled values. `left_basis`: every diagonal block is orthogonal before rounding to bfloat16. `right_basis`: every diagonal block is orthogonal before rounding to bfloat16.
All inputs are finite; a program needn't handle non-finite values.
Results may differ from a plain program's by a relative error of at most 0.0045.
Values may be sent and summed in bfloat16 or wider, within the bound.
No kernel may reach another device: no remote copies, remote signals or barrier semaphores. Data moves between devices by JAX's collectives and lax.ppermute only.
A program may use at most 128 MiB of HBM per device.

v0:
```python
import jax
import jax.numpy as jnp
from jax import lax
from jax.sharding import Mesh
from jax.sharding import PartitionSpec as P

TILE = ("tile_0", "tile_1")
EXPERT_TILE = ("expert_0", "expert_1", "tile_0", "tile_1")
EXPERT = ("expert_0", "expert_1")


beta_one = 0.9
beta_two = 0.95
epsilon = 1e-08
learn_rate = 0.25
decay_rate = 0.1


def one_axis_at_a_time(value, axes):
    for axis in axes:
        value = lax.psum(value, axis)
    return value


def swapped(value, axis, distance):
    mask = 2**distance
    pairs = [(source, source ^ mask) for source in range(lax.axis_size(axis))]
    return lax.ppermute(value, axis, pairs)


def doubling(items, position, send):
    other = send(items, 0)
    lower = position >> 0 & 1 == 0
    items = jnp.where(
        lower, jnp.concatenate((items, other), axis=2), jnp.concatenate((other, items), axis=2)
    )
    return items


def on_device(weight, grad, first_moment, second_moment, left_basis, right_basis):
    experts, rows, width = grad.shape
    block = right_basis.shape[1]
    group = block // width
    levels = group.bit_length() - 1
    position = lax.axis_index(TILE) % group
    left_count = rows // block
    local_total = jnp.sum(jnp.square(grad.astype(jnp.float32)))
    total = one_axis_at_a_time(local_total, EXPERT_TILE)
    count = experts * lax.axis_size(EXPERT) * rows * width * lax.axis_size(TILE)
    clip = 1.0 / jnp.maximum(1.0, jnp.sqrt(total / count))
    whole_left = lax.all_gather(left_basis, TILE, axis=2, tiled=True)
    left4 = whole_left.reshape(experts, block, left_count, block)
    grad4 = grad.reshape(experts, left_count, block, width)
    rotated_left = jnp.einsum("ekbi,ebkw->ebiw", left4, grad4, preferred_element_type=jnp.float32)
    rotated_left = rotated_left.reshape(experts, rows, width).astype(jnp.bfloat16)

    def send_rows(items, bit):
        return swapped(items, TILE, bit)

    left_block = doubling(rotated_left, position, send_rows)
    rotated = jnp.einsum(
        "edk,ekj->edj", left_block, right_basis, preferred_element_type=jnp.float32
    )
    clipped = clip * rotated
    new_first = beta_one * first_moment + (1.0 - beta_one) * clipped
    new_second = beta_two * second_moment + (1.0 - beta_two) * clipped * clipped
    update = (new_first / (jnp.sqrt(new_second) + epsilon)).astype(jnp.bfloat16)
    partial_term = jnp.einsum(
        "edj,ekj->edk", update, right_basis, preferred_element_type=jnp.float32
    )
    for bit in reversed(range(levels)):
        half = partial_term.shape[2] // 2
        first_half = partial_term[:, :, :half]
        second_half = partial_term[:, :, half:]
        upper = position >> bit & 1 == 1
        keeping = jnp.where(upper, second_half, first_half)
        sending = jnp.where(upper, first_half, second_half)
        partial_term = keeping + swapped(sending.astype(jnp.bfloat16), TILE, bit).astype(
            sending.dtype
        )
    back_right = partial_term.astype(jnp.bfloat16)
    back4 = back_right.reshape(experts, left_count, block, width)
    back = jnp.einsum("ekbi,ebiw->ebkw", left4, back4, preferred_element_type=jnp.float32).reshape(
        experts, rows, width
    )
    weight32 = weight.astype(jnp.float32)
    new_weight = (weight32 - learn_rate * (back + decay_rate * weight32)).astype(jnp.bfloat16)
    return (new_weight, new_first, new_second)


def solution(mesh):
    finer = Mesh(mesh.devices.reshape(4, 2, 4, 4), ("expert_0", "expert_1", "tile_0", "tile_1"))
    in_specs = (
        P(EXPERT, None, TILE),
        P(EXPERT, None, TILE),
        P(EXPERT, None, TILE),
        P(EXPERT, None, TILE),
        P(EXPERT, None, TILE),
        P(EXPERT, None, TILE),
    )
    out_specs = (P(EXPERT, None, TILE), P(EXPERT, None, TILE), P(EXPERT, None, TILE))
    return jax.shard_map(
        on_device, mesh=finer, in_specs=in_specs, out_specs=out_specs, check_vma=False
    )
```

profile of v0, /device:TPU:0, one launch (start us, length us, event | category | flops | bytes accessed | tf_op | source)
XLA Modules:
  0.0 212.0 jit_solution(10057856764942879282)
XLA Ops:
  7.2 0.0 copy-start
  7.2 0.0 all-gather.2.cloned.1.call-start
  7.2 0.7 all-gather.2.cloned.1.call-update
  7.9 0.0 copy-start.2
  7.9 61.7 %all-gather.2.cloned.1.call-done = bf16[1,1024,2048]{2,1,0:T(8,128)(2,1)} async-done(((bf16[1,1024,128]{2,1,0:T(8,128)(2,1)}), bf16[1,1024,2048]{2,1,0:T(8,128)(2,1)}) %all-gather.2.cloned.1.call-update) | async-done | bytes 4194320 | tf_op jit(solution)/shard_map/all_gather | solution.py:51
  69.6 6.4 %copy.12 = bf16[1,1024,2048]{1,2,0:T(8,128)(2,1)} copy(bf16[1,1024,2048]{2,1,0:T(8,128)(2,1)} %all-gather.2.cloned.1.call-done) | data formatting | bytes 8388608 | tf_op jit(solution)/shard_map/all_gather | solution.py:51
  76.0 0.0 copy-done.2
  76.0 5.8 %convolution_convert_fusion = bf16[2,1024,512]{2,1,0:T(8,128)(2,1)} fusion(bf16[1024,2,1024]{0,2,1:T(8,128)(2,1)} %bitcast.34, bf16[2,1024,512]{2,1,0:T(8,128)(2,1)S(1)} %bitcast.37), kind=kOutput, calls=%fused_computation.24 | convolution fusion | flops 2148532224 | bytes 8388608 | tf_op jit(solution)/shard_map/ekbi,ebkw->ebiw/dot_general | solution.py:54
  81.8 1.2 collective-permute-start
  83.0 1.7 multiply_reduce_fusion
  84.7 11.0 %psum.28 = f32[]{:T(128)} all-reduce(f32[]{:T(128)} %multiply_reduce_fusion), channel_id=1, replica_groups=mesh['expert_0'=4,'expert_1'=2,'tile_0'=4,'tile_1'=4] {'expert_0'}, use_global_device_ids=true, to_apply=%region_1.2 | all-reduce | flops 1 | bytes 8 | tf_op jit(solution)/shard_map/psum | solution.py:21
  95.7 3.1 %psum.29 = f32[]{:T(128)} all-reduce(f32[]{:T(128)} %psum.28), channel_id=1, replica_groups=mesh['expert_0'=4,'expert_1'=2,'tile_0'=4,'tile_1'=4] {'expert_1'}, use_global_device_ids=true, to_apply=%region_2.3 | all-reduce | flops 1 | bytes 8 | tf_op jit(solution)/shard_map/psum | solution.py:21
  98.8 9.8 %psum.30 = f32[]{:T(128)} all-reduce(f32[]{:T(128)} %psum.29), channel_id=1, replica_groups=mesh['expert_0'=4,'expert_1'=2,'tile_0'=4,'tile_1'=4] {'tile_0'}, use_global_device_ids=true, to_apply=%region_3.4 | all-reduce | flops 1 | bytes 8 | tf_op jit(solution)/shard_map/psum | solution.py:21
  108.6 24.2 %psum.31 = f32[]{:T(128)} all-reduce(f32[]{:T(128)} %psum.30), channel_id=1, replica_groups=mesh['expert_0'=4,'expert_1'=2,'tile_0'=4,'tile_1'=4] {'tile_1'}, use_global_device_ids=true, to_apply=%region_4.5 | all-reduce | flops 1 | bytes 8 | tf_op jit(solution)/shard_map/psum | solution.py:21
  133.5 0.0 collective-permute-done
  133.5 0.0 copy-done
  133.5 7.8 %fusion.4 = (f32[1,2048,512]{2,1,0:T(8,128)S(1)}, f32[1,2048,512]{2,1,0:T(8,128)S(1)}) fusion(f32[1,2048,512]{2,1,0:T(8,128)} %param.9, f32[]{:T(128)S(6)} %div.10, f32[1,2048,512]{2,1,0:T(8,128)} %param.8, bf16[1,1024,512]{2,1,0:T(8,128)(2,1)S(1)} %copy-done, bf16[2048,512]{1,0:T(8,128)(2,1)} %bitcast.4, bf16[2048,512]{1,0:T(8,128)(2,1)} %bitcast.2, pred[]{:T(512)S(6)} %eq.9), kind=kOutput, calls=%fused_computation.8 | convolution fusion | flops 2174746624 | bytes 22020100 | tf_op jit(solution)/shard_map/edk,ekj->edj/dot_general | solution.py:61
  141.4 0.0 copy-start.4
  141.4 0.0 copy-start.5
  141.4 2.8 %convolution_bitcast_fusion = f32[1,2048,1024]{2,1,0:T(8,128)S(1)} fusion(f32[1,2048,512]{2,1,0:T(8,128)S(1)} %get-tuple-element.4, f32[1,2048,512]{2,1,0:T(8,128)S(1)} %get-tuple-element.3, bf16[1,1024,512]{2,1,0:T(8,128)(2,1)S(1)} %copy-done), kind=kOutput, calls=%fused_computation.3 | convolution fusion | flops 2150629376 | bytes 17825792 | tf_op jit(solution)/shard_map/edj,ekj->edk/dot_general | solution.py:68
  144.2 0.0 copy-done.4
  144.2 0.5 copy-done.5
  144.7 0.4 select_convert_fusion
  145.1 0.0 copy-start.1
  145.1 0.3 collective-permute-start.1
  145.4 44.3 %collective-permute-done.1 = bf16[1,2048,512]{2,1,0:T(8,128)(2,1)S(1)} collective-permute-done((bf16[1,2048,512]{2,1,0:T(8,128)(2,1)S(1)}, bf16[1,2048,512]{2,1,0:T(8,128)(2,1)S(1)}, u32[]{:S(2)}, u32[]{:S(2)}) %collective-permute-start.1) | collective-permute-done | bytes 2097184 | tf_op jit(solution)/shard_map/ppermute | solution.py:28
  189.7 1.2 add_convert_fusion
  190.9 0.0 copy-done.1
  190.9 4.3 %convolution_bitcast_fusion.1 = f32[2,1024,512]{1,2,0:T(8,128)} fusion(bf16[2,1024,512]{2,1,0:T(8,128)(2,1)S(1)} %bitcast.36, bf16[1024,2,1024]{0,2,1:T(8,128)(2,1)S(1)} %bitcast.35), kind=kOutput, calls=%fused_computation.22 | convolution fusion | flops 2147483648 | bytes 10485760 | tf_op jit(solution)/shard_map/ekbi,ebiw->ebkw/dot_general | solution.py:83
  195.2 0.0 copy-start.3
  195.2 5.6 %copy.15 = f32[2,1024,512]{2,1,0:T(8,128)} copy(f32[2,1024,512]{1,2,0:T(8,128)} %convolution_bitcast_fusion.1) | data formatting | bytes 8388608 | tf_op jit(solution)/shard_map/ekbi,ebiw->ebkw/dot_general | solution.py:83
  200.8 0.0 copy-done.3
  200.8 4.3 %fusion.2 = bf16[1,2048,512]{2,1,0:T(8,128)(2,1)} fusion(bf16[1,2048,512]{2,1,0:T(8,128)(2,1)S(1)} %copy-done.3, f32[1,2048,512]{2,1,0:T(8,128)} %bitcast.33), kind=kLoop, calls=%fused_computation.6 | loop fusion | flops 6291456 | bytes 8388608 | tf_op jit(solution)/shard_map/convert_element_type | solution.py:87
Async XLA Ops:
  7.2 126.4 %copy-start = (bf16[1,1024,512]{2,1,0:T(8,128)(2,1)S(1)}, bf16[1,1024,512]{2,1,0:T(8,128)(2,1)}, u32[]{:S(2)}) copy-start(bf16[1,1024,512]{2,1,0:T(8,128)(2,1)} %param.11) | copy-start | bytes 3145732
  7.2 62.4 %all-gather.2.cloned.1.call-start = ((), (), s32[]{:S(2)}) async-start(), calls=%async_computation | async-start | bytes 4456448 | tf_op jit(solution)/shard_map/all_gather | solution.py:51
  7.9 68.1 %copy-start.2 = (bf16[1,2048,512]{2,1,0:T(8,128)(2,1)S(1)}, bf16[1,2048,512]{2,1,0:T(8,128)(2,1)}, u32[]{:S(2)}) copy-start(bf16[1,2048,512]{2,1,0:T(8,128)(2,1)} %param.7) | copy-start | bytes 6291460
  81.8 51.7 %collective-permute-start = (bf16[1,2048,512]{2,1,0:T(8,128)(2,1)}, bf16[1,2048,512]{2,1,0:T(8,128)(2,1)}, u32[]{:S(2)}, u32[]{:S(2)}) collective-permute-start(bf16[1,2048,512]{2,1,0:T(8,128)(2,1)} %bitcast.3), channel_id=1, source_target_pairs={{0,1},{1,0},{2,3},{3,2},{4,5},{5,4},{6,7},{7,6},{8,9},{9,8},{10,11... | collective-permute-start | bytes 6291464 | tf_op jit(solution)/shard_map/ppermute | solution.py:28
  141.4 2.8 %copy-start.4 = (f32[1,2048,512]{2,1,0:T(8,128)}, f32[1,2048,512]{2,1,0:T(8,128)S(1)}, u32[]{:S(2)}) copy-start(f32[1,2048,512]{2,1,0:T(8,128)S(1)} %get-tuple-element.3) | copy-start | bytes 12582916
  141.4 3.4 %copy-start.5 = (f32[1,2048,512]{2,1,0:T(8,128)}, f32[1,2048,512]{2,1,0:T(8,128)S(1)}, u32[]{:S(2)}) copy-start(f32[1,2048,512]{2,1,0:T(8,128)S(1)} %get-tuple-element.4) | copy-start | bytes 12582916
  145.1 45.8 %copy-start.1 = (bf16[1,1024,2048]{1,2,0:T(8,128)(2,1)S(1)}, bf16[1,1024,2048]{1,2,0:T(8,128)(2,1)}, u32[]{:S(2)}) copy-start(bf16[1,1024,2048]{1,2,0:T(8,128)(2,1)} %copy.12) | copy-start | bytes 12582916
  145.1 44.5 %collective-permute-start.1 = (bf16[1,2048,512]{2,1,0:T(8,128)(2,1)S(1)}, bf16[1,2048,512]{2,1,0:T(8,128)(2,1)S(1)}, u32[]{:S(2)}, u32[]{:S(2)}) collective-permute-start(bf16[1,2048,512]{2,1,0:T(8,128)(2,1)S(1)} %select_convert_fusion), channel_id=1, source_target_pairs={{0,1},{1,0},{2,3},{3,2},{4,5},{5,4},{6,7},{7,6},{8,9},{9,8},{10,11... | collective-permute-start | bytes 6291464 | tf_op jit(solution)/shard_map/ppermute | solution.py:28
  195.2 5.6 %copy-start.3 = (bf16[1,2048,512]{2,1,0:T(8,128)(2,1)S(1)}, bf16[1,2048,512]{2,1,0:T(8,128)(2,1)}, u32[]{:S(2)}) copy-start(bf16[1,2048,512]{2,1,0:T(8,128)(2,1)} %param.6) | copy-start | bytes 6291460
Sparse Core Ops, SparseCore 0:
  10.1 59.4 all-gather.1
where the time goes:
time: 212 us
  waiting for transfers between devices  107 us (50%)
  blocking collectives  48.1 us (23%)
  matrix products  20.8 us (10%)
  between operations  14.9 us (7%)
  local copies, waits for them, and re-layouts  12.5 us (6%)
  other arithmetic  7.61 us (4%)
    all_gather x1, waiting for transfers between devices, on_device(): whole_left = lax.all_gather(left_basis, TILE, axis=2, tiled=True)  61.7 us
    psum x4, blocking collectives, one_axis_at_a_time(): value = lax.psum(value, axis)  48.1 us
    ppermute x2, waiting for transfers between devices, swapped(): return lax.ppermute(value, axis, pairs)  44.3 us
    dot_general x1, matrix products, on_device(): jnp.einsum('edk,ekj->edj', left_block, right_basis, preferred_element_typ...  7.82 us
    all_gather x1, local copies, waits for them, and re-layouts, on_device(): whole_left = lax.all_gather(left_basis, TILE, axis=2, tiled=True)  6.4 us
    dot_general x1, matrix products, on_device(): jnp.einsum('ekbi,ebkw->ebiw', left4, grad4, preferred_element_type=jnp.fl...  5.83 us
    dot_general x1, local copies, waits for them, and re-layouts, on_device(): jnp.einsum('ekbi,ebiw->ebkw', left4, back4, preferred_element_type=jnp.fl...  5.56 us
    convert_element_type x1, other arithmetic, on_device(): (weight32 - learn_rate * (back + decay_rate * weight32)).astype(jnp.bfloa...  4.33 us
  transfers between devices with their start and end apart: 3, of which 2 were waited for; matrix products, arithmetic and copies ran while one was open for 1% of the time, Pallas kernels for 0%

commit v1 on v0

v1 whole, which is shorter than its diff:
```python
import functools

import jax
import jax.numpy as jnp
from jax import lax
from jax.experimental import pallas as pl
from jax.experimental.pallas import tpu as pltpu
from jax.sharding import Mesh
from jax.sharding import PartitionSpec as P

AXES = ("x", "core", "z", "y")
EXPERT = ("x", "core")
TILE = ("z", "y")

beta_one = 0.9
beta_two = 0.95
epsilon = 1e-08
learn_rate = 0.25
decay_rate = 0.1


f32 = jnp.float32
bf16 = jnp.bfloat16
ANY = pl.BlockSpec(memory_space=pl.ANY)


def cost(flops, bytes_accessed):
    return pl.CostEstimate(flops=flops, bytes_accessed=bytes_accessed, transcendentals=0)


def permute(value, axis, target):
    pairs = [(source, target(source)) for source in range(lax.axis_size(axis))]
    return lax.ppermute(value, axis, pairs)


def pair(y):
    return y ^ 1


def side(y):
    return 3 - y


def after(z):
    return (z + 1) % 4


def before(z):
    return (z + 3) % 4


def opposite(z):
    return (z + 2) % 4


def whole_sum(value):
    value = value + permute(value, "y", pair)
    for _ in range(1):
        value = value + permute(value, "core", pair)
    value = sum(
        [permute(value, "x", f) for f in (after, before, opposite)],
        value,
    )
    value = value + permute(value, "y", side)
    value = sum(
        [permute(value, "z", f) for f in (after, before, opposite)],
        value,
    )
    return value


def gather_left(shard):
    c0 = shard
    c1 = permute(c0, "y", pair)
    c2 = permute(c0, "y", side)
    c3 = permute(c1, "y", side)
    columns = (c0, c1, c2, c3)
    ups = [permute(c, "z", after) for c in columns]
    downs = [permute(c, "z", before) for c in columns]
    relays = [permute(ups[i], "z", after) for i in (0, 1)]
    relays += [permute(downs[i], "z", before) for i in (2, 3)]
    return [*columns, *ups, *downs, *relays]


def forward_kernel(block_index, chained, *refs):
    clip_ref = refs[0]
    shards = refs[1:17]
    own_ref, other_ref, right_ref, first_ref, second_ref = refs[17:22]
    rest = refs[24:] if chained else refs[22:]
    new_first_ref, new_second_ref, left_ref, send_ref, keep_ref, sems = rest
    width = right_ref.shape[2]
    rows = new_first_ref.shape[1]
    z = lax.axis_index("z")
    y = lax.axis_index("y")
    step = pl.program_id(0)
    partner = lax.rem(y + 1, 2) * 2 - 1 + y

    @pl.when(step == 0)
    def _():
        columns = (y, partner, 3 - y, 3 - partner)
        for phase in range(2):
            for group, distance in enumerate((0, 3, 1, 2)):
                row = lax.rem(z + distance, 4)

                @pl.when(lax.div(row, 2) == block_index)
                def _():
                    for k in range(4):
                        slot = lax.rem(row, 2) * 4 + columns[k]
                        lanes = pl.ds(pl.multiple_of(slot * 128, 128), 128)
                        copy = pltpu.make_async_copy(
                            shards[group * 4 + k].at[0],
                            left_ref.at[:, lanes],
                            sems.at[group * 4 + k],
                        )
                        if phase == 0:
                            copy.start()
                        else:
                            copy.wait()

    position = lax.rem(y, 2)
    lanes = pl.ds(pl.multiple_of(step * rows, rows), rows)
    left = left_ref[:, lanes]
    right_own = right_ref[0, pl.ds(pl.multiple_of(position * width, width), width), :]
    right_other = right_ref[0, pl.ds(pl.multiple_of((1 - position) * width, width), width), :]
    tn = (((0,), (0,)), ((), ()))
    nt = (((1,), (1,)), ((), ()))
    rotated_own = lax.dot_general(left, own_ref[0], tn, preferred_element_type=f32).astype(bf16)
    rotated_other = lax.dot_general(left, other_ref[0], tn, preferred_element_type=f32).astype(bf16)
    rotated = jnp.dot(rotated_own, right_own, preferred_element_type=f32) + jnp.dot(
        rotated_other, right_other, preferred_element_type=f32
    )
    clipped = clip_ref[0, 0] * rotated
    new_first = beta_one * first_ref[0] + (1.0 - beta_one) * clipped
    new_second = beta_two * second_ref[0] + (1.0 - beta_two) * clipped * clipped
    new_first_ref[0] = new_first
    new_second_ref[0] = new_second
    update = (new_first / (jnp.sqrt(new_second) + epsilon)).astype(bf16)
    send_ref[...] = lax.dot_general(update, right_other, nt, preferred_element_type=f32).astype(bf16)
    keep_ref[...] = lax.dot_general(update, right_own, nt, preferred_element_type=f32).astype(bf16)


def forward(block_index, clip, shards, grad, other, right, first, second, previous):
    _, all_rows, width = grad.shape
    block = right.shape[1]
    rows = 256
    steps = block // rows
    chained = previous is not None
    moment = pl.BlockSpec((1, rows, width), lambda s: (0, block_index * steps + s, 0))
    term = pl.BlockSpec((rows, width), lambda s: (s, 0))
    moments = jax.ShapeDtypeStruct((1, all_rows, width), f32)
    terms = jax.ShapeDtypeStruct((block, width), bf16)
    in_specs = [pl.BlockSpec(memory_space=pltpu.SMEM)] + [ANY] * 16
    in_specs += [
        pl.BlockSpec((1, block, width), lambda s: (0, block_index, 0)),
        pl.BlockSpec((1, block, width), lambda s: (0, 0, 0)),
        pl.BlockSpec((1, block, width), lambda s: (0, 0, 0)),
        moment,
        moment,
    ]
    operands = [clip, *shards, grad, other, right, first, second]
    aliases = {}
    if chained:
        in_specs += [ANY, ANY]
        operands += list(previous)
        aliases = {22: 0, 23: 1}
    return pl.pallas_call(
        functools.partial(forward_kernel, block_index, chained),
        grid=(steps,),
        out_shape=[moments, moments, jax.ShapeDtypeStruct((block, block), bf16), terms, terms],
        in_specs=in_specs,
        out_specs=[moment, moment, pl.BlockSpec((block, block), lambda s: (0, 0)), term, term],
        scratch_shapes=[pltpu.SemaphoreType.DMA((16,))],
        input_output_aliases=aliases,
        cost_estimate=cost(8 * block * block * width, 16 * block * block),
        compiler_params=pltpu.CompilerParams(vmem_limit_bytes=48 * 1024 * 1024),
    )(*operands)


def back_kernel(left_ref, term_ref, out_ref):
    out_ref[...] = jnp.dot(left_ref[...], term_ref[...], preferred_element_type=f32).astype(bf16)


def back_send(left, term, start, count):
    block, width = term.shape
    rows = 256
    return pl.pallas_call(
        back_kernel,
        grid=(count // rows,),
        out_shape=jax.ShapeDtypeStruct((count, width), bf16),
        in_specs=[
            pl.BlockSpec((rows, block), lambda s: (start // rows + s, 0)),
            pl.BlockSpec((block, width), lambda s: (0, 0)),
        ],
        out_specs=pl.BlockSpec((rows, width), lambda s: (s, 0)),
        cost_estimate=cost(2 * count * block * width, 2 * count * block + 2 * block * width),
    )(left, term)


def base_kernel(left_ref, term_ref, weight_ref, out_ref):
    back = jnp.dot(left_ref[...], term_ref[...], preferred_element_type=f32)
    weight = weight_ref[0].astype(f32)
    out_ref[...] = weight - learn_rate * (back + decay_rate * weight)


def base(block_index, left, term, weight):
    block, width = term.shape
    rows = 256
    steps = block // rows
    return pl.pallas_call(
        base_kernel,
        grid=(steps,),
        out_shape=jax.ShapeDtypeStruct((block, width), f32),
        in_specs=[
            pl.BlockSpec((rows, block), lambda s: (s, 0)),
            pl.BlockSpec((block, width), lambda s: (0, 0)),
            pl.BlockSpec((1, rows, width), lambda s: (0, block_index * steps + s, 0)),
        ],
        out_specs=pl.BlockSpec((rows, width), lambda s: (s, 0)),
        cost_estimate=cost(2 * block * block * width, 8 * block * width),
    )(left, term, weight)


def finish_kernel(base_ref, received_ref, *refs):
    out_ref = refs[-1]
    out_ref[0] = (base_ref[...] - learn_rate * received_ref[...].astype(f32)).astype(bf16)


def finish(base_term, received, start, offset, total_rows, previous):
    count, width = received.shape
    rows = 128
    in_specs = [
        pl.BlockSpec((rows, width), lambda s: (offset // rows + s, 0)),
        pl.BlockSpec((rows, width), lambda s: (s, 0)),
    ]
    operands = [base_term, received]
    aliases = {}
    if previous is not None:
        in_specs.append(ANY)
        operands.append(previous)
        aliases = {2: 0}
    return pl.pallas_call(
        finish_kernel,
        grid=(count // rows,),
        out_shape=jax.ShapeDtypeStruct((1, total_rows, width), bf16),
        in_specs=in_specs,
        out_specs=pl.BlockSpec((1, rows, width), lambda s: (0, start // rows + s, 0)),
        input_output_aliases=aliases,
        cost_estimate=cost(2 * count * width, 8 * count * width),
    )(*operands)


def on_device(weight, grad, first_moment, second_moment, left_basis, right_basis):
    _, rows, width = grad.shape
    block = right_basis.shape[1]
    count = 8 * rows * width * 16

    other0 = permute(grad[:, :block], "y", pair)
    other1 = permute(grad[:, block:], "y", pair)
    local_total = jnp.sum(jnp.square(grad.astype(f32))).reshape(1, 1)
    total = whole_sum(local_total)
    clip = 1.0 / jnp.maximum(1.0, jnp.sqrt(total / count))
    shards = gather_left(left_basis)

    nf, ns, left0, send0, keep0 = forward(
        0, clip, shards, grad, other0, right_basis, first_moment, second_moment, None
    )
    back0 = back_send(left0, send0, 0, block)
    received0 = permute(back0, "y", pair)
    base0 = base(0, left0, keep0, weight)

    nf, ns, left1, send1, keep1 = forward(
        1, clip, shards, grad, other1, right_basis, first_moment, second_moment, (nf, ns)
    )
    pieces = ((0, 512), (512, 256), (768, 256))
    received1 = []
    for start, size in pieces:
        part = back_send(left1, send1, start, size)
        received1.append(permute(part, "y", pair))
    base1 = base(1, left1, keep1, weight)

    new_weight = finish(base0, received0, 0, 0, rows, None)
    for i, (start, size) in enumerate(pieces):
        new_weight = finish(base1, received1[i], block + start, start, rows, new_weight)
    return (new_weight, nf, ns)


def solution(mesh):
    finer = Mesh(mesh.devices.reshape(4, 2, 4, 4), AXES)
    spec = P(EXPERT, None, TILE)
    return jax.shard_map(
        on_device, mesh=finer, in_specs=(spec,) * 6, out_specs=(spec,) * 3, check_vma=False
    )
```

time: 212 us -> 156 us (0.74)
  waiting for transfers between devices: 107 us -> 34 us
  Pallas kernels: 0 us -> 58.4 us
  blocking collectives: 48.1 us -> 0 us
  starting transfers between devices: 1.49 us -> 43 us
  matrix products: 20.8 us -> 0 us
  between operations: 14.9 us -> 7.07 us
  other arithmetic: 7.61 us -> 3.27 us
  local copies, waits for them, and re-layouts: 12.5 us -> 9.19 us
    all_gather x1 -> x0, waiting for transfers between devices: 61.7 us -> none  [on_device(): whole_left = lax.all_gather(left_basis, TILE, axis=2, tiled=True)]
    pallas_call x0 -> x12, Pallas kernels: none -> 58.4 us  [the longest x2 22.8 us: forward(): pl.pallas_call(functools.partial(forward_kernel, block_index, chained), g...]
    psum x4 -> x0, blocking collectives: 48.1 us -> none  [one_axis_at_a_time(): value = lax.psum(value, axis)]
    ppermute x2 -> x30, starting transfers between devices: 1.46 us -> 43 us  [permute(): return lax.ppermute(value, axis, pairs)]
    dot_general x4 -> x0, matrix products: 20.8 us -> none  [the longest x1 7.82 us: on_device(): jnp.einsum('edk,ekj->edj', left_block, right_basis, preferred_element_typ...]
    ppermute x2 -> x30, waiting for transfers between devices: 44.3 us -> 34 us  [permute(): return lax.ppermute(value, axis, pairs)]
    unnamed x12 -> x28, local copies, waits for them, and re-layouts: 0.58 us -> 8.07 us
    all_gather x1 -> x0, local copies, waits for them, and re-layouts: 6.4 us -> none  [on_device(): whole_left = lax.all_gather(left_basis, TILE, axis=2, tiled=True)]
  transfers between devices with their start and end apart: 3 -> 30, of which waited for: 2 -> 14; matrix products, arithmetic and copies ran while one was open for 1% -> 3% of each run, Pallas kernels for 0% -> 37%
where the time goes in v1:
time: 156 us; the launch traced here: 155 us
  Pallas kernels  58.4 us (37%)
  starting transfers between devices  43 us (28%)
  waiting for transfers between devices  34 us (22%)
  local copies, waits for them, and re-layouts  9.19 us (6%)
  between operations  7.07 us (5%)
  other arithmetic  3.27 us (2%)
    ppermute x30, starting transfers between devices, permute(): return lax.ppermute(value, axis, pairs)  43 us
    ppermute x30, waiting for transfers between devices, permute(): return lax.ppermute(value, axis, pairs)  34 us
    pallas_call x2, Pallas kernels, forward(): pl.pallas_call(functools.partial(forward_kernel, block_index, chained), g...  22.8 us
    pallas_call x4, Pallas kernels, back_send(): pl.pallas_call(back_kernel, grid=(count // rows,), out_shape=jax.ShapeDty...  12.8 us
    pallas_call x4, Pallas kernels, finish(): pl.pallas_call(finish_kernel, grid=(count // rows,), out_shape=jax.ShapeD...  12.6 us
    pallas_call x2, Pallas kernels, base(): pl.pallas_call(base_kernel, grid=(steps,), out_shape=jax.ShapeDtypeStruct...  10.3 us
    unnamed x28, local copies, waits for them, and re-layouts  8.07 us
    reduce_sum x1, other arithmetic, on_device(): local_total = jnp.sum(jnp.square(grad.astype(f32))).reshape(1, 1)  3.27 us
  transfers between devices with their start and end apart: 30, of which 14 were waited for; matrix products, arithmetic and copies ran while one was open for 3% of the time, Pallas kernels for 37%

profile of v1, /device:TPU:0, one launch (start us, length us, event | category | flops | bytes accessed | tf_op | source)
XLA Modules:
  0.0 155.0 jit_solution(17375152957295003537)
XLA Ops:
  0.6 1.8 %collective-permute-start.9 = (bf16[1,1024,128]{2,1,0:T(8,128)(2,1)}, bf16[1,1024,128]{2,1,0:T(8,128)(2,1)S(1)}, u32[]{:S(2)}, u32[]{:S(2)}) collective-permute-start(bf16[1,1024,128]{2,1,0:T(8,128)(2,1)} %refs_1_.3), channel_id=1, source_target_pairs={{0,1},{1,0},{2,3},{3,2},{4,5},{5,4},{6,7},{7,6},{8,9},{9,8},{10,11... | collective-permute-start | bytes 786440 | tf_op jit(solution)/shard_map/ppermute | solution.py:33
  2.4 2.2 %collective-permute-start.10 = (bf16[1,1024,128]{2,1,0:T(8,128)(2,1)}, bf16[1,1024,128]{2,1,0:T(8,128)(2,1)S(1)}, u32[]{:S(2)}, u32[]{:S(2)}) collective-permute-start(bf16[1,1024,128]{2,1,0:T(8,128)(2,1)} %refs_1_.3), channel_id=1, source_target_pairs={{0,3},{1,2},{2,1},{3,0},{4,7},{5,6},{6,5},{7,4},{8,11},{9,10},{10,... | collective-permute-start | bytes 786440 | tf_op jit(solution)/shard_map/ppermute | solution.py:33
  4.6 1.9 %collective-permute-start.12 = (bf16[1,1024,128]{2,1,0:T(8,128)(2,1)}, bf16[1,1024,128]{2,1,0:T(8,128)(2,1)S(1)}, u32[]{:S(2)}, u32[]{:S(2)}) collective-permute-start(bf16[1,1024,128]{2,1,0:T(8,128)(2,1)} %refs_1_.3), channel_id=1, source_target_pairs={{0,4},{4,8},{8,12},{12,0},{1,5},{5,9},{9,13},{13,1},{2,6},{6,10},{... | collective-permute-start | bytes 786440 | tf_op jit(solution)/shard_map/ppermute | solution.py:33
  6.5 2.1 %collective-permute-start.16 = (bf16[1,1024,128]{2,1,0:T(8,128)(2,1)}, bf16[1,1024,128]{2,1,0:T(8,128)(2,1)S(1)}, u32[]{:S(2)}, u32[]{:S(2)}) collective-permute-start(bf16[1,1024,128]{2,1,0:T(8,128)(2,1)} %refs_1_.3), channel_id=1, source_target_pairs={{0,12},{4,0},{8,4},{12,8},{1,13},{5,1},{9,5},{13,9},{2,14},{6,2},{... | collective-permute-start | bytes 786440 | tf_op jit(solution)/shard_map/ppermute | solution.py:33
  8.6 3.3 %multiply_reduce_fusion = f32[]{:T(128)} fusion(bf16[1,2048,512]{2,1,0:T(8,128)(2,1)} %refs_17_.3), kind=kLoop, calls=%fused_computation | loop fusion | flops 3145727 | bytes 2097156 | tf_op jit(solution)/shard_map/reduce_sum | solution.py:259
  12.6 1.1 fusion
  13.7 1.9 %collective-permute-done = f32[1,1]{1,0:T(1,128)} collective-permute-done((f32[1,1]{1,0:T(1,128)}, f32[1,1]{1,0:T(1,128)}, u32[]{:S(2)}, u32[]{:S(2)}) %collective-permute-start) | collective-permute-done | bytes 36 | tf_op jit(solution)/shard_map/ppermute | solution.py:33
  18.7 2.9 %collective-permute-start.2 = (f32[1,1]{1,0:T(1,128)}, f32[1,1]{1,0:T(1,128)}, u32[]{:S(2)}, u32[]{:S(2)}) collective-permute-start(f32[1,1]{1,0:T(1,128)} %add.28), channel_id=1, source_target_pairs={{0,32},{32,64},{64,96},{96,0},{1,33},{33,65},{65,97},{97,1},{2,34}... | collective-permute-start | bytes 20 | tf_op jit(solution)/shard_map/ppermute | solution.py:33
  21.5 1.9 %collective-permute-done.2 = f32[1,1]{1,0:T(1,128)} collective-permute-done((f32[1,1]{1,0:T(1,128)}, f32[1,1]{1,0:T(1,128)}, u32[]{:S(2)}, u32[]{:S(2)}) %collective-permute-start.2) | collective-permute-done | bytes 36 | tf_op jit(solution)/shard_map/ppermute | solution.py:33
  23.5 2.8 %collective-permute-start.3 = (f32[1,1]{1,0:T(1,128)}, f32[1,1]{1,0:T(1,128)}, u32[]{:S(2)}, u32[]{:S(2)}) collective-permute-start(f32[1,1]{1,0:T(1,128)} %add.28), channel_id=1, source_target_pairs={{0,96},{32,0},{64,32},{96,64},{1,97},{33,1},{65,33},{97,65},{2,98}... | collective-permute-start | bytes 20 | tf_op jit(solution)/shard_map/ppermute | solution.py:33
  27.0 3.1 %collective-permute-start.4 = (f32[1,1]{1,0:T(1,128)}, f32[1,1]{1,0:T(1,128)}, u32[]{:S(2)}, u32[]{:S(2)}) collective-permute-start(f32[1,1]{1,0:T(1,128)} %add.28), channel_id=1, source_target_pairs={{0,64},{32,96},{64,0},{96,32},{1,65},{33,97},{65,1},{97,33},{2,66}... | collective-permute-start | bytes 20 | tf_op jit(solution)/shard_map/ppermute | solution.py:33
  30.7 1.4 collective-permute-done.4
  32.8 2.4 %collective-permute-start.5 = (f32[1,1]{1,0:T(1,128)}, f32[1,1]{1,0:T(1,128)}, u32[]{:S(2)}, u32[]{:S(2)}) collective-permute-start(f32[1,1]{1,0:T(1,128)} %add.31), channel_id=1, source_target_pairs={{0,3},{1,2},{2,1},{3,0},{4,7},{5,6},{6,5},{7,4},{8,11},{9,10},{10,... | collective-permute-start | bytes 20 | tf_op jit(solution)/shard_map/ppermute | solution.py:33
  35.2 2.4 %collective-permute-done.5 = f32[1,1]{1,0:T(1,128)} collective-permute-done((f32[1,1]{1,0:T(1,128)}, f32[1,1]{1,0:T(1,128)}, u32[]{:S(2)}, u32[]{:S(2)}) %collective-permute-start.5) | collective-permute-done | bytes 36 | tf_op jit(solution)/shard_map/ppermute | solution.py:33
  38.2 1.4 collective-permute-start.6
  39.6 3.6 %collective-permute-done.6 = f32[1,1]{1,0:T(1,128)} collective-permute-done((f32[1,1]{1,0:T(1,128)}, f32[1,1]{1,0:T(1,128)}, u32[]{:S(2)}, u32[]{:S(2)}) %collective-permute-start.6) | collective-permute-done | bytes 36 | tf_op jit(solution)/shard_map/ppermute | solution.py:33
  43.2 2.1 %collective-permute-start.7 = (f32[1,1]{1,0:T(1,128)}, f32[1,1]{1,0:T(1,128)}, u32[]{:S(2)}, u32[]{:S(2)}) collective-permute-start(f32[1,1]{1,0:T(1,128)} %add.32), channel_id=1, source_target_pairs={{0,12},{4,0},{8,4},{12,8},{1,13},{5,1},{9,5},{13,9},{2,14},{6,2},{... | collective-permute-start | bytes 20 | tf_op jit(solution)/shard_map/ppermute | solution.py:33
  45.3 1.6 %collective-permute-done.7 = f32[1,1]{1,0:T(1,128)} collective-permute-done((f32[1,1]{1,0:T(1,128)}, f32[1,1]{1,0:T(1,128)}, u32[]{:S(2)}, u32[]{:S(2)}) %collective-permute-start.7) | collective-permute-done | bytes 36 | tf_op jit(solution)/shard_map/ppermute | solution.py:33
  46.9 2.0 %collective-permute-start.8 = (f32[1,1]{1,0:T(1,128)}, f32[1,1]{1,0:T(1,128)}, u32[]{:S(2)}, u32[]{:S(2)}) collective-permute-start(f32[1,1]{1,0:T(1,128)} %add.32), channel_id=1, source_target_pairs={{0,8},{4,12},{8,0},{12,4},{1,9},{5,13},{9,1},{13,5},{2,10},{6,14},... | collective-permute-start | bytes 20 | tf_op jit(solution)/shard_map/ppermute | solution.py:33
  48.8 3.2 %collective-permute-done.8 = f32[1,1]{1,0:T(1,128)} collective-permute-done((f32[1,1]{1,0:T(1,128)}, f32[1,1]{1,0:T(1,128)}, u32[]{:S(2)}, u32[]{:S(2)}) %collective-permute-start.8) | collective-permute-done | bytes 36 | tf_op jit(solution)/shard_map/ppermute | solution.py:33
  52.1 1.1 collective-permute-start.11
  53.1 3.2 %collective-permute-start.18 = (bf16[1,1024,128]{2,1,0:T(8,128)(2,1)S(1)}, bf16[1,1024,128]{2,1,0:T(8,128)(2,1)S(1)}, u32[]{:S(2)}, u32[]{:S(2)}) collective-permute-start(bf16[1,1024,128]{2,1,0:T(8,128)(2,1)S(1)} %collective-permute-done.10.refs_3_), channel_id=1, source_target_pairs={{0,12},{4,0},{8,4},{12,8},{1,13},{5,1},{9,5},{13,9},{2,14},{6,2},{... | collective-permute-start | bytes 786440 | tf_op jit(solution)/shard_map/ppermute | solution.py:33
  57.2 2.5 %collective-permute-done.11.refs_4_ = bf16[1,1024,128]{2,1,0:T(8,128)(2,1)S(1)} collective-permute-done((bf16[1,1024,128]{2,1,0:T(8,128)(2,1)S(1)}, bf16[1,1024,128]{2,1,0:T(8,128)(2,1)S(1)}, u32[]{:S(2)}, u32[]{:S(2)}) %collective-permute-start.11) | collective-permute-done | bytes 262176 | tf_op jit(solution)/shard_map/ppermute | solution.py:33
  59.6 3.9 %collective-permute-done.13.refs_6_ = bf16[1,1024,128]{2,1,0:T(8,128)(2,1)S(1)} collective-permute-done((bf16[1,1024,128]{2,1,0:T(8,128)(2,1)S(1)}, bf16[1,1024,128]{2,1,0:T(8,128)(2,1)S(1)}, u32[]{:S(2)}, u32[]{:S(2)}) %collective-permute-start.13) | collective-permute-done | bytes 262176 | tf_op jit(solution)/shard_map/ppermute | solution.py:33
  63.5 3.2 %collective-permute-start.19 = (bf16[1,1024,128]{2,1,0:T(8,128)(2,1)S(1)}, bf16[1,1024,128]{2,1,0:T(8,128)(2,1)S(1)}, u32[]{:S(2)}, u32[]{:S(2)}) collective-permute-start(bf16[1,1024,128]{2,1,0:T(8,128)(2,1)S(1)} %collective-permute-done.11.refs_4_), channel_id=1, source_target_pairs={{0,12},{4,0},{8,4},{12,8},{1,13},{5,1},{9,5},{13,9},{2,14},{6,2},{... | collective-permute-start | bytes 786440 | tf_op jit(solution)/shard_map/ppermute | solution.py:33
  66.8 3.3 %collective-permute-done.14.refs_7_ = bf16[1,1024,128]{2,1,0:T(8,128)(2,1)S(1)} collective-permute-done((bf16[1,1024,128]{2,1,0:T(8,128)(2,1)S(1)}, bf16[1,1024,128]{2,1,0:T(8,128)(2,1)S(1)}, u32[]{:S(2)}, u32[]{:S(2)}) %collective-permute-start.14) | collective-permute-done | bytes 262176 | tf_op jit(solution)/shard_map/ppermute | solution.py:33
  70.8 3.6 %collective-permute-done.20.refs_13_ = bf16[1,1024,128]{2,1,0:T(8,128)(2,1)S(1)} collective-permute-done((bf16[1,1024,128]{2,1,0:T(8,128)(2,1)S(1)}, bf16[1,1024,128]{2,1,0:T(8,128)(2,1)S(1)}, u32[]{:S(2)}, u32[]{:S(2)}) %collective-permute-start.20) | collective-permute-done | bytes 262176 | tf_op jit(solution)/shard_map/ppermute | solution.py:33
  74.4 3.2 %collective-permute-start.22 = (bf16[1,1024,128]{2,1,0:T(8,128)(2,1)S(1)}, bf16[1,1024,128]{2,1,0:T(8,128)(2,1)S(1)}, u32[]{:S(2)}, u32[]{:S(2)}) collective-permute-start(bf16[1,1024,128]{2,1,0:T(8,128)(2,1)S(1)} %collective-permute-done.18.refs_11_), channel_id=1, source_target_pairs={{0,12},{4,0},{8,4},{12,8},{1,13},{5,1},{9,5},{13,9},{2,14},{6,2},{... | collective-permute-start | bytes 786440 | tf_op jit(solution)/shard_map/ppermute | solution.py:33
  79.8 2.1 %collective-permute-done.21.refs_14_ = bf16[1,1024,128]{2,1,0:T(8,128)(2,1)S(1)} collective-permute-done((bf16[1,1024,128]{2,1,0:T(8,128)(2,1)S(1)}, bf16[1,1024,128]{2,1,0:T(8,128)(2,1)S(1)}, u32[]{:S(2)}, u32[]{:S(2)}) %collective-permute-start.21) | collective-permute-done | bytes 262176 | tf_op jit(solution)/shard_map/ppermute | solution.py:33
  82.0 2.4 %collective-permute-done.23.refs_16_ = bf16[1,1024,128]{2,1,0:T(8,128)(2,1)S(1)} collective-permute-done((bf16[1,1024,128]{2,1,0:T(8,128)(2,1)S(1)}, bf16[1,1024,128]{2,1,0:T(8,128)(2,1)S(1)}, u32[]{:S(2)}, u32[]{:S(2)}) %collective-permute-start.23) | collective-permute-done | bytes 262176 | tf_op jit(solution)/shard_map/ppermute | solution.py:33
  84.3 1.0 copy-done.10
  85.4 11.4 %shard_map.85 = (f32[1,2048,512]{2,1,0:T(8,128)}, f32[1,2048,512]{2,1,0:T(8,128)}, bf16[1024,1024]{1,0:T(8,128)(2,1)}, bf16[1024,512]{1,0:T(8,128)(2,1)S(1)}, bf16[1024,512]{1,0:T(8,128)(2,1)}) custom-call(f32[1,1]{1,0:T(1,128)S(6)} %div.7.refs_0_, bf16[1,1024,128]{2,1,0:T(8,128)(2,1)S(1)} %copy-done.1, ...), custom_call_target="tpu_custom_call" | custom-call | flops 4294967296 | bytes 16777216 | tf_op jit(solution)/shard_map/pallas_call | solution.py:166
  96.8 1.0 copy-done.8
  97.8 4.8 %shard_map.92 = bf16[1024,512]{1,0:T(8,128)(2,1)} custom-call(bf16[1024,1024]{1,0:T(8,128)(2,1)} %get-tuple-element.18.left_ref, bf16[1024,512]{1,0:T(8,128)(2,1)} %copy-done.8), custom_call_target="tpu_custom_call" | custom-call | flops 1073741824 | bytes 3145728 | tf_op jit(solution)/shard_map/pallas_call | solution.py:186
  103.4 0.9 copy-done.3
  106.2 11.4 %shard_map.86 = (f32[1,2048,512]{2,1,0:T(8,128)}, f32[1,2048,512]{2,1,0:T(8,128)}, bf16[1024,1024]{1,0:T(8,128)(2,1)}, bf16[1024,512]{1,0:T(8,128)(2,1)S(1)}, bf16[1024,512]{1,0:T(8,128)(2,1)}) custom-call(f32[1,1]{1,0:T(1,128)S(6)} %div.7.refs_0_, bf16[1,1024,128]{2,1,0:T(8,128)(2,1)S(1)} %copy-done.1, ...), custom_call_target="tpu_custom_call", output_to_operand_aliasing={{0}: (22, {}), {1}: (23, {})} | custom-call | flops 4294967296 | bytes 16777216 | tf_op jit(solution)/shard_map/pallas_call | solution.py:166
  117.6 1.0 copy-done
  118.6 3.0 %shard_map.90 = bf16[512,512]{1,0:T(8,128)(2,1)} custom-call(bf16[1024,1024]{1,0:T(8,128)(2,1)} %get-tuple-element.15.left_ref, bf16[1024,512]{1,0:T(8,128)(2,1)} %copy-done), custom_call_target="tpu_custom_call" | custom-call | flops 536870912 | bytes 2097152 | tf_op jit(solution)/shard_map/pallas_call | solution.py:186
  121.5 1.2 collective-permute-start.28
  122.7 2.5 %shard_map.89 = bf16[256,512]{1,0:T(8,128)(2,1)} custom-call(bf16[1024,1024]{1,0:T(8,128)(2,1)} %get-tuple-element.15.left_ref, bf16[1024,512]{1,0:T(8,128)(2,1)} %copy-done), custom_call_target="tpu_custom_call" | custom-call | flops 268435456 | bytes 1572864 | tf_op jit(solution)/shard_map/pallas_call | solution.py:186
  126.1 2.5 %shard_map.88 = bf16[256,512]{1,0:T(8,128)(2,1)} custom-call(bf16[1024,1024]{1,0:T(8,128)(2,1)} %get-tuple-element.15.left_ref, bf16[1024,512]{1,0:T(8,128)(2,1)} %copy-done), custom_call_target="tpu_custom_call" | custom-call | flops 268435456 | bytes 1572864 | tf_op jit(solution)/shard_map/pallas_call | solution.py:186
  128.6 1.2 collective-permute-start.26
  129.8 5.1 %shard_map.91.base_ref = f32[1024,512]{1,0:T(8,128)} custom-call(bf16[1024,1024]{1,0:T(8,128)(2,1)} %get-tuple-element.18.left_ref, bf16[1024,512]{1,0:T(8,128)(2,1)} %get-tuple-element.19.term_ref, bf16[1,2048,512]{2,1,0:T(8,128)(2,1)} %weight_ref.3), custom_call_target="tpu_custom_call" | custom-call | flops 1073741824 | bytes 4194304 | tf_op jit(solution)/shard_map/pallas_call | solution.py:209
  135.0 5.2 %shard_map.87.base_ref = f32[1024,512]{1,0:T(8,128)} custom-call(bf16[1024,1024]{1,0:T(8,128)(2,1)} %get-tuple-element.15.left_ref, bf16[1024,512]{1,0:T(8,128)(2,1)} %get-tuple-element.16.term_ref, bf16[1,2048,512]{2,1,0:T(8,128)(2,1)} %weight_ref.3), custom_call_target="tpu_custom_call" | custom-call | flops 1073741824 | bytes 4194304 | tf_op jit(solution)/shard_map/pallas_call | solution.py:209
  140.1 5.6 %shard_map.93.refs_0_ = bf16[1,2048,512]{2,1,0:T(8,128)(2,1)} custom-call(f32[1024,512]{1,0:T(8,128)} %shard_map.91.base_ref, bf16[1024,512]{1,0:T(8,128)(2,1)} %collective-permute-done.29.received_ref), custom_call_target="tpu_custom_call" | custom-call | flops 1048576 | bytes 4194304 | tf_op jit(solution)/shard_map/pallas_call | solution.py:241
  146.5 3.4 %shard_map.94.refs_0_ = bf16[1,2048,512]{2,1,0:T(8,128)(2,1)} custom-call(f32[1024,512]{1,0:T(8,128)} %shard_map.87.base_ref, bf16[512,512]{1,0:T(8,128)(2,1)} %copy-done.11, bf16[1,2048,512]{2,1,0:T(8,128)(2,1)} %shard_map.93.refs_0_), custom_call_target="tpu_custom_call", output_to_operand_aliasing={{}: (2, {})} | custom-call | flops 524288 | bytes 2097152 | tf_op jit(solution)/shard_map/pallas_call | solution.py:241
  150.6 1.8 %shard_map.95.refs_0_ = bf16[1,2048,512]{2,1,0:T(8,128)(2,1)} custom-call(f32[1024,512]{1,0:T(8,128)} %shard_map.87.base_ref, bf16[256,512]{1,0:T(8,128)(2,1)} %copy-done.13, bf16[1,2048,512]{2,1,0:T(8,128)(2,1)} %shard_map.94.refs_0_), custom_call_target="tpu_custom_call", output_to_operand_aliasing={{}: (2, {})} | custom-call | flops 262144 | bytes 1048576 | tf_op jit(solution)/shard_map/pallas_call | solution.py:241
  153.2 1.8 %shard_map.96 = bf16[1,2048,512]{2,1,0:T(8,128)(2,1)} custom-call(f32[1024,512]{1,0:T(8,128)} %shard_map.87.base_ref, bf16[256,512]{1,0:T(8,128)(2,1)} %copy-done.12, bf16[1,2048,512]{2,1,0:T(8,128)(2,1)} %shard_map.95.refs_0_), custom_call_target="tpu_custom_call", output_to_operand_aliasing={{}: (2, {})} | custom-call | flops 262144 | bytes 1048576 | tf_op jit(solution)/shard_map/pallas_call | solution.py:241
  (54 shorter events, 9.8 us)
Async XLA Ops:
  0.6 12.0 %copy-start.9 = (bf16[1,2048,512]{2,1,0:T(8,128)(2,1)S(1)}, bf16[1,2048,512]{2,1,0:T(8,128)(2,1)}, u32[]{:S(2)}) copy-start(bf16[1,2048,512]{2,1,0:T(8,128)(2,1)} %refs_17_.3) | copy-start | bytes 6291460
  0.6 51.4 %collective-permute-start.9 = (bf16[1,1024,128]{2,1,0:T(8,128)(2,1)}, bf16[1,1024,128]{2,1,0:T(8,128)(2,1)S(1)}, u32[]{:S(2)}, u32[]{:S(2)}) collective-permute-start(bf16[1,1024,128]{2,1,0:T(8,128)(2,1)} %refs_1_.3), channel_id=1, source_target_pairs={{0,1},{1,0},{2,3},{3,2},{4,5},{5,4},{6,7},{7,6},{8,9},{9,8},{10,11... | collective-permute-start | bytes 786440 | tf_op jit(solution)/shard_map/ppermute | solution.py:33
  2.4 50.7 %collective-permute-start.10 = (bf16[1,1024,128]{2,1,0:T(8,128)(2,1)}, bf16[1,1024,128]{2,1,0:T(8,128)(2,1)S(1)}, u32[]{:S(2)}, u32[]{:S(2)}) collective-permute-start(bf16[1,1024,128]{2,1,0:T(8,128)(2,1)} %refs_1_.3), channel_id=1, source_target_pairs={{0,3},{1,2},{2,1},{3,0},{4,7},{5,6},{6,5},{7,4},{8,11},{9,10},{10,... | collective-permute-start | bytes 786440 | tf_op jit(solution)/shard_map/ppermute | solution.py:33
  4.6 48.5 %collective-permute-start.12 = (bf16[1,1024,128]{2,1,0:T(8,128)(2,1)}, bf16[1,1024,128]{2,1,0:T(8,128)(2,1)S(1)}, u32[]{:S(2)}, u32[]{:S(2)}) collective-permute-start(bf16[1,1024,128]{2,1,0:T(8,128)(2,1)} %refs_1_.3), channel_id=1, source_target_pairs={{0,4},{4,8},{8,12},{12,0},{1,5},{5,9},{9,13},{13,1},{2,6},{6,10},{... | collective-permute-start | bytes 786440 | tf_op jit(solution)/shard_map/ppermute | solution.py:33
  6.5 49.9 %collective-permute-start.16 = (bf16[1,1024,128]{2,1,0:T(8,128)(2,1)}, bf16[1,1024,128]{2,1,0:T(8,128)(2,1)S(1)}, u32[]{:S(2)}, u32[]{:S(2)}) collective-permute-start(bf16[1,1024,128]{2,1,0:T(8,128)(2,1)} %refs_1_.3), channel_id=1, source_target_pairs={{0,12},{4,0},{8,4},{12,8},{1,13},{5,1},{9,5},{13,9},{2,14},{6,2},{... | collective-permute-start | bytes 786440 | tf_op jit(solution)/shard_map/ppermute | solution.py:33
  11.9 73.5 %copy-start.1 = (bf16[1,1024,128]{2,1,0:T(8,128)(2,1)S(1)}, bf16[1,1024,128]{2,1,0:T(8,128)(2,1)}, u32[]{:S(2)}) copy-start(bf16[1,1024,128]{2,1,0:T(8,128)(2,1)} %refs_1_.3) | copy-start | bytes 786436
  11.9 3.7 %collective-permute-start = (f32[1,1]{1,0:T(1,128)}, f32[1,1]{1,0:T(1,128)}, u32[]{:S(2)}, u32[]{:S(2)}) collective-permute-start(f32[1,1]{1,0:T(1,128)} %bitcast), channel_id=1, source_target_pairs={{0,1},{1,0},{2,3},{3,2},{4,5},{5,4},{6,7},{7,6},{8,9},{9,8},{10,11... | collective-permute-start | bytes 20 | tf_op jit(solution)/shard_map/ppermute | solution.py:33
  16.8 1.2 collective-permute-start.1
  18.7 4.8 %collective-permute-start.2 = (f32[1,1]{1,0:T(1,128)}, f32[1,1]{1,0:T(1,128)}, u32[]{:S(2)}, u32[]{:S(2)}) collective-permute-start(f32[1,1]{1,0:T(1,128)} %add.28), channel_id=1, source_target_pairs={{0,32},{32,64},{64,96},{96,0},{1,33},{33,65},{65,97},{97,1},{2,34}... | collective-permute-start | bytes 20 | tf_op jit(solution)/shard_map/ppermute | solution.py:33
  23.5 3.5 %collective-permute-start.3 = (f32[1,1]{1,0:T(1,128)}, f32[1,1]{1,0:T(1,128)}, u32[]{:S(2)}, u32[]{:S(2)}) collective-permute-start(f32[1,1]{1,0:T(1,128)} %add.28), channel_id=1, source_target_pairs={{0,96},{32,0},{64,32},{96,64},{1,97},{33,1},{65,33},{97,65},{2,98}... | collective-permute-start | bytes 20 | tf_op jit(solution)/shard_map/ppermute | solution.py:33
  27.0 5.1 %collective-permute-start.4 = (f32[1,1]{1,0:T(1,128)}, f32[1,1]{1,0:T(1,128)}, u32[]{:S(2)}, u32[]{:S(2)}) collective-permute-start(f32[1,1]{1,0:T(1,128)} %add.28), channel_id=1, source_target_pairs={{0,64},{32,96},{64,0},{96,32},{1,65},{33,97},{65,1},{97,33},{2,66}... | collective-permute-start | bytes 20 | tf_op jit(solution)/shard_map/ppermute | solution.py:33
  32.8 4.8 %collective-permute-start.5 = (f32[1,1]{1,0:T(1,128)}, f32[1,1]{1,0:T(1,128)}, u32[]{:S(2)}, u32[]{:S(2)}) collective-permute-start(f32[1,1]{1,0:T(1,128)} %add.31), channel_id=1, source_target_pairs={{0,3},{1,2},{2,1},{3,0},{4,7},{5,6},{6,5},{7,4},{8,11},{9,10},{10,... | collective-permute-start | bytes 20 | tf_op jit(solution)/shard_map/ppermute | solution.py:33
  38.2 5.0 %collective-permute-start.6 = (f32[1,1]{1,0:T(1,128)}, f32[1,1]{1,0:T(1,128)}, u32[]{:S(2)}, u32[]{:S(2)}) collective-permute-start(f32[1,1]{1,0:T(1,128)} %add.32), channel_id=1, source_target_pairs={{0,4},{4,8},{8,12},{12,0},{1,5},{5,9},{9,13},{13,1},{2,6},{6,10},{... | collective-permute-start | bytes 20 | tf_op jit(solution)/shard_map/ppermute | solution.py:33
  43.2 3.7 %collective-permute-start.7 = (f32[1,1]{1,0:T(1,128)}, f32[1,1]{1,0:T(1,128)}, u32[]{:S(2)}, u32[]{:S(2)}) collective-permute-start(f32[1,1]{1,0:T(1,128)} %add.32), channel_id=1, source_target_pairs={{0,12},{4,0},{8,4},{12,8},{1,13},{5,1},{9,5},{13,9},{2,14},{6,2},{... | collective-permute-start | bytes 20 | tf_op jit(solution)/shard_map/ppermute | solution.py:33
  46.9 5.2 %collective-permute-start.8 = (f32[1,1]{1,0:T(1,128)}, f32[1,1]{1,0:T(1,128)}, u32[]{:S(2)}, u32[]{:S(2)}) collective-permute-start(f32[1,1]{1,0:T(1,128)} %add.32), channel_id=1, source_target_pairs={{0,8},{4,12},{8,0},{12,4},{1,9},{5,13},{9,1},{13,5},{2,10},{6,14},... | collective-permute-start | bytes 20 | tf_op jit(solution)/shard_map/ppermute | solution.py:33
  52.1 32.3 %collective-permute-start.25 = (bf16[1,1024,512]{2,1,0:T(8,128)(2,1)S(1)}, bf16[1,1024,512]{2,1,0:T(8,128)(2,1)S(1)}, u32[]{:S(2)}, u32[]{:S(2)}) collective-permute-start(bf16[1,1024,512]{2,1,0:T(8,128)(2,1)S(1)} %get-tuple-element.23), channel_id=1, source_target_pairs={{0,1},{1,0},{2,3},{3,2},{4,5},{5,4},{6,7},{7,6},{8,9},{9,8},{10,11... | collective-permute-start | bytes 3145736 | tf_op jit(solution)/shard_map/ppermute | solution.py:33
  52.1 7.6 %collective-permute-start.11 = (bf16[1,1024,128]{2,1,0:T(8,128)(2,1)S(1)}, bf16[1,1024,128]{2,1,0:T(8,128)(2,1)S(1)}, u32[]{:S(2)}, u32[]{:S(2)}) collective-permute-start(bf16[1,1024,128]{2,1,0:T(8,128)(2,1)S(1)} %collective-permute-done.9.refs_2_), channel_id=1, source_target_pairs={{0,3},{1,2},{2,1},{3,0},{4,7},{5,6},{6,5},{7,4},{8,11},{9,10},{10,... | collective-permute-start | bytes 786440 | tf_op jit(solution)/shard_map/ppermute | solution.py:33
  53.1 10.4 %collective-permute-start.13 = (bf16[1,1024,128]{2,1,0:T(8,128)(2,1)S(1)}, bf16[1,1024,128]{2,1,0:T(8,128)(2,1)S(1)}, u32[]{:S(2)}, u32[]{:S(2)}) collective-permute-start(bf16[1,1024,128]{2,1,0:T(8,128)(2,1)S(1)} %collective-permute-done.9.refs_2_), channel_id=1, source_target_pairs={{0,4},{4,8},{8,12},{12,0},{1,5},{5,9},{9,13},{13,1},{2,6},{6,10},{... | collective-permute-start | bytes 786440 | tf_op jit(solution)/shard_map/ppermute | solution.py:33
  53.1 10.4 %collective-permute-start.18 = (bf16[1,1024,128]{2,1,0:T(8,128)(2,1)S(1)}, bf16[1,1024,128]{2,1,0:T(8,128)(2,1)S(1)}, u32[]{:S(2)}, u32[]{:S(2)}) collective-permute-start(bf16[1,1024,128]{2,1,0:T(8,128)(2,1)S(1)} %collective-permute-done.10.refs_3_), channel_id=1, source_target_pairs={{0,12},{4,0},{8,4},{12,8},{1,13},{5,1},{9,5},{13,9},{2,14},{6,2},{... | collective-permute-start | bytes 786440 | tf_op jit(solution)/shard_map/ppermute | solution.py:33
  56.4 10.4 %collective-permute-start.17 = (bf16[1,1024,128]{2,1,0:T(8,128)(2,1)S(1)}, bf16[1,1024,128]{2,1,0:T(8,128)(2,1)S(1)}, u32[]{:S(2)}, u32[]{:S(2)}) collective-permute-start(bf16[1,1024,128]{2,1,0:T(8,128)(2,1)S(1)} %collective-permute-done.9.refs_2_), channel_id=1, source_target_pairs={{0,12},{4,0},{8,4},{12,8},{1,13},{5,1},{9,5},{13,9},{2,14},{6,2},{... | collective-permute-start | bytes 786440 | tf_op jit(solution)/shard_map/ppermute | solution.py:33
  59.6 10.4 %collective-permute-start.14 = (bf16[1,1024,128]{2,1,0:T(8,128)(2,1)S(1)}, bf16[1,1024,128]{2,1,0:T(8,128)(2,1)S(1)}, u32[]{:S(2)}, u32[]{:S(2)}) collective-permute-start(bf16[1,1024,128]{2,1,0:T(8,128)(2,1)S(1)} %collective-permute-done.10.refs_3_), channel_id=1, source_target_pairs={{0,4},{4,8},{8,12},{12,0},{1,5},{5,9},{9,13},{13,1},{2,6},{6,10},{... | collective-permute-start | bytes 786440 | tf_op jit(solution)/shard_map/ppermute | solution.py:33
  63.5 10.9 %collective-permute-start.20 = (bf16[1,1024,128]{2,1,0:T(8,128)(2,1)S(1)}, bf16[1,1024,128]{2,1,0:T(8,128)(2,1)S(1)}, u32[]{:S(2)}, u32[]{:S(2)}) collective-permute-start(bf16[1,1024,128]{2,1,0:T(8,128)(2,1)S(1)} %collective-permute-done.12.refs_5_), channel_id=1, source_target_pairs={{0,4},{4,8},{8,12},{12,0},{1,5},{5,9},{9,13},{13,1},{2,6},{6,10},{... | collective-permute-start | bytes 786440 | tf_op jit(solution)/shard_map/ppermute | solution.py:33
  63.5 10.9 %collective-permute-start.19 = (bf16[1,1024,128]{2,1,0:T(8,128)(2,1)S(1)}, bf16[1,1024,128]{2,1,0:T(8,128)(2,1)S(1)}, u32[]{:S(2)}, u32[]{:S(2)}) collective-permute-start(bf16[1,1024,128]{2,1,0:T(8,128)(2,1)S(1)} %collective-permute-done.11.refs_4_), channel_id=1, source_target_pairs={{0,12},{4,0},{8,4},{12,8},{1,13},{5,1},{9,5},{13,9},{2,14},{6,2},{... | collective-permute-start | bytes 786440 | tf_op jit(solution)/shard_map/ppermute | solution.py:33
  66.8 10.9 %collective-permute-start.15 = (bf16[1,1024,128]{2,1,0:T(8,128)(2,1)S(1)}, bf16[1,1024,128]{2,1,0:T(8,128)(2,1)S(1)}, u32[]{:S(2)}, u32[]{:S(2)}) collective-permute-start(bf16[1,1024,128]{2,1,0:T(8,128)(2,1)S(1)} %collective-permute-done.11.refs_4_), channel_id=1, source_target_pairs={{0,4},{4,8},{8,12},{12,0},{1,5},{5,9},{9,13},{13,1},{2,6},{6,10},{... | collective-permute-start | bytes 786440 | tf_op jit(solution)/shard_map/ppermute | solution.py:33
  70.0 33.3 %collective-permute-start.24 = (bf16[1,1024,512]{2,1,0:T(8,128)(2,1)}, bf16[1,1024,512]{2,1,0:T(8,128)(2,1)}, u32[]{:S(2)}, u32[]{:S(2)}) collective-permute-start(bf16[1,1024,512]{2,1,0:T(8,128)(2,1)} %get-tuple-element.24), channel_id=1, source_target_pairs={{0,1},{1,0},{2,3},{3,2},{4,5},{5,4},{6,7},{7,6},{8,9},{9,8},{10,11... | collective-permute-start | bytes 3145736 | tf_op jit(solution)/shard_map/ppermute | solution.py:33
  74.4 7.6 %collective-permute-start.21 = (bf16[1,1024,128]{2,1,0:T(8,128)(2,1)S(1)}, bf16[1,1024,128]{2,1,0:T(8,128)(2,1)S(1)}, u32[]{:S(2)}, u32[]{:S(2)}) collective-permute-start(bf16[1,1024,128]{2,1,0:T(8,128)(2,1)S(1)} %collective-permute-done.13.refs_6_), channel_id=1, source_target_pairs={{0,4},{4,8},{8,12},{12,0},{1,5},{5,9},{9,13},{13,1},{2,6},{6,10},{... | collective-permute-start | bytes 786440 | tf_op jit(solution)/shard_map/ppermute | solution.py:33
  74.4 7.6 %collective-permute-start.22 = (bf16[1,1024,128]{2,1,0:T(8,128)(2,1)S(1)}, bf16[1,1024,128]{2,1,0:T(8,128)(2,1)S(1)}, u32[]{:S(2)}, u32[]{:S(2)}) collective-permute-start(bf16[1,1024,128]{2,1,0:T(8,128)(2,1)S(1)} %collective-permute-done.18.refs_11_), channel_id=1, source_target_pairs={{0,12},{4,0},{8,4},{12,8},{1,13},{5,1},{9,5},{13,9},{2,14},{6,2},{... | collective-permute-start | bytes 786440 | tf_op jit(solution)/shard_map/ppermute | solution.py:33
  77.6 6.7 %collective-permute-start.23 = (bf16[1,1024,128]{2,1,0:T(8,128)(2,1)S(1)}, bf16[1,1024,128]{2,1,0:T(8,128)(2,1)S(1)}, u32[]{:S(2)}, u32[]{:S(2)}) collective-permute-start(bf16[1,1024,128]{2,1,0:T(8,128)(2,1)S(1)} %collective-permute-done.19.refs_12_), channel_id=1, source_target_pairs={{0,12},{4,0},{8,4},{12,8},{1,13},{5,1},{9,5},{13,9},{2,14},{6,2},{... | collective-permute-start | bytes 786440 | tf_op jit(solution)/shard_map/ppermute | solution.py:33
  82.0 14.8 %copy-start.2 = (bf16[1,1024,128]{2,1,0:T(8,128)(2,1)}, bf16[1,1024,128]{2,1,0:T(8,128)(2,1)S(1)}, u32[]{:S(2)}) copy-start(bf16[1,1024,128]{2,1,0:T(8,128)(2,1)S(1)} %collective-permute-done.21.refs_14_) | copy-start | bytes 786436
  82.0 14.8 %copy-start.4 = (bf16[1,1024,128]{2,1,0:T(8,128)(2,1)}, bf16[1,1024,128]{2,1,0:T(8,128)(2,1)S(1)}, u32[]{:S(2)}) copy-start(bf16[1,1024,128]{2,1,0:T(8,128)(2,1)S(1)} %collective-permute-done.22.refs_15_) | copy-start | bytes 786436
  84.3 12.4 %copy-start.6 = (bf16[1,1024,128]{2,1,0:T(8,128)(2,1)}, bf16[1,1024,128]{2,1,0:T(8,128)(2,1)S(1)}, u32[]{:S(2)}) copy-start(bf16[1,1024,128]{2,1,0:T(8,128)(2,1)S(1)} %collective-permute-done.23.refs_16_) | copy-start | bytes 786436
  84.3 1.0 copy-start.10
  96.8 1.0 copy-start.8
  102.5 37.6 %collective-permute-start.29 = (bf16[1024,512]{1,0:T(8,128)(2,1)}, bf16[1024,512]{1,0:T(8,128)(2,1)}, u32[]{:S(2)}, u32[]{:S(2)}) collective-permute-start(bf16[1024,512]{1,0:T(8,128)(2,1)} %shard_map.92), channel_id=1, source_target_pairs={{0,1},{1,0},{2,3},{3,2},{4,5},{5,4},{6,7},{7,6},{8,9},{9,8},{10,11... | collective-permute-start | bytes 3145736 | tf_op jit(solution)/shard_map/ppermute | solution.py:33
  103.4 1.0 copy-start.3
  104.3 0.9 copy-start.5
  105.3 0.9 copy-start.7
  117.6 1.0 copy-start
  121.5 24.2 %collective-permute-start.28 = (bf16[512,512]{1,0:T(8,128)(2,1)}, bf16[512,512]{1,0:T(8,128)(2,1)S(1)}, u32[]{:S(2)}, u32[]{:S(2)}) collective-permute-start(bf16[512,512]{1,0:T(8,128)(2,1)} %shard_map.90), channel_id=1, source_target_pairs={{0,1},{1,0},{2,3},{3,2},{4,5},{5,4},{6,7},{7,6},{8,9},{9,8},{10,11... | collective-permute-start | bytes 1572872 | tf_op jit(solution)/shard_map/ppermute | solution.py:33
  125.3 24.6 %collective-permute-start.27 = (bf16[256,512]{1,0:T(8,128)(2,1)}, bf16[256,512]{1,0:T(8,128)(2,1)S(1)}, u32[]{:S(2)}, u32[]{:S(2)}) collective-permute-start(bf16[256,512]{1,0:T(8,128)(2,1)} %shard_map.89), channel_id=1, source_target_pairs={{0,1},{1,0},{2,3},{3,2},{4,5},{5,4},{6,7},{7,6},{8,9},{9,8},{10,11... | collective-permute-start | bytes 786440 | tf_op jit(solution)/shard_map/ppermute | solution.py:33
  128.6 23.8 %collective-permute-start.26 = (bf16[256,512]{1,0:T(8,128)(2,1)}, bf16[256,512]{1,0:T(8,128)(2,1)S(1)}, u32[]{:S(2)}, u32[]{:S(2)}) collective-permute-start(bf16[256,512]{1,0:T(8,128)(2,1)} %shard_map.88), channel_id=1, source_target_pairs={{0,1},{1,0},{2,3},{3,2},{4,5},{5,4},{6,7},{7,6},{8,9},{9,8},{10,11... | collective-permute-start | bytes 786440 | tf_op jit(solution)/shard_map/ppermute | solution.py:33
  145.7 0.8 copy-start.11
  149.9 0.7 copy-start.13
  152.4 0.7 copy-start.12

commit v2 on v0

v2 whole, which is shorter than its diff:
```python
import functools

import jax
import jax.numpy as jnp
from jax import lax
from jax.experimental import pallas as pl
from jax.experimental.pallas import tpu as pltpu
from jax.sharding import Mesh
from jax.sharding import PartitionSpec as P


AXES = ("x", "core", "z", "y")
EXPERT = ("x", "core")
TILE = ("z", "y")

beta_one = 0.9
beta_two = 0.95
epsilon = 1e-08
learn_rate = 0.25
decay_rate = 0.1


f32 = jnp.float32
bf16 = jnp.bfloat16
ANY = pl.BlockSpec(memory_space=pl.ANY)
MIB = 1024 * 1024
PIECES = ((0, 512), (512, 384), (896, 128))


def cost(flops, bytes_accessed):
    return pl.CostEstimate(flops=flops, bytes_accessed=bytes_accessed, transcendentals=0)


def limit(mib):
    return pltpu.CompilerParams(vmem_limit_bytes=mib * MIB)


def near(i):
    return i ^ 1


def far(i):
    return 3 - i


def permute(value, axis, target):
    pairs = [(source, target(source)) for source in range(lax.axis_size(axis))]
    return lax.ppermute(value, axis, pairs)


def every_sum(value):
    devices = lax.axis_size(AXES)
    return lax.all_to_all(jnp.broadcast_to(value, (devices, 1, 128)), AXES, 0, 0, tiled=True)


def gather_left(shard):
    row = jnp.concatenate((shard, permute(shard, "y", near)), axis=1)
    row_far = permute(row, "y", far)
    near0 = permute(row, "z", near)
    far0 = permute(row, "z", far)
    near1 = permute(row_far, "z", near)
    far1 = permute(row_far, "z", far)
    far2 = permute(jnp.concatenate((near0, near1), axis=1), "z", far)
    return row, (row, row_far, near0, near1), (far0, far1, far2)


def rotate_right_kernel(own_ref, other_ref, right_ref, out_ref):
    width = right_ref.shape[2]
    position = lax.rem(lax.axis_index("y"), 2)
    right_own = right_ref[0, pl.ds(pl.multiple_of(position * width, width), width), :]
    right_other = right_ref[0, pl.ds(pl.multiple_of((1 - position) * width, width), width), :]
    out_ref[...] = (
        jnp.dot(own_ref[0], right_own, preferred_element_type=f32)
        + jnp.dot(other_ref[0], right_other, preferred_element_type=f32)
    ).astype(bf16)


def rotate_right(own, other, right):
    _, block, width = own.shape
    rows = 256
    chunk = pl.BlockSpec((1, rows, width), lambda s: (0, s, 0))
    return pl.pallas_call(
        rotate_right_kernel,
        grid=(block // rows,),
        out_shape=jax.ShapeDtypeStruct((block, width), bf16),
        in_specs=[chunk, chunk, pl.BlockSpec((1, block, width), lambda s: (0, 0, 0))],
        out_specs=pl.BlockSpec((rows, width), lambda s: (s, 0)),
        cost_estimate=cost(4 * block * width * width, 8 * block * width),
        compiler_params=limit(58),
    )(own, other, right)


def moments_kernel(is_near, groups, count, block_ref, sums_ref, *refs):
    shards = refs[:groups]
    term_ref, right_ref, first_ref, second_ref = refs[groups : groups + 4]
    new_first_ref, new_second_ref, send_ref, turned_ref, left_ref, update_ref, sems = refs[-7:]
    width = right_ref.shape[2]
    block = left_ref.shape[0]
    rows = new_first_ref.shape[1]
    steps = block // rows
    z = lax.axis_index("z")
    y = lax.axis_index("y")
    step = pl.program_id(0)

    @pl.when(step == 0)
    def _():
        partner = y + 1 - 2 * lax.rem(y, 2)
        columns = (y, partner, 3 - y, 3 - partner)
        if is_near:
            parity = lax.rem(z, 2)
            places = [(0, 0, 0), (0, 1, 0), (1, 0, 0), (1, 1, 0), (2, 0, 1), (2, 1, 1), (3, 0, 1), (3, 1, 1)]
        else:
            parity = lax.rem(z + 1, 2)
            places = [(0, 0, 0), (0, 1, 0), (1, 0, 0), (1, 1, 0), (2, 0, 1), (2, 1, 1), (2, 2, 1), (2, 3, 1)]
        copies = []
        for k, (group, part, other_row) in enumerate(places):
            row = 1 - parity if other_row else parity
            slot = row * 4 + columns[k % 4]
            copies.append(
                pltpu.make_async_copy(
                    shards[group].at[0, pl.ds(part * block, block), :],
                    left_ref.at[:, pl.ds(pl.multiple_of(slot * 128, 128), 128)],
                    sems.at[k],
                )
            )
        for copy in copies:
            copy.start()
        for copy in copies:
            copy.wait()

    @pl.when(step < steps)
    def _():
        chunk = pl.ds(pl.multiple_of(step * rows, rows), rows)
        rotated = lax.dot_general(
            left_ref[:, chunk], term_ref[...], (((0,), (0,)), ((), ())), preferred_element_type=f32
        )
        total = jnp.sum(sums_ref[...], axis=0)
        clip = 1.0 / jnp.maximum(1.0, jnp.sqrt(total / count))
        clipped = jnp.concatenate([clip] * (width // 128), axis=1) * rotated
        new_first = beta_one * first_ref[0] + (1.0 - beta_one) * clipped
        new_second = beta_two * second_ref[0] + (1.0 - beta_two) * clipped * clipped
        new_first_ref[0] = new_first
        new_second_ref[0] = new_second
        update_ref[chunk, :] = (new_first / (jnp.sqrt(new_second) + epsilon)).astype(bf16)

    @pl.when(step >= steps)
    def _():
        position = lax.rem(y, 2)
        right_other = right_ref[0, pl.ds(pl.multiple_of((1 - position) * width, width), width), :]
        chunk = pl.ds(pl.multiple_of((step - steps) * rows, rows), rows)
        turned = jnp.dot(left_ref[chunk, :], update_ref[...], preferred_element_type=f32).astype(bf16)
        turned_ref[...] = turned
        send_ref[...] = lax.dot_general(
            turned, right_other, (((1,), (1,)), ((), ())), preferred_element_type=f32
        ).astype(bf16)


def moments(is_near, which, sums, shards, term, right, first, second, previous):
    _, all_rows, width = first.shape
    block = right.shape[1]
    rows = 256
    steps = block // rows
    groups = len(shards)
    count = sums.shape[0] * all_rows * width
    moment = pl.BlockSpec(
        (1, rows, width), lambda s, b: (0, b[0] * steps + jnp.minimum(s, steps - 1), 0)
    )
    late = pl.BlockSpec((rows, width), lambda s, b: (jnp.maximum(s - steps, 0), 0))
    whole = jax.ShapeDtypeStruct((1, all_rows, width), f32)
    part = jax.ShapeDtypeStruct((block, width), bf16)
    in_specs = [pl.BlockSpec(sums.shape, lambda s, b: (0, 0, 0))] + [ANY] * groups
    in_specs += [
        pl.BlockSpec((block, width), lambda s, b: (0, 0)),
        pl.BlockSpec((1, block, width), lambda s, b: (0, 0, 0)),
        moment,
        moment,
    ]
    operands = [which, sums, *shards, term, right, first, second]
    aliases = {}
    if previous is not None:
        in_specs += [ANY, ANY]
        aliases = {len(operands): 0, len(operands) + 1: 1}
        operands += list(previous)
    return pl.pallas_call(
        functools.partial(moments_kernel, is_near, groups, count),
        grid_spec=pltpu.PrefetchScalarGridSpec(
            num_scalar_prefetch=1,
            grid=(2 * steps,),
            in_specs=in_specs,
            out_specs=[moment, moment, late, late],
            scratch_shapes=[
                pltpu.VMEM((block, block), bf16),
                pltpu.VMEM((block, width), bf16),
                pltpu.SemaphoreType.DMA((8,)),
            ],
        ),
        out_shape=[whole, whole, part, part],
        input_output_aliases=aliases,
        cost_estimate=cost(5 * block * block * width, 20 * block * width),
        compiler_params=limit(58),
    )(*operands)


def base_kernel(block_ref, turned_ref, right_ref, weight_ref, out_ref):
    width = right_ref.shape[2]
    position = lax.rem(lax.axis_index("y"), 2)
    right_own = right_ref[0, pl.ds(pl.multiple_of(position * width, width), width), :]
    back = lax.dot_general(
        turned_ref[...], right_own, (((1,), (1,)), ((), ())), preferred_element_type=f32
    )
    weight = weight_ref[0].astype(f32)
    out_ref[...] = weight - learn_rate * (back + decay_rate * weight)


def base(which, turned, right, weight):
    block, width = turned.shape
    rows = 256
    steps = block // rows
    return pl.pallas_call(
        base_kernel,
        grid_spec=pltpu.PrefetchScalarGridSpec(
            num_scalar_prefetch=1,
            grid=(steps,),
            in_specs=[
                pl.BlockSpec((rows, width), lambda s, b: (s, 0)),
                pl.BlockSpec((1, block, width), lambda s, b: (0, 0, 0)),
                pl.BlockSpec((1, rows, width), lambda s, b: (0, b[0] * steps + s, 0)),
            ],
            out_specs=pl.BlockSpec((rows, width), lambda s, b: (s, 0)),
        ),
        out_shape=jax.ShapeDtypeStruct((block, width), f32),
        cost_estimate=cost(2 * block * width * width, 10 * block * width),
        compiler_params=limit(12),
    )(which, turned, right, weight)


def finish_kernel(block_ref, base_ref, received_ref, *refs):
    refs[-1][0] = (base_ref[...] - learn_rate * received_ref[...].astype(f32)).astype(bf16)


def finish(which, base_term, received, start, total_rows, previous):
    block = base_term.shape[0]
    count, width = received.shape
    rows = 128
    in_specs = [
        pl.BlockSpec((rows, width), lambda s, b: (start // rows + s, 0)),
        pl.BlockSpec((rows, width), lambda s, b: (s, 0)),
    ]
    operands = [which, base_term, received]
    aliases = {}
    if previous is not None:
        in_specs.append(ANY)
        aliases = {len(operands): 0}
        operands.append(previous)
    return pl.pallas_call(
        finish_kernel,
        grid_spec=pltpu.PrefetchScalarGridSpec(
            num_scalar_prefetch=1,
            grid=(count // rows,),
            in_specs=in_specs,
            out_specs=pl.BlockSpec(
                (1, rows, width), lambda s, b: (0, (b[0] * block + start) // rows + s, 0)
            ),
        ),
        out_shape=jax.ShapeDtypeStruct((1, total_rows, width), bf16),
        input_output_aliases=aliases,
        cost_estimate=cost(2 * count * width, 8 * count * width),
        compiler_params=limit(8),
    )(*operands)


def on_device(weight, grad, first_moment, second_moment, left_basis, right_basis):
    _, rows, _ = grad.shape
    block = right_basis.shape[1]
    near_block = lax.axis_index("z") // 2
    far_block = 1 - near_block
    near_id = near_block.reshape(1)
    far_id = far_block.reshape(1)

    own_near = lax.dynamic_slice_in_dim(grad, near_block * block, block, axis=1)
    other_near = permute(own_near, "y", near)

    sums = every_sum(jnp.sum(jnp.square(grad.astype(f32))).reshape(1, 1, 1))
    row, left_near, left_far = gather_left(left_basis)

    later_block, _ = lax.optimization_barrier((far_block, row))
    own_far = lax.dynamic_slice_in_dim(grad, later_block * block, block, axis=1)
    other_far = permute(own_far, "y", near)

    term = rotate_right(own_near, other_near, right_basis)
    nf, ns, send, turned = moments(
        True, near_id, sums, left_near, term, right_basis, first_moment, second_moment, None
    )
    received_near = permute(send, "y", near)
    base_near = base(near_id, turned, right_basis, weight)

    term = rotate_right(own_far, other_far, right_basis)
    nf, ns, send, turned = moments(
        False, far_id, sums, left_far, term, right_basis, first_moment, second_moment, (nf, ns)
    )
    received_far = [permute(send[start : start + size], "y", near) for start, size in PIECES]
    base_far = base(far_id, turned, right_basis, weight)

    new_weight = finish(near_id, base_near, received_near, 0, rows, None)
    for i, (start, size) in enumerate(PIECES):
        new_weight = finish(far_id, base_far, received_far[i], start, rows, new_weight)
    return (new_weight, nf, ns)


def solution(mesh):
    finer = Mesh(mesh.devices.reshape(4, 2, 4, 4), AXES)
    spec = P(EXPERT, None, TILE)
    return jax.shard_map(
        on_device, mesh=finer, in_specs=(spec,) * 6, out_specs=(spec,) * 3, check_vma=False
    )
```

time: 212 us -> 141 us (0.67)
  waiting for transfers between devices: 107 us -> 53.7 us
  blocking collectives: 48.1 us -> 0 us
  Pallas kernels: 0 us -> 42.7 us
  starting transfers between devices: 1.49 us -> 29.3 us
  matrix products: 20.8 us -> 0 us
  between operations: 14.9 us -> 0.8 us
  other arithmetic: 7.61 us -> 3.76 us
  local copies, waits for them, and re-layouts: 12.5 us -> 9.96 us
    all_gather x1 -> x0, waiting for transfers between devices: 61.7 us -> none  [on_device(): whole_left = lax.all_gather(left_basis, TILE, axis=2, tiled=True)]
    psum x4 -> x0, blocking collectives: 48.1 us -> none  [one_axis_at_a_time(): value = lax.psum(value, axis)]
    pallas_call x0 -> x10, Pallas kernels: none -> 42.7 us  [the longest x2 23.9 us: moments(): pl.pallas_call(functools.partial(moments_kernel, is_near, groups, count),...]
    ppermute x2 -> x13, starting transfers between devices: 1.46 us -> 22.4 us  [permute(): return lax.ppermute(value, axis, pairs)]
    dot_general x4 -> x0, matrix products: 20.8 us -> none  [the longest x1 7.82 us: on_device(): jnp.einsum('edk,ekj->edj', left_block, right_basis, preferred_element_typ...]
    all_to_all x0 -> x1, waiting for transfers between devices: none -> 18.5 us  [every_sum(): lax.all_to_all(jnp.broadcast_to(value, (devices, 1, 128)), AXES, 0, 0, ti...]
    ppermute x2 -> x13, waiting for transfers between devices: 44.3 us -> 35.2 us  [permute(): return lax.ppermute(value, axis, pairs)]
    all_to_all x0 -> x1, starting transfers between devices: none -> 6.91 us  [every_sum(): lax.all_to_all(jnp.broadcast_to(value, (devices, 1, 128)), AXES, 0, 0, ti...]
  transfers between devices with their start and end apart: 3 -> 14, of which waited for: 2 -> 7; matrix products, arithmetic and copies ran while one was open for 1% -> 8% of each run, Pallas kernels for 0% -> 30%
where the time goes in v2:
time: 141 us; the launch traced here: 140 us
  waiting for transfers between devices  53.7 us (38%)
  Pallas kernels  42.7 us (30%)
  starting transfers between devices  29.3 us (21%)
  local copies, waits for them, and re-layouts  9.96 us (7%)
  other arithmetic  3.76 us (3%)
    ppermute x13, waiting for transfers between devices, permute(): return lax.ppermute(value, axis, pairs)  35.2 us
    pallas_call x2, Pallas kernels, moments(): pl.pallas_call(functools.partial(moments_kernel, is_near, groups, count),...  23.9 us
    ppermute x13, starting transfers between devices, permute(): return lax.ppermute(value, axis, pairs)  22.4 us
    all_to_all x1, waiting for transfers between devices, every_sum(): lax.all_to_all(jnp.broadcast_to(value, (devices, 1, 128)), AXES, 0, 0, ti...  18.5 us
    pallas_call x2, Pallas kernels, rotate_right(): pl.pallas_call(rotate_right_kernel, grid=(block // rows,), out_shape=jax....  9.5 us
    all_to_all x1, starting transfers between devices, every_sum(): lax.all_to_all(jnp.broadcast_to(value, (devices, 1, 128)), AXES, 0, 0, ti...  6.91 us
    pallas_call x4, Pallas kernels, finish(): pl.pallas_call(finish_kernel, grid_spec=pltpu.PrefetchScalarGridSpec(num_...  6.34 us
    slice x3, local copies, waits for them, and re-layouts, on_device(): send[start:start + size]  3.16 us
  transfers between devices with their start and end apart: 14, of which 7 were waited for; matrix products, arithmetic and copies ran while one was open for 8% of the time, Pallas kernels for 30%

profile of v2, /device:TPU:0, one launch (start us, length us, event | category | flops | bytes accessed | tf_op | source)
XLA Modules:
  0.0 140.2 jit_solution(12996055152365487071)
XLA Ops:
  0.6 1.8 %collective-permute-start = (bf16[1,1024,128]{2,1,0:T(8,128)(2,1)}, bf16[1,1024,128]{2,1,0:T(8,128)(2,1)S(1)}, u32[]{:S(2)}, u32[]{:S(2)}) collective-permute-start(bf16[1,1024,128]{2,1,0:T(8,128)(2,1)} %param.10), channel_id=1, source_target_pairs={{0,1},{1,0},{2,3},{3,2},{4,5},{5,4},{6,7},{7,6},{8,9},{9,8},{10,11... | collective-permute-start | bytes 786440 | tf_op jit(solution)/shard_map/ppermute | solution.py:48
  2.4 1.7 %constant_dynamic-update-slice_fusion.1 = bf16[1,2048,128]{2,1,0:T(8,128)(2,1)} fusion(bf16[1,1024,128]{2,1,0:T(8,128)(2,1)} %param.10), kind=kLoop, calls=%fused_computation.3 | loop fusion | bytes 524288
  4.1 4.8 %collective-permute-done = bf16[1,1024,128]{2,1,0:T(8,128)(2,1)S(1)} collective-permute-done((bf16[1,1024,128]{2,1,0:T(8,128)(2,1)}, bf16[1,1024,128]{2,1,0:T(8,128)(2,1)S(1)}, u32[]{:S(2)}, u32[]{:S(2)}) %collective-permute-start) | collective-permute-done | bytes 262176 | tf_op jit(solution)/shard_map/ppermute | solution.py:48
  8.9 0.7 constant_dynamic-update-slice_fusion.refs_0_
  9.7 3.2 %collective-permute-start.2 = (bf16[1,2048,128]{2,1,0:T(8,128)(2,1)}, bf16[1,2048,128]{2,1,0:T(8,128)(2,1)}, u32[]{:S(2)}, u32[]{:S(2)}) collective-permute-start(bf16[1,2048,128]{2,1,0:T(8,128)(2,1)} %constant_dynamic-update-slice_fusion.refs_0_), channel_id=1, source_target_pairs={{0,3},{1,2},{2,1},{3,0},{4,7},{5,6},{6,5},{7,4},{8,11},{9,10},{10,... | collective-permute-start | bytes 1572872 | tf_op jit(solution)/shard_map/ppermute | solution.py:48
  12.8 1.9 %collective-permute-start.4 = (bf16[1,2048,128]{2,1,0:T(8,128)(2,1)}, bf16[1,2048,128]{2,1,0:T(8,128)(2,1)S(1)}, u32[]{:S(2)}, u32[]{:S(2)}) collective-permute-start(bf16[1,2048,128]{2,1,0:T(8,128)(2,1)} %constant_dynamic-update-slice_fusion.refs_0_), channel_id=1, source_target_pairs={{0,4},{4,0},{8,12},{12,8},{1,5},{5,1},{9,13},{13,9},{2,6},{6,2},{1... | collective-permute-start | bytes 1572872 | tf_op jit(solution)/shard_map/ppermute | solution.py:48
  14.8 9.5 %collective-permute-done.2.refs_1_ = bf16[1,2048,128]{2,1,0:T(8,128)(2,1)} collective-permute-done((bf16[1,2048,128]{2,1,0:T(8,128)(2,1)}, bf16[1,2048,128]{2,1,0:T(8,128)(2,1)}, u32[]{:S(2)}, u32[]{:S(2)}) %collective-permute-start.2) | collective-permute-done | bytes 524320 | tf_op jit(solution)/shard_map/ppermute | solution.py:48
  24.2 1.9 %collective-permute-start.5 = (bf16[1,2048,128]{2,1,0:T(8,128)(2,1)}, bf16[1,2048,128]{2,1,0:T(8,128)(2,1)}, u32[]{:S(2)}, u32[]{:S(2)}) collective-permute-start(bf16[1,2048,128]{2,1,0:T(8,128)(2,1)} %collective-permute-done.2.refs_1_), channel_id=1, source_target_pairs={{0,4},{4,0},{8,12},{12,8},{1,5},{5,1},{9,13},{13,9},{2,6},{6,2},{1... | collective-permute-start | bytes 1572872 | tf_op jit(solution)/shard_map/ppermute | solution.py:48
  26.1 1.7 %constant_dynamic-slice_fusion = (bf16[1,1024,512]{2,1,0:T(8,128)(2,1)S(1)}, bf16[1,1024,512]{2,1,0:T(8,128)(2,1)S(1)}) fusion(bf16[1,2048,512]{2,1,0:T(8,128)(2,1)} %param.7, s32[]{:T(128)S(6)} %select_n.13, s32[]{:T(128)S(6)} %select_n.12), kind=kLoop, calls=%fused_computation.4 | loop fusion | bytes 4194312 | tf_op jit(solution)/shard_map/dynamic_slice | solution.py:280
  27.8 0.0 copy-start.6
  27.8 0.0 copy-start.4
  27.8 0.4 collective-permute-start.8
  28.2 1.7 %collective-permute-start.7 = (bf16[1,1024,512]{2,1,0:T(8,128)(2,1)S(1)}, bf16[1,1024,512]{2,1,0:T(8,128)(2,1)}, u32[]{:S(2)}, u32[]{:S(2)}) collective-permute-start(bf16[1,1024,512]{2,1,0:T(8,128)(2,1)S(1)} %get-tuple-element.22.own_ref), channel_id=1, source_target_pairs={{0,1},{1,0},{2,3},{3,2},{4,5},{5,4},{6,7},{7,6},{8,9},{9,8},{10,11... | collective-permute-start | bytes 3145736 | tf_op jit(solution)/shard_map/ppermute | solution.py:48
  30.0 0.0 collective-permute-done.4.refs_2_
  30.0 7.2 %collective-permute-done.5.refs_3_ = bf16[1,2048,128]{2,1,0:T(8,128)(2,1)} collective-permute-done((bf16[1,2048,128]{2,1,0:T(8,128)(2,1)}, bf16[1,2048,128]{2,1,0:T(8,128)(2,1)}, u32[]{:S(2)}, u32[]{:S(2)}) %collective-permute-start.5) | collective-permute-done | bytes 524320 | tf_op jit(solution)/shard_map/ppermute | solution.py:48
  37.1 2.1 %pad_maximum_fusion = bf16[1,4096,128]{2,1,0:T(8,128)(2,1)} fusion(bf16[1,2048,128]{2,1,0:T(8,128)(2,1)} %collective-permute-done.5.refs_3_, bf16[1,2048,128]{2,1,0:T(8,128)(2,1)S(1)} %collective-permute-done.4.refs_2_), kind=kLoop, calls=%fused_computation.1 | loop fusion | flops 2097152 | bytes 2097152 | tf_op jit(solution)/shard_map/concatenate | solution.py:63
  39.2 3.8 %collective-permute-start.6 = (bf16[1,4096,128]{2,1,0:T(8,128)(2,1)}, bf16[1,4096,128]{2,1,0:T(8,128)(2,1)}, u32[]{:S(2)}, u32[]{:S(2)}) collective-permute-start(bf16[1,4096,128]{2,1,0:T(8,128)(2,1)} %pad_maximum_fusion), channel_id=1, source_target_pairs={{0,12},{4,8},{8,4},{12,0},{1,13},{5,9},{9,5},{13,1},{2,14},{6,10},... | collective-permute-start | bytes 3145736 | tf_op jit(solution)/shard_map/ppermute | solution.py:48
  43.0 1.7 %multiply_reduce_fusion = f32[]{:T(128)} fusion(bf16[1,2048,512]{2,1,0:T(8,128)(2,1)S(1)} %copy-done.4), kind=kLoop, calls=%fused_computation | loop fusion | flops 3145727 | bytes 2097156 | tf_op jit(solution)/shard_map/reduce_sum | solution.py:283
  44.7 1.2 broadcast_in_dim.2
  46.0 6.9 %all-to-all-start = ((f32[128,1,128]{2,1,0:T(1,128)}), f32[128,1,128]{2,1,0:T(1,128)S(1)}, u32[]{:S(2)}, u32[]{:S(2)}) async-start(f32[128,1,128]{2,1,0:T(1,128)} %broadcast_in_dim.2), calls=%async_computation | async-start | bytes 131072 | tf_op jit(solution)/shard_map/all_to_all | solution.py:53
  52.9 2.9 %collective-permute-start.1 = (bf16[1,2048,128]{2,1,0:T(8,128)(2,1)}, bf16[1,2048,128]{2,1,0:T(8,128)(2,1)S(1)}, u32[]{:S(2)}, u32[]{:S(2)}) collective-permute-start(bf16[1,2048,128]{2,1,0:T(8,128)(2,1)} %constant_dynamic-update-slice_fusion.refs_0_), channel_id=1, source_target_pairs={{0,12},{4,8},{8,4},{12,0},{1,13},{5,9},{9,5},{13,1},{2,14},{6,10},... | collective-permute-start | bytes 1572872 | tf_op jit(solution)/shard_map/ppermute | solution.py:48
  55.8 0.4 collective-permute-start.3
  56.2 0.0 collective-permute-done.8.other_ref
  56.2 4.7 %shard_map.86.refs_4_ = bf16[1024,512]{1,0:T(8,128)(2,1)} custom-call(bf16[1,1024,512]{2,1,0:T(8,128)(2,1)} %copy-done.6, bf16[1,1024,512]{2,1,0:T(8,128)(2,1)} %collective-permute-done.8.other_ref, bf16[1,1024,512]{2,1,0:T(8,128)(2,1)} %right_ref.7), custom_call_target="tpu_custom_call" | custom-call | flops 1073741824 | bytes 4194304 | tf_op jit(solution)/shard_map/pallas_call | solution.py:82
  60.9 18.5 %all-to-all-done.sums_ref = f32[128,1,128]{2,1,0:T(1,128)S(1)} async-done(((f32[128,1,128]{2,1,0:T(1,128)}), f32[128,1,128]{2,1,0:T(1,128)S(1)}, u32[]{:S(2)}, u32[]{:S(2)}) %all-to-all-start) | async-done | bytes 65568 | tf_op jit(solution)/shard_map/all_to_all | solution.py:53
  79.4 0.6 copy-done.8
  80.0 11.9 %shard_map.87 = (f32[1,2048,512]{2,1,0:T(8,128)}, f32[1,2048,512]{2,1,0:T(8,128)}, bf16[1024,512]{1,0:T(8,128)(2,1)}, bf16[1024,512]{1,0:T(8,128)(2,1)}) custom-call(s32[1]{0:T(128)} %bitcast.1.block_ref, f32[128,1,128]{2,1,0:T(1,128)} %copy-done.8, bf16[1,2048,128]{2,1,0:T(8,128)(2,1)} %constant_dynamic-update-slice_fusion.refs_0_, ...), custom_call_target="tpu_custom_call" | custom-call | flops 2684354560 | bytes 10485760 | tf_op jit(solution)/shard_map/pallas_call | solution.py:184
  91.9 0.1 collective-permute-start.12
  92.0 0.0 collective-permute-done.7.other_ref
  92.0 4.8 %shard_map.85.refs_3_ = bf16[1024,512]{1,0:T(8,128)(2,1)} custom-call(bf16[1,1024,512]{2,1,0:T(8,128)(2,1)} %copy-done.5, bf16[1,1024,512]{2,1,0:T(8,128)(2,1)} %collective-permute-done.7.other_ref, bf16[1,1024,512]{2,1,0:T(8,128)(2,1)} %right_ref.7), custom_call_target="tpu_custom_call" | custom-call | flops 1073741824 | bytes 4194304 | tf_op jit(solution)/shard_map/pallas_call | solution.py:82
  96.8 0.8 copy-done.9
  97.6 12.0 %shard_map.88 = (f32[1,2048,512]{2,1,0:T(8,128)}, f32[1,2048,512]{2,1,0:T(8,128)}, bf16[1024,512]{1,0:T(8,128)(2,1)}, bf16[1024,512]{1,0:T(8,128)(2,1)}) custom-call(s32[1]{0:T(128)} %bitcast.block_ref, f32[128,1,128]{2,1,0:T(1,128)} %copy-done.8, bf16[1,2048,128]{2,1,0:T(8,128)(2,1)} %copy-done.9, ...), custom_call_target="tpu_custom_call", output_to_operand_aliasing={{0}: (9, {}), {1}: (10, {})} | custom-call | flops 2684354560 | bytes 10485760 | tf_op jit(solution)/shard_map/pallas_call | solution.py:184
  109.6 0.0 copy-start
  109.7 1.2 slice.11
  110.9 2.1 %collective-permute-start.11 = (bf16[512,512]{1,0:T(8,128)(2,1)S(1)}, bf16[512,512]{1,0:T(8,128)(2,1)S(1)}, u32[]{:S(2)}, u32[]{:S(2)}) collective-permute-start(bf16[512,512]{1,0:T(8,128)(2,1)S(1)} %slice.11), channel_id=1, source_target_pairs={{0,1},{1,0},{2,3},{3,2},{4,5},{5,4},{6,7},{7,6},{8,9},{9,8},{10,11... | collective-permute-start | bytes 1572872 | tf_op jit(solution)/shard_map/ppermute | solution.py:48
  113.0 1.0 slice.10
  114.0 0.1 collective-permute-start.10
  114.1 0.9 slice.9
  115.0 2.1 %collective-permute-start.9 = (bf16[128,512]{1,0:T(8,128)(2,1)S(1)}, bf16[128,512]{1,0:T(8,128)(2,1)S(1)}, u32[]{:S(2)}, u32[]{:S(2)}) collective-permute-start(bf16[128,512]{1,0:T(8,128)(2,1)S(1)} %slice.9), channel_id=1, source_target_pairs={{0,1},{1,0},{2,3},{3,2},{4,5},{5,4},{6,7},{7,6},{8,9},{9,8},{10,11... | collective-permute-start | bytes 393224 | tf_op jit(solution)/shard_map/ppermute | solution.py:48
  117.1 1.5 %shard_map.90.base_ref = f32[1024,512]{1,0:T(8,128)S(1)} custom-call(s32[1]{0:T(128)} %bitcast.1.block_ref, bf16[1024,512]{1,0:T(8,128)(2,1)S(1)} %copy-done.2, bf16[1,1024,512]{2,1,0:T(8,128)(2,1)S(1)} %copy-done, bf16[1,2048,512]{2,1,0:T(8,128)(2,1)S(1)} %copy-done.1), custom_call_target="tpu_custom_call" | custom-call | flops 536870912 | bytes 5242880 | tf_op jit(solution)/shard_map/pallas_call | solution.py:219
  118.6 2.9 %shard_map.91.refs_0_ = bf16[1,2048,512]{2,1,0:T(8,128)(2,1)} custom-call(s32[1]{0:T(128)} %bitcast.1.block_ref, f32[1024,512]{1,0:T(8,128)S(1)} %shard_map.90.base_ref, bf16[1024,512]{1,0:T(8,128)(2,1)S(1)} %collective-permute-done.12.received_ref), custom_call_target="tpu_custom_call" | custom-call | flops 1048576 | bytes 4194304 | tf_op jit(solution)/shard_map/pallas_call | solution.py:255
  121.5 1.5 %shard_map.89.base_ref = f32[1024,512]{1,0:T(8,128)S(1)} custom-call(s32[1]{0:T(128)} %bitcast.block_ref, bf16[1024,512]{1,0:T(8,128)(2,1)S(1)} %copy-done.3, bf16[1,1024,512]{2,1,0:T(8,128)(2,1)S(1)} %copy-done, bf16[1,2048,512]{2,1,0:T(8,128)(2,1)S(1)} %copy-done.1), custom_call_target="tpu_custom_call" | custom-call | flops 536870912 | bytes 5242880 | tf_op jit(solution)/shard_map/pallas_call | solution.py:219
  122.9 6.5 %collective-permute-done.11.received_ref = bf16[512,512]{1,0:T(8,128)(2,1)S(1)} collective-permute-done((bf16[512,512]{1,0:T(8,128)(2,1)S(1)}, bf16[512,512]{1,0:T(8,128)(2,1)S(1)}, u32[]{:S(2)}, u32[]{:S(2)}) %collective-permute-start.11) | collective-permute-done | bytes 524320 | tf_op jit(solution)/shard_map/ppermute | solution.py:48
  129.5 1.4 %shard_map.92.refs_0_ = bf16[1,2048,512]{2,1,0:T(8,128)(2,1)} custom-call(s32[1]{0:T(128)} %bitcast.block_ref, f32[1024,512]{1,0:T(8,128)S(1)} %shard_map.89.base_ref, bf16[512,512]{1,0:T(8,128)(2,1)S(1)} %collective-permute-done.11.received_ref, bf16[1,2048,512]{2,1,0:T(8,128)(2,1)} %shard_map.91.refs_0_), custom_call_target="tpu_custom_call", output_to_operand_aliasing={{}: (3, {})} | custom-call | flops 524288 | bytes 2097152 | tf_op jit(solution)/shard_map/pallas_call | solution.py:255
  130.9 7.0 %collective-permute-done.10.received_ref = bf16[384,512]{1,0:T(8,128)(2,1)S(1)} collective-permute-done((bf16[384,512]{1,0:T(8,128)(2,1)S(1)}, bf16[384,512]{1,0:T(8,128)(2,1)S(1)}, u32[]{:S(2)}, u32[]{:S(2)}) %collective-permute-start.10) | collective-permute-done | bytes 393248 | tf_op jit(solution)/shard_map/ppermute | solution.py:48
  137.9 1.4 shard_map.93.refs_0_
  139.3 0.2 collective-permute-done.9.received_ref
  139.5 0.7 shard_map.94
  (19 shorter events, 0.0 us)
Async XLA Ops:
  0.6 8.3 %collective-permute-start = (bf16[1,1024,128]{2,1,0:T(8,128)(2,1)}, bf16[1,1024,128]{2,1,0:T(8,128)(2,1)S(1)}, u32[]{:S(2)}, u32[]{:S(2)}) collective-permute-start(bf16[1,1024,128]{2,1,0:T(8,128)(2,1)} %param.10), channel_id=1, source_target_pairs={{0,1},{1,0},{2,3},{3,2},{4,5},{5,4},{6,7},{7,6},{8,9},{9,8},{10,11... | collective-permute-start | bytes 786440 | tf_op jit(solution)/shard_map/ppermute | solution.py:48
  9.7 14.6 %collective-permute-start.2 = (bf16[1,2048,128]{2,1,0:T(8,128)(2,1)}, bf16[1,2048,128]{2,1,0:T(8,128)(2,1)}, u32[]{:S(2)}, u32[]{:S(2)}) collective-permute-start(bf16[1,2048,128]{2,1,0:T(8,128)(2,1)} %constant_dynamic-update-slice_fusion.refs_0_), channel_id=1, source_target_pairs={{0,3},{1,2},{2,1},{3,0},{4,7},{5,6},{6,5},{7,4},{8,11},{9,10},{10,... | collective-permute-start | bytes 1572872 | tf_op jit(solution)/shard_map/ppermute | solution.py:48
  12.8 17.1 %collective-permute-start.4 = (bf16[1,2048,128]{2,1,0:T(8,128)(2,1)}, bf16[1,2048,128]{2,1,0:T(8,128)(2,1)S(1)}, u32[]{:S(2)}, u32[]{:S(2)}) collective-permute-start(bf16[1,2048,128]{2,1,0:T(8,128)(2,1)} %constant_dynamic-update-slice_fusion.refs_0_), channel_id=1, source_target_pairs={{0,4},{4,0},{8,12},{12,8},{1,5},{5,1},{9,13},{13,9},{2,6},{6,2},{1... | collective-permute-start | bytes 1572872 | tf_op jit(solution)/shard_map/ppermute | solution.py:48
  24.2 12.9 %collective-permute-start.5 = (bf16[1,2048,128]{2,1,0:T(8,128)(2,1)}, bf16[1,2048,128]{2,1,0:T(8,128)(2,1)}, u32[]{:S(2)}, u32[]{:S(2)}) collective-permute-start(bf16[1,2048,128]{2,1,0:T(8,128)(2,1)} %collective-permute-done.2.refs_1_), channel_id=1, source_target_pairs={{0,4},{4,0},{8,12},{12,8},{1,5},{5,1},{9,13},{13,9},{2,6},{6,2},{1... | collective-permute-start | bytes 1572872 | tf_op jit(solution)/shard_map/ppermute | solution.py:48
  27.8 16.9 %copy-start.5 = (bf16[1,1024,512]{2,1,0:T(8,128)(2,1)}, bf16[1,1024,512]{2,1,0:T(8,128)(2,1)S(1)}, u32[]{:S(2)}) copy-start(bf16[1,1024,512]{2,1,0:T(8,128)(2,1)S(1)} %get-tuple-element.22.own_ref) | copy-start | bytes 3145732
  27.8 16.9 %copy-start.6 = (bf16[1,1024,512]{2,1,0:T(8,128)(2,1)}, bf16[1,1024,512]{2,1,0:T(8,128)(2,1)S(1)}, u32[]{:S(2)}) copy-start(bf16[1,1024,512]{2,1,0:T(8,128)(2,1)S(1)} %get-tuple-element.21.own_ref) | copy-start | bytes 3145732
  27.8 15.2 %copy-start.4 = (bf16[1,2048,512]{2,1,0:T(8,128)(2,1)S(1)}, bf16[1,2048,512]{2,1,0:T(8,128)(2,1)}, u32[]{:S(2)}) copy-start(bf16[1,2048,512]{2,1,0:T(8,128)(2,1)} %param.7) | copy-start | bytes 6291460
  27.8 28.4 %collective-permute-start.8 = (bf16[1,1024,512]{2,1,0:T(8,128)(2,1)S(1)}, bf16[1,1024,512]{2,1,0:T(8,128)(2,1)}, u32[]{:S(2)}, u32[]{:S(2)}) collective-permute-start(bf16[1,1024,512]{2,1,0:T(8,128)(2,1)S(1)} %get-tuple-element.21.own_ref), channel_id=1, source_target_pairs={{0,1},{1,0},{2,3},{3,2},{4,5},{5,4},{6,7},{7,6},{8,9},{9,8},{10,11... | collective-permute-start | bytes 3145736 | tf_op jit(solution)/shard_map/ppermute | solution.py:48
  28.2 63.8 %collective-permute-start.7 = (bf16[1,1024,512]{2,1,0:T(8,128)(2,1)S(1)}, bf16[1,1024,512]{2,1,0:T(8,128)(2,1)}, u32[]{:S(2)}, u32[]{:S(2)}) collective-permute-start(bf16[1,1024,512]{2,1,0:T(8,128)(2,1)S(1)} %get-tuple-element.22.own_ref), channel_id=1, source_target_pairs={{0,1},{1,0},{2,3},{3,2},{4,5},{5,4},{6,7},{7,6},{8,9},{9,8},{10,11... | collective-permute-start | bytes 3145736 | tf_op jit(solution)/shard_map/ppermute | solution.py:48
  30.0 14.8 %copy-start.7 = (bf16[1,2048,128]{2,1,0:T(8,128)(2,1)}, bf16[1,2048,128]{2,1,0:T(8,128)(2,1)S(1)}, u32[]{:S(2)}) copy-start(bf16[1,2048,128]{2,1,0:T(8,128)(2,1)S(1)} %collective-permute-done.4.refs_2_) | copy-start | bytes 1572868
  39.2 57.6 %collective-permute-start.6 = (bf16[1,4096,128]{2,1,0:T(8,128)(2,1)}, bf16[1,4096,128]{2,1,0:T(8,128)(2,1)}, u32[]{:S(2)}, u32[]{:S(2)}) collective-permute-start(bf16[1,4096,128]{2,1,0:T(8,128)(2,1)} %pad_maximum_fusion), channel_id=1, source_target_pairs={{0,12},{4,8},{8,4},{12,0},{1,13},{5,9},{9,5},{13,1},{2,14},{6,10},... | collective-permute-start | bytes 3145736 | tf_op jit(solution)/shard_map/ppermute | solution.py:48
  46.0 33.5 %all-to-all-start = ((f32[128,1,128]{2,1,0:T(1,128)}), f32[128,1,128]{2,1,0:T(1,128)S(1)}, u32[]{:S(2)}, u32[]{:S(2)}) async-start(f32[128,1,128]{2,1,0:T(1,128)} %broadcast_in_dim.2), calls=%async_computation | async-start | bytes 131072 | tf_op jit(solution)/shard_map/all_to_all | solution.py:53
  52.9 43.9 %collective-permute-start.1 = (bf16[1,2048,128]{2,1,0:T(8,128)(2,1)}, bf16[1,2048,128]{2,1,0:T(8,128)(2,1)S(1)}, u32[]{:S(2)}, u32[]{:S(2)}) collective-permute-start(bf16[1,2048,128]{2,1,0:T(8,128)(2,1)} %constant_dynamic-update-slice_fusion.refs_0_), channel_id=1, source_target_pairs={{0,12},{4,8},{8,4},{12,0},{1,13},{5,9},{9,5},{13,1},{2,14},{6,10},... | collective-permute-start | bytes 1572872 | tf_op jit(solution)/shard_map/ppermute | solution.py:48
  55.8 41.0 %collective-permute-start.3 = (bf16[1,2048,128]{2,1,0:T(8,128)(2,1)}, bf16[1,2048,128]{2,1,0:T(8,128)(2,1)}, u32[]{:S(2)}, u32[]{:S(2)}) collective-permute-start(bf16[1,2048,128]{2,1,0:T(8,128)(2,1)} %collective-permute-done.2.refs_1_), channel_id=1, source_target_pairs={{0,12},{4,8},{8,4},{12,0},{1,13},{5,9},{9,5},{13,1},{2,14},{6,10},... | collective-permute-start | bytes 1572872 | tf_op jit(solution)/shard_map/ppermute | solution.py:48
  79.4 0.6 copy-start.8
  91.9 26.7 %collective-permute-start.12 = (bf16[1024,512]{1,0:T(8,128)(2,1)}, bf16[1024,512]{1,0:T(8,128)(2,1)S(1)}, u32[]{:S(2)}, u32[]{:S(2)}) collective-permute-start(bf16[1024,512]{1,0:T(8,128)(2,1)} %get-tuple-element.18), channel_id=1, source_target_pairs={{0,1},{1,0},{2,3},{3,2},{4,5},{5,4},{6,7},{7,6},{8,9},{9,8},{10,11... | collective-permute-start | bytes 3145736 | tf_op jit(solution)/shard_map/ppermute | solution.py:48
  96.8 0.8 copy-start.9
  97.6 19.5 %copy-start.1 = (bf16[1,2048,512]{2,1,0:T(8,128)(2,1)S(1)}, bf16[1,2048,512]{2,1,0:T(8,128)(2,1)}, u32[]{:S(2)}) copy-start(bf16[1,2048,512]{2,1,0:T(8,128)(2,1)} %weight_ref.3) | copy-start | bytes 6291460
  109.6 7.5 %copy-start = (bf16[1,1024,512]{2,1,0:T(8,128)(2,1)S(1)}, bf16[1,1024,512]{2,1,0:T(8,128)(2,1)}, u32[]{:S(2)}) copy-start(bf16[1,1024,512]{2,1,0:T(8,128)(2,1)} %right_ref.7) | copy-start | bytes 3145732
  109.7 7.4 %copy-start.2 = (bf16[1024,512]{1,0:T(8,128)(2,1)S(1)}, bf16[1024,512]{1,0:T(8,128)(2,1)}, u32[]{:S(2)}) copy-start(bf16[1024,512]{1,0:T(8,128)(2,1)} %get-tuple-element.17.turned_ref) | copy-start | bytes 3145732
  110.9 18.6 %collective-permute-start.11 = (bf16[512,512]{1,0:T(8,128)(2,1)S(1)}, bf16[512,512]{1,0:T(8,128)(2,1)S(1)}, u32[]{:S(2)}, u32[]{:S(2)}) collective-permute-start(bf16[512,512]{1,0:T(8,128)(2,1)S(1)} %slice.11), channel_id=1, source_target_pairs={{0,1},{1,0},{2,3},{3,2},{4,5},{5,4},{6,7},{7,6},{8,9},{9,8},{10,11... | collective-permute-start | bytes 1572872 | tf_op jit(solution)/shard_map/ppermute | solution.py:48
  114.0 23.9 %collective-permute-start.10 = (bf16[384,512]{1,0:T(8,128)(2,1)S(1)}, bf16[384,512]{1,0:T(8,128)(2,1)S(1)}, u32[]{:S(2)}, u32[]{:S(2)}) collective-permute-start(bf16[384,512]{1,0:T(8,128)(2,1)S(1)} %slice.10), channel_id=1, source_target_pairs={{0,1},{1,0},{2,3},{3,2},{4,5},{5,4},{6,7},{7,6},{8,9},{9,8},{10,11... | collective-permute-start | bytes 1179656 | tf_op jit(solution)/shard_map/ppermute | solution.py:48
  115.0 24.5 %collective-permute-start.9 = (bf16[128,512]{1,0:T(8,128)(2,1)S(1)}, bf16[128,512]{1,0:T(8,128)(2,1)S(1)}, u32[]{:S(2)}, u32[]{:S(2)}) collective-permute-start(bf16[128,512]{1,0:T(8,128)(2,1)S(1)} %slice.9), channel_id=1, source_target_pairs={{0,1},{1,0},{2,3},{3,2},{4,5},{5,4},{6,7},{7,6},{8,9},{9,8},{10,11... | collective-permute-start | bytes 393224 | tf_op jit(solution)/shard_map/ppermute | solution.py:48
  118.6 2.9 %copy-start.3 = (bf16[1024,512]{1,0:T(8,128)(2,1)S(1)}, bf16[1024,512]{1,0:T(8,128)(2,1)}, u32[]{:S(2)}) copy-start(bf16[1024,512]{1,0:T(8,128)(2,1)} %get-tuple-element.15.turned_ref) | copy-start | bytes 3145732

commit v3 on v2

v3 whole, which is shorter than its diff:
```python
import functools

import jax
import jax.numpy as jnp
from jax import lax
from jax.experimental import pallas as pl
from jax.experimental.pallas import tpu as pltpu
from jax.sharding import Mesh
from jax.sharding import PartitionSpec as P


AXES = ("x", "core", "z", "y")
EXPERT = ("x", "core")
TILE = ("z", "y")

beta_one = 0.9
beta_two = 0.95
epsilon = 1e-08
learn_rate = 0.25
decay_rate = 0.1


f32 = jnp.float32
bf16 = jnp.bfloat16
ANY = pl.BlockSpec(memory_space=pl.ANY)
HBM = pl.BlockSpec(memory_space=pltpu.HBM)
MIB = 1024 * 1024
PIECES = ((0, 512), (512, 384), (896, 128))


def cost(flops, bytes_accessed):
    return pl.CostEstimate(flops=flops, bytes_accessed=bytes_accessed, transcendentals=0)


def limit(mib):
    return pltpu.CompilerParams(vmem_limit_bytes=mib * MIB)


def near(i):
    return i ^ 1


def far(i):
    return 3 - i


def permute(value, axis, target):
    pairs = [(source, target(source)) for source in range(lax.axis_size(axis))]
    return lax.ppermute(value, axis, pairs)


def every_sum(value):
    devices = lax.axis_size(AXES)
    return lax.all_to_all(jnp.broadcast_to(value, (devices, 1, 128)), AXES, 0, 0, tiled=True)


def gather_left(shard):
    row = jnp.concatenate((shard, permute(shard, "y", near)), axis=1)
    row_far = permute(row, "y", far)
    near0 = permute(row, "z", near)
    far0 = permute(row, "z", far)
    near1 = permute(row_far, "z", near)
    far1 = permute(row_far, "z", far)
    near2 = permute(far0, "z", near)
    far3 = permute(near1, "z", far)
    return (row, row_far, near0, near1), (far0, far1, near2, far3)


def halves(right, y, width):
    position = lax.rem(y, 2)
    own = right[pl.ds(pl.multiple_of(position * width, width), width), :]
    other = right[pl.ds(pl.multiple_of((1 - position) * width, width), width), :]
    return own, other


def start_all(copies):
    for copy in copies:
        copy.start()


def wait_all(copies):
    for copy in copies:
        copy.wait()


def rotate_right_kernel(own_ref, other_ref, right_ref, out_ref, own, other, right, out, sems):
    block, width = out.shape
    rows = 256
    steps = block // rows
    chunks = [pl.ds(s * rows, rows) for s in range(steps)]
    load = pltpu.make_async_copy(right_ref.at[0], right, sems.at[0])
    loads = [
        (
            pltpu.make_async_copy(own_ref.at[0, c, :], own.at[c, :], sems.at[1 + 3 * s]),
            pltpu.make_async_copy(other_ref.at[0, c, :], other.at[c, :], sems.at[2 + 3 * s]),
        )
        for s, c in enumerate(chunks)
    ]
    stores = [
        pltpu.make_async_copy(out.at[c, :], out_ref.at[c, :], sems.at[3 + 3 * s])
        for s, c in enumerate(chunks)
    ]
    load.start()
    for pair in loads:
        start_all(pair)
    load.wait()
    right_own, right_other = halves(right, lax.axis_index("y"), width)
    for s, c in enumerate(chunks):
        wait_all(loads[s])
        out[c, :] = (
            jnp.dot(own[c, :], right_own, preferred_element_type=f32)
            + jnp.dot(other[c, :], right_other, preferred_element_type=f32)
        ).astype(bf16)
        stores[s].start()
    wait_all(stores)


def rotate_right(own, other, right):
    _, block, width = own.shape
    half = pltpu.VMEM((block, width), bf16)
    return pl.pallas_call(
        rotate_right_kernel,
        out_shape=jax.ShapeDtypeStruct((block, width), bf16),
        in_specs=[HBM] * 3,
        out_specs=HBM,
        scratch_shapes=[half, half, half, half, pltpu.SemaphoreType.DMA((13,))],
        cost_estimate=cost(4 * block * width * width, 8 * block * width),
        compiler_params=limit(63),
    )(own, other, right)


def moments_kernel(is_near, count, pieces, block_ref, sums_ref, *refs):
    shards = refs[:4]
    term_ref, right_ref, first_ref, second_ref = refs[4:8]
    new_first_ref, new_second_ref, turned_ref, *send_refs = refs[-12 - len(pieces) : -9]
    left, term, right, first, second, update, turned, send, sems = refs[-9:]
    block, width = term.shape
    rows = 256
    steps = block // rows
    z = lax.axis_index("z")
    y = lax.axis_index("y")
    base_row = block_ref[0] * block
    chunks = [pl.ds(s * rows, rows) for s in range(steps)]
    places = [pl.ds(pl.multiple_of(base_row + s * rows, rows), rows) for s in range(steps)]
    used = [0]

    def copy(source, target):
        used[0] += 1
        return pltpu.make_async_copy(source, target, sems.at[used[0] - 1])

    partner = y + 1 - 2 * lax.rem(y, 2)
    columns = (y, partner, 3 - y, 3 - partner)
    parity = lax.rem(z if is_near else z + 1, 2)
    entry = []
    for k in range(8):
        group, part = k // 2, k % 2
        row = parity if group < 2 else 1 - parity
        slot = row * 4 + columns[k % 4]
        entry.append(
            copy(
                shards[group].at[0, pl.ds(part * block, block), :],
                left.at[:, pl.ds(pl.multiple_of(slot * 128, 128), 128)],
            )
        )
    entry.append(copy(term_ref, term))
    loads = [
        (copy(first_ref.at[0, p, :], first.at[c, :]), copy(second_ref.at[0, p, :], second.at[c, :]))
        for c, p in zip(chunks, places)
    ]
    load_right = copy(right_ref.at[0], right)
    stores = [
        (
            copy(first.at[c, :], new_first_ref.at[0, p, :]),
            copy(second.at[c, :], new_second_ref.at[0, p, :]),
        )
        for c, p in zip(chunks, places)
    ]
    start_all(entry)
    for pair in loads:
        start_all(pair)
    load_right.start()

    total = jnp.sum(sums_ref[...], axis=0)
    clip = 1.0 / jnp.maximum(1.0, jnp.sqrt(total / count))
    clip = jnp.concatenate([clip] * (width // 128), axis=1)
    wait_all(entry)

    def rotate(s):
        return lax.dot_general(
            left[:, chunks[s]], term[...], (((0,), (0,)), ((), ())), preferred_element_type=f32
        )

    rotated = rotate(0)
    for s, c in enumerate(chunks):
        wait_all(loads[s])
        following = rotate(s + 1) if s + 1 < steps else None
        clipped = clip * rotated
        new_first = beta_one * first[c, :] + (1.0 - beta_one) * clipped
        new_second = beta_two * second[c, :] + (1.0 - beta_two) * clipped * clipped
        first[c, :] = new_first
        second[c, :] = new_second
        update[c, :] = (new_first / (jnp.sqrt(new_second) + epsilon)).astype(bf16)
        if s > 0:
            start_all(stores[s - 1])
        rotated = following

    load_right.wait()
    _, right_other = halves(right, y, width)
    send_stores = []
    for s, c in enumerate(chunks):
        piece = jnp.dot(left[c, :], update[...], preferred_element_type=f32).astype(bf16)
        turned[c, :] = piece
        send[c, :] = lax.dot_general(
            piece, right_other, (((1,), (1,)), ((), ())), preferred_element_type=f32
        ).astype(bf16)
        if s == 0:
            start_all(stores[steps - 1])
        for (start, size), send_ref in zip(pieces, send_refs):
            low, high = max(start, s * rows), min(start + size, (s + 1) * rows)
            if low < high:
                one = copy(
                    send.at[pl.ds(low, high - low), :],
                    send_ref.at[pl.ds(low - start, high - low), :],
                )
                one.start()
                send_stores.append(one)
    store_turned = copy(turned, turned_ref)
    store_turned.start()
    for pair in stores:
        wait_all(pair)
    wait_all(send_stores)
    store_turned.wait()


def moments(is_near, which, sums, shards, term, right, first, second, previous, pieces):
    _, all_rows, width = first.shape
    block = right.shape[1]
    count = sums.shape[0] * all_rows * width
    whole = jax.ShapeDtypeStruct((1, all_rows, width), f32)
    part = jax.ShapeDtypeStruct((block, width), bf16)
    sends = [jax.ShapeDtypeStruct((size, width), bf16) for _, size in pieces]
    operands = [which, sums, *shards, term, right, first, second]
    aliases = {}
    if previous is not None:
        aliases = {len(operands): 0, len(operands) + 1: 1}
        operands += list(previous)
    in_specs = [pl.BlockSpec(memory_space=pltpu.SMEM), pl.BlockSpec(memory_space=pltpu.VMEM)]
    in_specs += [HBM] * (len(operands) - 2)
    half = pltpu.VMEM((block, width), bf16)
    moment = pltpu.VMEM((block, width), f32)
    return pl.pallas_call(
        functools.partial(moments_kernel, is_near, count, pieces),
        out_shape=[whole, whole, part, *sends],
        in_specs=in_specs,
        out_specs=[HBM] * (3 + len(sends)),
        scratch_shapes=[
            pltpu.VMEM((block, block), bf16),
            half,
            half,
            moment,
            moment,
            half,
            half,
            half,
            pltpu.SemaphoreType.DMA((40,)),
        ],
        input_output_aliases=aliases,
        cost_estimate=cost(5 * block * block * width, 20 * block * width),
        compiler_params=limit(63),
    )(*operands)


def base_kernel(block_ref, turned_ref, right_ref, weight_ref, out_ref):
    width = right_ref.shape[2]
    position = lax.rem(lax.axis_index("y"), 2)
    right_own = right_ref[0, pl.ds(pl.multiple_of(position * width, width), width), :]
    back = lax.dot_general(
        turned_ref[...], right_own, (((1,), (1,)), ((), ())), preferred_element_type=f32
    )
    weight = weight_ref[0].astype(f32)
    out_ref[...] = weight - learn_rate * (back + decay_rate * weight)


def base(which, turned, right, weight):
    block, width = turned.shape
    rows = 256
    steps = block // rows
    return pl.pallas_call(
        base_kernel,
        grid_spec=pltpu.PrefetchScalarGridSpec(
            num_scalar_prefetch=1,
            grid=(steps,),
            in_specs=[
                pl.BlockSpec((rows, width), lambda s, b: (s, 0)),
                pl.BlockSpec((1, block, width), lambda s, b: (0, 0, 0)),
                pl.BlockSpec((1, rows, width), lambda s, b: (0, b[0] * steps + s, 0)),
            ],
            out_specs=pl.BlockSpec((rows, width), lambda s, b: (s, 0)),
        ),
        out_shape=jax.ShapeDtypeStruct((block, width), f32),
        cost_estimate=cost(2 * block * width * width, 10 * block * width),
        compiler_params=limit(12),
    )(which, turned, right, weight)


def finish_kernel(block_ref, base_ref, received_ref, *refs):
    refs[-1][0] = (base_ref[...] - learn_rate * received_ref[...].astype(f32)).astype(bf16)


def finish(which, base_term, received, start, total_rows, previous):
    block = base_term.shape[0]
    count, width = received.shape
    rows = 128
    in_specs = [
        pl.BlockSpec((rows, width), lambda s, b: (start // rows + s, 0)),
        pl.BlockSpec((rows, width), lambda s, b: (s, 0)),
    ]
    operands = [which, base_term, received]
    aliases = {}
    if previous is not None:
        in_specs.append(ANY)
        aliases = {len(operands): 0}
        operands.append(previous)
    return pl.pallas_call(
        finish_kernel,
        grid_spec=pltpu.PrefetchScalarGridSpec(
            num_scalar_prefetch=1,
            grid=(count // rows,),
            in_specs=in_specs,
            out_specs=pl.BlockSpec(
                (1, rows, width), lambda s, b: (0, (b[0] * block + start) // rows + s, 0)
            ),
        ),
        out_shape=jax.ShapeDtypeStruct((1, total_rows, width), bf16),
        input_output_aliases=aliases,
        cost_estimate=cost(2 * count * width, 8 * count * width),
        compiler_params=limit(8),
    )(*operands)


def on_device(weight, grad, first_moment, second_moment, left_basis, right_basis):
    _, rows, _ = grad.shape
    block = right_basis.shape[1]
    near_block = lax.axis_index("z") // 2
    far_block = 1 - near_block
    near_id = near_block.reshape(1)
    far_id = far_block.reshape(1)

    own_near = lax.dynamic_slice_in_dim(grad, near_block * block, block, axis=1)
    other_near = permute(own_near, "y", near)

    local_sum = jnp.sum(jnp.square(grad.astype(f32))).reshape(1, 1, 1)
    sums = every_sum(local_sum)
    left_near, left_far = gather_left(left_basis)

    own_far = lax.dynamic_slice_in_dim(grad, far_block * block, block, axis=1)
    other_far = permute(own_far, "y", near)

    term = rotate_right(own_near, other_near, right_basis)
    nf, ns, turned, send = moments(
        True, near_id, sums, left_near, term, right_basis, first_moment, second_moment, None,
        ((0, block),),
    )
    received_near = permute(send, "y", near)
    base_near = base(near_id, turned, right_basis, weight)

    term = rotate_right(own_far, other_far, right_basis)
    nf, ns, turned, *sends = moments(
        False, far_id, sums, left_far, term, right_basis, first_moment, second_moment, (nf, ns),
        PIECES,
    )
    received_far = [permute(send, "y", near) for send in sends]
    base_far = base(far_id, turned, right_basis, weight)

    new_weight = finish(near_id, base_near, received_near, 0, rows, None)
    for i, (start, size) in enumerate(PIECES):
        new_weight = finish(far_id, base_far, received_far[i], start, rows, new_weight)
    return (new_weight, nf, ns)


def solution(mesh):
    finer = Mesh(mesh.devices.reshape(4, 2, 4, 4), AXES)
    spec = P(EXPERT, None, TILE)
    return jax.shard_map(
        on_device, mesh=finer, in_specs=(spec,) * 6, out_specs=(spec,) * 3, check_vma=False
    )
```

time: 141 us -> 120 us (0.85)
  waiting for transfers between devices: 53.7 us -> 37.5 us
  Pallas kernels: 42.7 us -> 39.3 us
  other arithmetic: 3.76 us -> 1.68 us
    ppermute x13 -> x14, waiting for transfers between devices: 35.2 us -> 24.9 us  [permute(): return lax.ppermute(value, axis, pairs)]
    all_to_all x1, waiting for transfers between devices: 18.5 us -> 12.6 us  [every_sum(): lax.all_to_all(jnp.broadcast_to(value, (devices, 1, 128)), AXES, 0, 0, ti...]
    pallas_call x4, Pallas kernels: 33.4 us -> 27.6 us  [the longest x2 19.8 us: moments(): pl.pallas_call(functools.partial(moments_kernel, is_near, count, pieces),...]
    all_to_all x1, starting transfers between devices: 6.91 us -> 10.8 us  [every_sum(): lax.all_to_all(jnp.broadcast_to(value, (devices, 1, 128)), AXES, 0, 0, ti...]
    slice x3 -> x0, local copies, waits for them, and re-layouts: 3.16 us -> none  [on_device(): send[start:start + size]]
    ppermute x13 -> x14, starting transfers between devices: 22.4 us -> 19.8 us  [permute(): return lax.ppermute(value, axis, pairs)]
    unnamed x21, local copies, waits for them, and re-layouts: 3.15 us -> 5.66 us
    pallas_call x4, Pallas kernels: 6.34 us -> 8.75 us  [finish(): pl.pallas_call(finish_kernel, grid_spec=pltpu.PrefetchScalarGridSpec(num_...]
  transfers between devices with their start and end apart: 14 -> 15, of which waited for: 7 -> 7; matrix products, arithmetic and copies ran while one was open for 8% -> 5% of each run, Pallas kernels for 30% -> 32%
where the time goes in v3:
time: 120 us
  Pallas kernels  39.3 us (33%)
  waiting for transfers between devices  37.5 us (31%)
  starting transfers between devices  30.6 us (26%)
  local copies, waits for them, and re-layouts  9.8 us (8%)
  other arithmetic  1.68 us (1%)
    ppermute x14, waiting for transfers between devices, permute(): return lax.ppermute(value, axis, pairs)  24.9 us
    ppermute x14, starting transfers between devices, permute(): return lax.ppermute(value, axis, pairs)  19.8 us
    pallas_call x2, Pallas kernels, moments(): pl.pallas_call(functools.partial(moments_kernel, is_near, count, pieces),...  19.8 us
    all_to_all x1, waiting for transfers between devices, every_sum(): lax.all_to_all(jnp.broadcast_to(value, (devices, 1, 128)), AXES, 0, 0, ti...  12.6 us
    all_to_all x1, starting transfers between devices, every_sum(): lax.all_to_all(jnp.broadcast_to(value, (devices, 1, 128)), AXES, 0, 0, ti...  10.8 us
    pallas_call x4, Pallas kernels, finish(): pl.pallas_call(finish_kernel, grid_spec=pltpu.PrefetchScalarGridSpec(num_...  8.75 us
    pallas_call x2, Pallas kernels, rotate_right(): pl.pallas_call(rotate_right_kernel, out_shape=jax.ShapeDtypeStruct((block...  7.84 us
    unnamed x21, local copies, waits for them, and re-layouts  5.66 us
  transfers between devices with their start and end apart: 15, of which 7 were waited for; matrix products, arithmetic and copies ran while one was open for 5% of the time, Pallas kernels for 32%

profile of v3, /device:TPU:0, one launch (start us, length us, event | category | flops | bytes accessed | tf_op | source)
XLA Modules:
  0.0 119.7 jit_solution(16038533226493501560)
XLA Ops:
  0.6 1.8 %collective-permute-start = (bf16[1,1024,128]{2,1,0:T(8,128)(2,1)}, bf16[1,1024,128]{2,1,0:T(8,128)(2,1)S(1)}, u32[]{:S(2)}, u32[]{:S(2)}) collective-permute-start(bf16[1,1024,128]{2,1,0:T(8,128)(2,1)} %param.10), channel_id=1, source_target_pairs={{0,1},{1,0},{2,3},{3,2},{4,5},{5,4},{6,7},{7,6},{8,9},{9,8},{10,11... | collective-permute-start | bytes 786440 | tf_op jit(solution)/shard_map/ppermute | solution.py:49
  2.4 2.8 %constant_dynamic-slice_fusion = (bf16[1,1024,512]{2,1,0:T(8,128)(2,1)S(1)}, bf16[1,1024,512]{2,1,0:T(8,128)(2,1)}) fusion(bf16[1,2048,512]{2,1,0:T(8,128)(2,1)} %param.7, s32[]{:T(128)S(6)} %select_n.13, s32[]{:T(128)S(6)} %select_n.12), kind=kLoop, calls=%fused_computation.3 | loop fusion | bytes 4194312 | tf_op jit(solution)/shard_map/dynamic_slice | solution.py:349
  5.2 0.3 collective-permute-start.9
  5.6 4.5 %collective-permute-done = bf16[1,1024,128]{2,1,0:T(8,128)(2,1)S(1)} collective-permute-done((bf16[1,1024,128]{2,1,0:T(8,128)(2,1)}, bf16[1,1024,128]{2,1,0:T(8,128)(2,1)S(1)}, u32[]{:S(2)}, u32[]{:S(2)}) %collective-permute-start) | collective-permute-done | bytes 262176 | tf_op jit(solution)/shard_map/ppermute | solution.py:49
  10.1 3.2 %collective-permute-start.2 = (bf16[1,2048,128]{2,1,0:T(8,128)(2,1)S(1)}, bf16[1,2048,128]{2,1,0:T(8,128)(2,1)}, u32[]{:S(2)}, u32[]{:S(2)}) collective-permute-start(bf16[1,2048,128]{2,1,0:T(8,128)(2,1)S(1)} %constant_dynamic-update-slice_fusion.refs_0_), channel_id=1, source_target_pairs={{0,3},{1,2},{2,1},{3,0},{4,7},{5,6},{6,5},{7,4},{8,11},{9,10},{10,... | collective-permute-start | bytes 1572872 | tf_op jit(solution)/shard_map/ppermute | solution.py:49
  13.4 4.0 %collective-permute-start.1 = (bf16[1,2048,128]{2,1,0:T(8,128)(2,1)S(1)}, bf16[1,2048,128]{2,1,0:T(8,128)(2,1)}, u32[]{:S(2)}, u32[]{:S(2)}) collective-permute-start(bf16[1,2048,128]{2,1,0:T(8,128)(2,1)S(1)} %constant_dynamic-update-slice_fusion.refs_0_), channel_id=1, source_target_pairs={{0,12},{4,8},{8,4},{12,0},{1,13},{5,9},{9,5},{13,1},{2,14},{6,10},... | collective-permute-start | bytes 1572872 | tf_op jit(solution)/shard_map/ppermute | solution.py:49
  17.4 0.1 collective-permute-start.7
  17.5 5.9 %collective-permute-done.2.refs_1_ = bf16[1,2048,128]{2,1,0:T(8,128)(2,1)} collective-permute-done((bf16[1,2048,128]{2,1,0:T(8,128)(2,1)S(1)}, bf16[1,2048,128]{2,1,0:T(8,128)(2,1)}, u32[]{:S(2)}, u32[]{:S(2)}) %collective-permute-start.2) | collective-permute-done | bytes 524320 | tf_op jit(solution)/shard_map/ppermute | solution.py:49
  23.4 1.9 %collective-permute-start.5 = (bf16[1,2048,128]{2,1,0:T(8,128)(2,1)}, bf16[1,2048,128]{2,1,0:T(8,128)(2,1)}, u32[]{:S(2)}, u32[]{:S(2)}) collective-permute-start(bf16[1,2048,128]{2,1,0:T(8,128)(2,1)} %collective-permute-done.2.refs_1_), channel_id=1, source_target_pairs={{0,4},{4,0},{8,12},{12,8},{1,5},{5,1},{9,13},{13,9},{2,6},{6,2},{1... | collective-permute-start | bytes 1572872 | tf_op jit(solution)/shard_map/ppermute | solution.py:49
  25.3 0.1 collective-permute-start.8
  25.4 1.7 %multiply_reduce_fusion = f32[]{:T(128)} fusion(bf16[1,2048,512]{2,1,0:T(8,128)(2,1)S(1)} %copy-done.4), kind=kLoop, calls=%fused_computation | loop fusion | flops 3145727 | bytes 2097156 | tf_op jit(solution)/shard_map/reduce_sum | solution.py:352
  27.1 1.3 %broadcast_in_dim.2 = f32[128,1,128]{2,1,0:T(1,128)} broadcast(f32[]{:T(128)} %multiply_reduce_fusion), dimensions={} | broadcast | bytes 65540 | tf_op jit(solution)/shard_map/broadcast_in_dim | solution.py:54
  28.4 10.8 %all-to-all-start = ((f32[128,1,128]{2,1,0:T(1,128)}), f32[128,1,128]{2,1,0:T(1,128)S(1)}, u32[]{:S(2)}, u32[]{:S(2)}) async-start(f32[128,1,128]{2,1,0:T(1,128)} %broadcast_in_dim.2), calls=%async_computation | async-start | bytes 131072 | tf_op jit(solution)/shard_map/all_to_all | solution.py:54
  39.2 0.0 collective-permute-done.1.refs_0_
  39.2 2.9 %collective-permute-start.3 = (bf16[1,2048,128]{2,1,0:T(8,128)(2,1)}, bf16[1,2048,128]{2,1,0:T(8,128)(2,1)}, u32[]{:S(2)}, u32[]{:S(2)}) collective-permute-start(bf16[1,2048,128]{2,1,0:T(8,128)(2,1)} %collective-permute-done.2.refs_1_), channel_id=1, source_target_pairs={{0,12},{4,8},{8,4},{12,0},{1,13},{5,9},{9,5},{13,1},{2,14},{6,10},... | collective-permute-start | bytes 1572872 | tf_op jit(solution)/shard_map/ppermute | solution.py:49
  42.2 0.0 collective-permute-done.9.other_ref
  42.2 1.0 copy-done.7
  43.1 0.0 collective-permute-start.4
  43.1 3.9 %shard_map.86.refs_4_ = bf16[1024,512]{1,0:T(8,128)(2,1)} custom-call(bf16[1,1024,512]{2,1,0:T(8,128)(2,1)} %copy-done.5, bf16[1,1024,512]{2,1,0:T(8,128)(2,1)} %copy-done.7, bf16[1,1024,512]{2,1,0:T(8,128)(2,1)} %right_ref.7), custom_call_target="tpu_custom_call" | custom-call | flops 1073741824 | bytes 4194304 | tf_op jit(solution)/shard_map/pallas_call | solution.py:121
  47.1 0.0 collective-permute-done.5.refs_3_
  47.1 1.0 collective-permute-start.6
  48.0 12.6 %all-to-all-done.sums_ref = f32[128,1,128]{2,1,0:T(1,128)S(1)} async-done(((f32[128,1,128]{2,1,0:T(1,128)}), f32[128,1,128]{2,1,0:T(1,128)S(1)}, u32[]{:S(2)}, u32[]{:S(2)}) %all-to-all-start) | async-done | bytes 65568 | tf_op jit(solution)/shard_map/all_to_all | solution.py:54
  60.6 0.0 collective-permute-done.8.refs_2_
  60.6 0.6 copy-done.8
  61.2 9.9 %shard_map.87 = (f32[1,2048,512]{2,1,0:T(8,128)}, f32[1,2048,512]{2,1,0:T(8,128)}, bf16[1024,512]{1,0:T(8,128)(2,1)}, bf16[1024,512]{1,0:T(8,128)(2,1)}) custom-call(s32[1]{0:T(128)} %bitcast.1.block_ref, f32[128,1,128]{2,1,0:T(1,128)} %copy-done.8, bf16[1,2048,128]{2,1,0:T(8,128)(2,1)} %copy-done.6, bf16[1,2048,128]{2,1,0:T(8,128)(2,1)} %collective-permute-done.2.refs_1_, ...), custom_call_target="tpu_custom_call" | custom-call | flops 2684354560 | bytes 10485760 | tf_op jit(solution)/shard_map/pallas_call | solution.py:251
  71.1 0.4 collective-permute-start.13
  71.5 0.0 collective-permute-done.7.other_ref
  71.5 3.9 %shard_map.85.refs_4_ = bf16[1024,512]{1,0:T(8,128)(2,1)} custom-call(bf16[1,1024,512]{2,1,0:T(8,128)(2,1)} %get-tuple-element.24.own_ref, bf16[1,1024,512]{2,1,0:T(8,128)(2,1)} %collective-permute-done.7.other_ref, bf16[1,1024,512]{2,1,0:T(8,128)(2,1)} %right_ref.7), custom_call_target="tpu_custom_call" | custom-call | flops 1073741824 | bytes 4194304 | tf_op jit(solution)/shard_map/pallas_call | solution.py:121
  75.5 0.0 collective-permute-done.3.refs_1_
  75.5 0.0 collective-permute-done.4.refs_2_
  75.5 0.0 collective-permute-done.6.refs_3_
  75.5 9.9 %shard_map.88 = (f32[1,2048,512]{2,1,0:T(8,128)}, f32[1,2048,512]{2,1,0:T(8,128)}, bf16[1024,512]{1,0:T(8,128)(2,1)}, bf16[512,512]{1,0:T(8,128)(2,1)}, bf16[384...) custom-call(s32[1]{0:T(128)} %bitcast.block_ref, ...), custom_call_target="tpu_custom_call", output_to_operand_aliasing={{0}: (10, {}), {1}: (11, {})} | custom-call | flops 2684354560 | bytes 10485760 | tf_op jit(solution)/shard_map/pallas_call | solution.py:251
  85.4 2.0 %collective-permute-start.12 = (bf16[512,512]{1,0:T(8,128)(2,1)}, bf16[512,512]{1,0:T(8,128)(2,1)S(1)}, u32[]{:S(2)}, u32[]{:S(2)}) collective-permute-start(bf16[512,512]{1,0:T(8,128)(2,1)} %get-tuple-element.18), channel_id=1, source_target_pairs={{0,1},{1,0},{2,3},{3,2},{4,5},{5,4},{6,7},{7,6},{8,9},{9,8},{10,11... | collective-permute-start | bytes 1572872 | tf_op jit(solution)/shard_map/ppermute | solution.py:49
  87.4 0.1 collective-permute-start.11
  87.5 1.9 %collective-permute-start.10 = (bf16[128,512]{1,0:T(8,128)(2,1)}, bf16[128,512]{1,0:T(8,128)(2,1)S(1)}, u32[]{:S(2)}, u32[]{:S(2)}) collective-permute-start(bf16[128,512]{1,0:T(8,128)(2,1)} %get-tuple-element.16), channel_id=1, source_target_pairs={{0,1},{1,0},{2,3},{3,2},{4,5},{5,4},{6,7},{7,6},{8,9},{9,8},{10,11... | collective-permute-start | bytes 393224 | tf_op jit(solution)/shard_map/ppermute | solution.py:49
  89.4 1.2 %copy-done = bf16[1,1024,512]{2,1,0:T(8,128)(2,1)S(1)} copy-done((bf16[1,1024,512]{2,1,0:T(8,128)(2,1)S(1)}, bf16[1,1024,512]{2,1,0:T(8,128)(2,1)}, u32[]{:S(2)}) %copy-start) | copy-done | bytes 1048600
  90.6 1.6 %copy-done.1 = bf16[1,2048,512]{2,1,0:T(8,128)(2,1)S(1)} copy-done((bf16[1,2048,512]{2,1,0:T(8,128)(2,1)S(1)}, bf16[1,2048,512]{2,1,0:T(8,128)(2,1)}, u32[]{:S(2)}) %copy-start.1) | copy-done | bytes 2097176
  92.2 1.2 %copy-done.2 = bf16[1024,512]{1,0:T(8,128)(2,1)S(1)} copy-done((bf16[1024,512]{1,0:T(8,128)(2,1)S(1)}, bf16[1024,512]{1,0:T(8,128)(2,1)}, u32[]{:S(2)}) %copy-start.2) | copy-done | bytes 1048600
  93.4 1.5 %shard_map.90.base_ref = f32[1024,512]{1,0:T(8,128)S(1)} custom-call(s32[1]{0:T(128)} %bitcast.1.block_ref, bf16[1024,512]{1,0:T(8,128)(2,1)S(1)} %copy-done.2, bf16[1,1024,512]{2,1,0:T(8,128)(2,1)S(1)} %copy-done, bf16[1,2048,512]{2,1,0:T(8,128)(2,1)S(1)} %copy-done.1), custom_call_target="tpu_custom_call" | custom-call | flops 536870912 | bytes 5242880 | tf_op jit(solution)/shard_map/pallas_call | solution.py:288
  94.9 1.5 %shard_map.89.base_ref = f32[1024,512]{1,0:T(8,128)S(1)} custom-call(s32[1]{0:T(128)} %bitcast.block_ref, bf16[1024,512]{1,0:T(8,128)(2,1)S(1)} %copy-done.3, bf16[1,1024,512]{2,1,0:T(8,128)(2,1)S(1)} %copy-done, bf16[1,2048,512]{2,1,0:T(8,128)(2,1)S(1)} %copy-done.1), custom_call_target="tpu_custom_call" | custom-call | flops 536870912 | bytes 5242880 | tf_op jit(solution)/shard_map/pallas_call | solution.py:288
  96.4 1.3 %collective-permute-done.13.received_ref = bf16[1024,512]{1,0:T(8,128)(2,1)} collective-permute-done((bf16[1024,512]{1,0:T(8,128)(2,1)}, bf16[1024,512]{1,0:T(8,128)(2,1)}, u32[]{:S(2)}, u32[]{:S(2)}) %collective-permute-start.13) | collective-permute-done | bytes 1048608 | tf_op jit(solution)/shard_map/ppermute | solution.py:49
  97.8 5.3 %shard_map.91.refs_0_ = bf16[1,2048,512]{2,1,0:T(8,128)(2,1)} custom-call(s32[1]{0:T(128)} %bitcast.1.block_ref, f32[1024,512]{1,0:T(8,128)S(1)} %shard_map.90.base_ref, bf16[1024,512]{1,0:T(8,128)(2,1)} %collective-permute-done.13.received_ref), custom_call_target="tpu_custom_call" | custom-call | flops 1048576 | bytes 4194304 | tf_op jit(solution)/shard_map/pallas_call | solution.py:324
  103.0 5.9 %collective-permute-done.12.received_ref = bf16[512,512]{1,0:T(8,128)(2,1)S(1)} collective-permute-done((bf16[512,512]{1,0:T(8,128)(2,1)}, bf16[512,512]{1,0:T(8,128)(2,1)S(1)}, u32[]{:S(2)}, u32[]{:S(2)}) %collective-permute-start.12) | collective-permute-done | bytes 524320 | tf_op jit(solution)/shard_map/ppermute | solution.py:49
  108.9 1.4 %shard_map.92.refs_0_ = bf16[1,2048,512]{2,1,0:T(8,128)(2,1)} custom-call(s32[1]{0:T(128)} %bitcast.block_ref, f32[1024,512]{1,0:T(8,128)S(1)} %shard_map.89.base_ref, bf16[512,512]{1,0:T(8,128)(2,1)S(1)} %collective-permute-done.12.received_ref, bf16[1,2048,512]{2,1,0:T(8,128)(2,1)} %shard_map.91.refs_0_), custom_call_target="tpu_custom_call", output_to_operand_aliasing={{}: (3, {})} | custom-call | flops 524288 | bytes 2097152 | tf_op jit(solution)/shard_map/pallas_call | solution.py:324
  110.3 7.0 %collective-permute-done.11.received_ref = bf16[384,512]{1,0:T(8,128)(2,1)S(1)} collective-permute-done((bf16[384,512]{1,0:T(8,128)(2,1)}, bf16[384,512]{1,0:T(8,128)(2,1)S(1)}, u32[]{:S(2)}, u32[]{:S(2)}) %collective-permute-start.11) | collective-permute-done | bytes 393248 | tf_op jit(solution)/shard_map/ppermute | solution.py:49
  117.3 1.4 %shard_map.93.refs_0_ = bf16[1,2048,512]{2,1,0:T(8,128)(2,1)} custom-call(s32[1]{0:T(128)} %bitcast.block_ref, f32[1024,512]{1,0:T(8,128)S(1)} %shard_map.89.base_ref, bf16[384,512]{1,0:T(8,128)(2,1)S(1)} %collective-permute-done.11.received_ref, bf16[1,2048,512]{2,1,0:T(8,128)(2,1)} %shard_map.92.refs_0_), custom_call_target="tpu_custom_call", output_to_operand_aliasing={{}: (3, {})} | custom-call | flops 393216 | bytes 1572864 | tf_op jit(solution)/shard_map/pallas_call | solution.py:324
  118.7 0.3 collective-permute-done.10.received_ref
  119.0 0.7 shard_map.94
  (17 shorter events, 0.1 us)
Async XLA Ops:
  0.6 9.5 %collective-permute-start = (bf16[1,1024,128]{2,1,0:T(8,128)(2,1)}, bf16[1,1024,128]{2,1,0:T(8,128)(2,1)S(1)}, u32[]{:S(2)}, u32[]{:S(2)}) collective-permute-start(bf16[1,1024,128]{2,1,0:T(8,128)(2,1)} %param.10), channel_id=1, source_target_pairs={{0,1},{1,0},{2,3},{3,2},{4,5},{5,4},{6,7},{7,6},{8,9},{9,8},{10,11... | collective-permute-start | bytes 786440 | tf_op jit(solution)/shard_map/ppermute | solution.py:49
  2.4 3.1 %copy-start.9 = (bf16[1,1024,128]{2,1,0:T(8,128)(2,1)S(1)}, bf16[1,1024,128]{2,1,0:T(8,128)(2,1)}, u32[]{:S(2)}) copy-start(bf16[1,1024,128]{2,1,0:T(8,128)(2,1)} %param.10) | copy-start | bytes 786436
  2.4 23.0 %copy-start.4 = (bf16[1,2048,512]{2,1,0:T(8,128)(2,1)S(1)}, bf16[1,2048,512]{2,1,0:T(8,128)(2,1)}, u32[]{:S(2)}) copy-start(bf16[1,2048,512]{2,1,0:T(8,128)(2,1)} %param.7) | copy-start | bytes 6291460
  5.2 21.9 %copy-start.5 = (bf16[1,1024,512]{2,1,0:T(8,128)(2,1)}, bf16[1,1024,512]{2,1,0:T(8,128)(2,1)S(1)}, u32[]{:S(2)}) copy-start(bf16[1,1024,512]{2,1,0:T(8,128)(2,1)S(1)} %get-tuple-element.23.own_ref) | copy-start | bytes 3145732
  5.2 37.0 %collective-permute-start.9 = (bf16[1,1024,512]{2,1,0:T(8,128)(2,1)S(1)}, bf16[1,1024,512]{2,1,0:T(8,128)(2,1)S(1)}, u32[]{:S(2)}, u32[]{:S(2)}) collective-permute-start(bf16[1,1024,512]{2,1,0:T(8,128)(2,1)S(1)} %get-tuple-element.23.own_ref), channel_id=1, source_target_pairs={{0,1},{1,0},{2,3},{3,2},{4,5},{5,4},{6,7},{7,6},{8,9},{9,8},{10,11... | collective-permute-start | bytes 3145736 | tf_op jit(solution)/shard_map/ppermute | solution.py:49
  10.1 36.9 %copy-start.6 = (bf16[1,2048,128]{2,1,0:T(8,128)(2,1)}, bf16[1,2048,128]{2,1,0:T(8,128)(2,1)S(1)}, u32[]{:S(2)}) copy-start(bf16[1,2048,128]{2,1,0:T(8,128)(2,1)S(1)} %constant_dynamic-update-slice_fusion.refs_0_) | copy-start | bytes 1572868
  10.1 13.2 %collective-permute-start.2 = (bf16[1,2048,128]{2,1,0:T(8,128)(2,1)S(1)}, bf16[1,2048,128]{2,1,0:T(8,128)(2,1)}, u32[]{:S(2)}, u32[]{:S(2)}) collective-permute-start(bf16[1,2048,128]{2,1,0:T(8,128)(2,1)S(1)} %constant_dynamic-update-slice_fusion.refs_0_), channel_id=1, source_target_pairs={{0,3},{1,2},{2,1},{3,0},{4,7},{5,6},{6,5},{7,4},{8,11},{9,10},{10,... | collective-permute-start | bytes 1572872 | tf_op jit(solution)/shard_map/ppermute | solution.py:49
  13.4 25.9 %collective-permute-start.1 = (bf16[1,2048,128]{2,1,0:T(8,128)(2,1)S(1)}, bf16[1,2048,128]{2,1,0:T(8,128)(2,1)}, u32[]{:S(2)}, u32[]{:S(2)}) collective-permute-start(bf16[1,2048,128]{2,1,0:T(8,128)(2,1)S(1)} %constant_dynamic-update-slice_fusion.refs_0_), channel_id=1, source_target_pairs={{0,12},{4,8},{8,4},{12,0},{1,13},{5,9},{9,5},{13,1},{2,14},{6,10},... | collective-permute-start | bytes 1572872 | tf_op jit(solution)/shard_map/ppermute | solution.py:49
  17.4 54.2 %collective-permute-start.7 = (bf16[1,1024,512]{2,1,0:T(8,128)(2,1)}, bf16[1,1024,512]{2,1,0:T(8,128)(2,1)}, u32[]{:S(2)}, u32[]{:S(2)}) collective-permute-start(bf16[1,1024,512]{2,1,0:T(8,128)(2,1)} %get-tuple-element.24.own_ref), channel_id=1, source_target_pairs={{0,1},{1,0},{2,3},{3,2},{4,5},{5,4},{6,7},{7,6},{8,9},{9,8},{10,11... | collective-permute-start | bytes 3145736 | tf_op jit(solution)/shard_map/ppermute | solution.py:49
  23.4 23.7 %collective-permute-start.5 = (bf16[1,2048,128]{2,1,0:T(8,128)(2,1)}, bf16[1,2048,128]{2,1,0:T(8,128)(2,1)}, u32[]{:S(2)}, u32[]{:S(2)}) collective-permute-start(bf16[1,2048,128]{2,1,0:T(8,128)(2,1)} %collective-permute-done.2.refs_1_), channel_id=1, source_target_pairs={{0,4},{4,0},{8,12},{12,8},{1,5},{5,1},{9,13},{13,9},{2,6},{6,2},{1... | collective-permute-start | bytes 1572872 | tf_op jit(solution)/shard_map/ppermute | solution.py:49
  25.3 35.3 %collective-permute-start.8 = (bf16[1,2048,128]{2,1,0:T(8,128)(2,1)S(1)}, bf16[1,2048,128]{2,1,0:T(8,128)(2,1)}, u32[]{:S(2)}, u32[]{:S(2)}) collective-permute-start(bf16[1,2048,128]{2,1,0:T(8,128)(2,1)S(1)} %constant_dynamic-update-slice_fusion.refs_0_), channel_id=1, source_target_pairs={{0,4},{4,0},{8,12},{12,8},{1,5},{5,1},{9,13},{13,9},{2,6},{6,2},{1... | collective-permute-start | bytes 1572872 | tf_op jit(solution)/shard_map/ppermute | solution.py:49
  28.4 32.2 %all-to-all-start = ((f32[128,1,128]{2,1,0:T(1,128)}), f32[128,1,128]{2,1,0:T(1,128)S(1)}, u32[]{:S(2)}, u32[]{:S(2)}) async-start(f32[128,1,128]{2,1,0:T(1,128)} %broadcast_in_dim.2), calls=%async_computation | async-start | bytes 131072 | tf_op jit(solution)/shard_map/all_to_all | solution.py:54
  39.2 36.2 %collective-permute-start.3 = (bf16[1,2048,128]{2,1,0:T(8,128)(2,1)}, bf16[1,2048,128]{2,1,0:T(8,128)(2,1)}, u32[]{:S(2)}, u32[]{:S(2)}) collective-permute-start(bf16[1,2048,128]{2,1,0:T(8,128)(2,1)} %collective-permute-done.2.refs_1_), channel_id=1, source_target_pairs={{0,12},{4,8},{8,4},{12,0},{1,13},{5,9},{9,5},{13,1},{2,14},{6,10},... | collective-permute-start | bytes 1572872 | tf_op jit(solution)/shard_map/ppermute | solution.py:49
  42.2 1.0 copy-start.7
  43.1 32.4 %collective-permute-start.4 = (bf16[1,2048,128]{2,1,0:T(8,128)(2,1)}, bf16[1,2048,128]{2,1,0:T(8,128)(2,1)}, u32[]{:S(2)}, u32[]{:S(2)}) collective-permute-start(bf16[1,2048,128]{2,1,0:T(8,128)(2,1)} %collective-permute-done.1.refs_0_), channel_id=1, source_target_pairs={{0,4},{4,0},{8,12},{12,8},{1,5},{5,1},{9,13},{13,9},{2,6},{6,2},{1... | collective-permute-start | bytes 1572872 | tf_op jit(solution)/shard_map/ppermute | solution.py:49
  47.1 28.4 %collective-permute-start.6 = (bf16[1,2048,128]{2,1,0:T(8,128)(2,1)}, bf16[1,2048,128]{2,1,0:T(8,128)(2,1)}, u32[]{:S(2)}, u32[]{:S(2)}) collective-permute-start(bf16[1,2048,128]{2,1,0:T(8,128)(2,1)} %collective-permute-done.5.refs_3_), channel_id=1, source_target_pairs={{0,12},{4,8},{8,4},{12,0},{1,13},{5,9},{9,5},{13,1},{2,14},{6,10},... | collective-permute-start | bytes 1572872 | tf_op jit(solution)/shard_map/ppermute | solution.py:49
  60.6 0.6 copy-start.8
  71.1 26.6 %collective-permute-start.13 = (bf16[1024,512]{1,0:T(8,128)(2,1)}, bf16[1024,512]{1,0:T(8,128)(2,1)}, u32[]{:S(2)}, u32[]{:S(2)}) collective-permute-start(bf16[1024,512]{1,0:T(8,128)(2,1)} %get-tuple-element.20), channel_id=1, source_target_pairs={{0,1},{1,0},{2,3},{3,2},{4,5},{5,4},{6,7},{7,6},{8,9},{9,8},{10,11... | collective-permute-start | bytes 3145736 | tf_op jit(solution)/shard_map/ppermute | solution.py:49
  85.4 23.5 %collective-permute-start.12 = (bf16[512,512]{1,0:T(8,128)(2,1)}, bf16[512,512]{1,0:T(8,128)(2,1)S(1)}, u32[]{:S(2)}, u32[]{:S(2)}) collective-permute-start(bf16[512,512]{1,0:T(8,128)(2,1)} %get-tuple-element.18), channel_id=1, source_target_pairs={{0,1},{1,0},{2,3},{3,2},{4,5},{5,4},{6,7},{7,6},{8,9},{9,8},{10,11... | collective-permute-start | bytes 1572872 | tf_op jit(solution)/shard_map/ppermute | solution.py:49
  87.4 29.9 %collective-permute-start.11 = (bf16[384,512]{1,0:T(8,128)(2,1)}, bf16[384,512]{1,0:T(8,128)(2,1)S(1)}, u32[]{:S(2)}, u32[]{:S(2)}) collective-permute-start(bf16[384,512]{1,0:T(8,128)(2,1)} %get-tuple-element.17), channel_id=1, source_target_pairs={{0,1},{1,0},{2,3},{3,2},{4,5},{5,4},{6,7},{7,6},{8,9},{9,8},{10,11... | collective-permute-start | bytes 1179656 | tf_op jit(solution)/shard_map/ppermute | solution.py:49
  87.5 31.5 %collective-permute-start.10 = (bf16[128,512]{1,0:T(8,128)(2,1)}, bf16[128,512]{1,0:T(8,128)(2,1)S(1)}, u32[]{:S(2)}, u32[]{:S(2)}) collective-permute-start(bf16[128,512]{1,0:T(8,128)(2,1)} %get-tuple-element.16), channel_id=1, source_target_pairs={{0,1},{1,0},{2,3},{3,2},{4,5},{5,4},{6,7},{7,6},{8,9},{9,8},{10,11... | collective-permute-start | bytes 393224 | tf_op jit(solution)/shard_map/ppermute | solution.py:49
  89.4 1.2 %copy-start = (bf16[1,1024,512]{2,1,0:T(8,128)(2,1)S(1)}, bf16[1,1024,512]{2,1,0:T(8,128)(2,1)}, u32[]{:S(2)}) copy-start(bf16[1,1024,512]{2,1,0:T(8,128)(2,1)} %right_ref.7) | copy-start | bytes 3145732
  90.6 1.6 %copy-start.1 = (bf16[1,2048,512]{2,1,0:T(8,128)(2,1)S(1)}, bf16[1,2048,512]{2,1,0:T(8,128)(2,1)}, u32[]{:S(2)}) copy-start(bf16[1,2048,512]{2,1,0:T(8,128)(2,1)} %weight_ref.3) | copy-start | bytes 6291460
  92.2 1.2 %copy-start.2 = (bf16[1024,512]{1,0:T(8,128)(2,1)S(1)}, bf16[1024,512]{1,0:T(8,128)(2,1)}, u32[]{:S(2)}) copy-start(bf16[1024,512]{1,0:T(8,128)(2,1)} %get-tuple-element.19.turned_ref) | copy-start | bytes 3145732
  93.4 1.5 %copy-start.3 = (bf16[1024,512]{1,0:T(8,128)(2,1)S(1)}, bf16[1024,512]{1,0:T(8,128)(2,1)}, u32[]{:S(2)}) copy-start(bf16[1024,512]{1,0:T(8,128)(2,1)} %get-tuple-element.15.turned_ref) | copy-start | bytes 3145732

commit v4 on v3

--- a/solution.py
+++ b/solution.py
@@ -50,8 +50,56 @@
 
 
 def every_sum(value):
-    devices = lax.axis_size(AXES)
-    return lax.all_to_all(jnp.broadcast_to(value, (devices, 1, 128)), AXES, 0, 0, tiled=True)
+    value = value + permute(value, "y", near)
+    value = value + permute(value, "y", far)
+    axes = ("x", "core", "z")
+    return lax.all_to_all(
+        jnp.broadcast_to(value, (lax.axis_size(axes), 1, 128)), axes, 0, 0, tiled=True
+    )
+
+
+def split_kernel(block_ref, first_ref, second_ref, near_ref, far_ref, sum_ref, partial):
+    step = pl.program_id(0)
+
+    @pl.when(step == 0)
+    def _():
+        partial[...] = jnp.zeros_like(partial)
+
+    near_ref[...] = first_ref[...]
+    far_ref[...] = second_ref[...]
+    one = first_ref[0].astype(f32)
+    two = second_ref[0].astype(f32)
+    squares = (one * one + two * two).reshape(-1, *partial.shape)
+    partial[...] += jnp.sum(squares, axis=0)
+
+    @pl.when(step == pl.num_programs(0) - 1)
+    def _():
+        sum_ref[0] = jnp.broadcast_to(jnp.sum(partial[...], keepdims=True), (1, 128))
+
+
+def split(which, grad, block):
+    _, _, width = grad.shape
+    rows = 512
+    steps = block // rows
+    half = jax.ShapeDtypeStruct((1, block, width), bf16)
+    chunk = pl.BlockSpec((1, rows, width), lambda s, b: (0, s, 0))
+    return pl.pallas_call(
+        split_kernel,
+        grid_spec=pltpu.PrefetchScalarGridSpec(
+            num_scalar_prefetch=1,
+            grid=(steps,),
+            in_specs=[
+                pl.BlockSpec((1, rows, width), lambda s, b: (0, b[0] * steps + s, 0)),
+                pl.BlockSpec((1, rows, width), lambda s, b: (0, (1 - b[0]) * steps + s, 0)),
+            ],
+            out_specs=[chunk, chunk, pl.BlockSpec((1, 1, 128), lambda s, b: (0, 0, 0))],
+            scratch_shapes=[pltpu.VMEM((8, width), f32)],
+        ),
+        out_shape=[half, half, jax.ShapeDtypeStruct((1, 1, 128), f32)],
+        cost_estimate=cost(4 * block * width, 8 * block * width),
+        compiler_params=limit(63),
+        name="split",
+    )(which, grad, grad)
 
 
 def gather_left(shard):
@@ -235,7 +283,7 @@
 def moments(is_near, which, sums, shards, term, right, first, second, previous, pieces):
     _, all_rows, width = first.shape
     block = right.shape[1]
-    count = sums.shape[0] * all_rows * width
+    count = lax.axis_size(AXES) * all_rows * width
     whole = jax.ShapeDtypeStruct((1, all_rows, width), f32)
     part = jax.ShapeDtypeStruct((block, width), bf16)
     sends = [jax.ShapeDtypeStruct((size, width), bf16) for _, size in pieces]
@@ -346,14 +394,11 @@
     near_id = near_block.reshape(1)
     far_id = far_block.reshape(1)
 
-    own_near = lax.dynamic_slice_in_dim(grad, near_block * block, block, axis=1)
+    own_near, own_far, local_sum = split(near_id, grad, block)
     other_near = permute(own_near, "y", near)
-
-    local_sum = jnp.sum(jnp.square(grad.astype(f32))).reshape(1, 1, 1)
     sums = every_sum(local_sum)
     left_near, left_far = gather_left(left_basis)
 
-    own_far = lax.dynamic_slice_in_dim(grad, far_block * block, block, axis=1)
     other_far = permute(own_far, "y", near)
 
     term = rotate_right(own_near, other_near, right_basis)

time: 120 us -> 147 us (1.23)
  waiting for transfers between devices: 37.5 us -> 61.6 us
  starting transfers between devices: 30.6 us -> 35.1 us
  local copies, waits for them, and re-layouts: 9.8 us -> 6.32 us
  Pallas kernels: 39.3 us -> 42.1 us
    ppermute x14 -> x16, waiting for transfers between devices: 24.9 us -> 52.3 us  [permute(): return lax.ppermute(value, axis, pairs)]
    ppermute x14 -> x16, starting transfers between devices: 19.8 us -> 27.3 us  [permute(): return lax.ppermute(value, axis, pairs)]
    all_to_all x1, waiting for transfers between devices: 12.6 us -> 9.32 us  [every_sum(): lax.all_to_all(jnp.broadcast_to(value, (lax.axis_size(axes), 1, 128)), ax...]
    pallas_call x0 -> x1, Pallas kernels: none -> 3.11 us  [split(): pl.pallas_call(split_kernel, grid_spec=pltpu.PrefetchScalarGridSpec(num_s...]
    all_to_all x1, starting transfers between devices: 10.8 us -> 7.71 us  [every_sum(): lax.all_to_all(jnp.broadcast_to(value, (lax.axis_size(axes), 1, 128)), ax...]
    dynamic_slice x1 -> x0, local copies, waits for them, and re-layouts: 2.79 us -> none  [on_device(): own_near = lax.dynamic_slice_in_dim(grad, near_block * block, block, axis=1)]
    reduce_sum x1 -> x0, other arithmetic: 1.68 us -> none  [on_device(): local_sum = jnp.sum(jnp.square(grad.astype(f32))).reshape(1, 1, 1)]
    unnamed x21 -> x17, local copies, waits for them, and re-layouts: 5.66 us -> 4.72 us
  transfers between devices with their start and end apart: 15 -> 17, of which waited for: 7 -> 7; matrix products, arithmetic and copies ran while one was open for 5% -> 2% of each run, Pallas kernels for 32% -> 28%
where the time goes in v4:
time: 147 us
  waiting for transfers between devices  61.6 us (42%)
  Pallas kernels  42.1 us (29%)
  starting transfers between devices  35.1 us (24%)
  local copies, waits for them, and re-layouts  6.32 us (4%)
    ppermute x16, waiting for transfers between devices, permute(): return lax.ppermute(value, axis, pairs)  52.3 us
    ppermute x16, starting transfers between devices, permute(): return lax.ppermute(value, axis, pairs)  27.3 us
    pallas_call x2, Pallas kernels, moments(): pl.pallas_call(functools.partial(moments_kernel, is_near, count, pieces),...  19.5 us
    all_to_all x1, waiting for transfers between devices, every_sum(): lax.all_to_all(jnp.broadcast_to(value, (lax.axis_size(axes), 1, 128)), ax...  9.32 us
    pallas_call x4, Pallas kernels, finish(): pl.pallas_call(finish_kernel, grid_spec=pltpu.PrefetchScalarGridSpec(num_...  8.75 us
    pallas_call x2, Pallas kernels, rotate_right(): pl.pallas_call(rotate_right_kernel, out_shape=jax.ShapeDtypeStruct((block...  7.83 us
    all_to_all x1, starting transfers between devices, every_sum(): lax.all_to_all(jnp.broadcast_to(value, (lax.axis_size(axes), 1, 128)), ax...  7.71 us
    unnamed x17, local copies, waits for them, and re-layouts  4.72 us
  transfers between devices with their start and end apart: 17, of which 7 were waited for; matrix products, arithmetic and copies ran while one was open for 2% of the time, Pallas kernels for 28%

profile of v4, /device:TPU:0, one launch (start us, length us, event | category | flops | bytes accessed | tf_op | source)
XLA Modules:
  0.0 146.6 jit_solution(15201133446541359495)
XLA Ops:
  0.6 1.8 %collective-permute-start.2 = (bf16[1,1024,128]{2,1,0:T(8,128)(2,1)}, bf16[1,1024,128]{2,1,0:T(8,128)(2,1)}, u32[]{:S(2)}, u32[]{:S(2)}) collective-permute-start(bf16[1,1024,128]{2,1,0:T(8,128)(2,1)} %param.10), channel_id=1, source_target_pairs={{0,1},{1,0},{2,3},{3,2},{4,5},{5,4},{6,7},{7,6},{8,9},{9,8},{10,11... | collective-permute-start | bytes 786440 | tf_op jit(solution)/shard_map/ppermute | solution.py:49
  2.4 3.1 %split.1 = (bf16[1,1024,512]{2,1,0:T(8,128)(2,1)}, bf16[1,1024,512]{2,1,0:T(8,128)(2,1)}, f32[1,1,128]{2,1,0:T(1,128)}) custom-call(s32[1]{0:T(128)} %bitcast.1.block_ref, bf16[1,2048,512]{2,1,0:T(8,128)(2,1)} %second_ref.1, bf16[1,2048,512]{2,1,0:T(8,128)(2,1)} %second_ref.1), custom_call_target="tpu_custom_call" | custom-call | flops 2097152 | bytes 4194304 | tf_op jit(solution)/shard_map/split/pallas_call | solution.py:86
  5.5 0.3 collective-permute-start.11
  5.9 4.2 %collective-permute-done.2 = bf16[1,1024,128]{2,1,0:T(8,128)(2,1)} collective-permute-done((bf16[1,1024,128]{2,1,0:T(8,128)(2,1)}, bf16[1,1024,128]{2,1,0:T(8,128)(2,1)}, u32[]{:S(2)}, u32[]{:S(2)}) %collective-permute-start.2) | collective-permute-done | bytes 262176 | tf_op jit(solution)/shard_map/ppermute | solution.py:49
  10.1 1.0 constant_dynamic-update-slice_fusion.refs_0_
  11.1 3.3 %collective-permute-start.4 = (bf16[1,2048,128]{2,1,0:T(8,128)(2,1)S(1)}, bf16[1,2048,128]{2,1,0:T(8,128)(2,1)}, u32[]{:S(2)}, u32[]{:S(2)}) collective-permute-start(bf16[1,2048,128]{2,1,0:T(8,128)(2,1)S(1)} %constant_dynamic-update-slice_fusion.refs_0_), channel_id=1, source_target_pairs={{0,3},{1,2},{2,1},{3,0},{4,7},{5,6},{6,5},{7,4},{8,11},{9,10},{10,... | collective-permute-start | bytes 1572872 | tf_op jit(solution)/shard_map/ppermute | solution.py:49
  14.4 4.0 %collective-permute-start.3 = (bf16[1,2048,128]{2,1,0:T(8,128)(2,1)S(1)}, bf16[1,2048,128]{2,1,0:T(8,128)(2,1)}, u32[]{:S(2)}, u32[]{:S(2)}) collective-permute-start(bf16[1,2048,128]{2,1,0:T(8,128)(2,1)S(1)} %constant_dynamic-update-slice_fusion.refs_0_), channel_id=1, source_target_pairs={{0,12},{4,8},{8,4},{12,0},{1,13},{5,9},{9,5},{13,1},{2,14},{6,10},... | collective-permute-start | bytes 1572872 | tf_op jit(solution)/shard_map/ppermute | solution.py:49
  18.4 0.1 collective-permute-start.9
  18.6 1.9 %collective-permute-start = (f32[1,1,128]{2,1,0:T(1,128)}, f32[1,1,128]{2,1,0:T(1,128)S(1)}, u32[]{:S(2)}, u32[]{:S(2)}) collective-permute-start(f32[1,1,128]{2,1,0:T(1,128)} %get-tuple-element.16), channel_id=1, source_target_pairs={{0,1},{1,0},{2,3},{3,2},{4,5},{5,4},{6,7},{7,6},{8,9},{9,8},{10,11... | collective-permute-start | bytes 1544 | tf_op jit(solution)/shard_map/ppermute | solution.py:49
  20.5 33.5 %collective-permute-done = f32[1,1,128]{2,1,0:T(1,128)S(1)} collective-permute-done((f32[1,1,128]{2,1,0:T(1,128)}, f32[1,1,128]{2,1,0:T(1,128)S(1)}, u32[]{:S(2)}, u32[]{:S(2)}) %collective-permute-start) | collective-permute-done | bytes 544 | tf_op jit(solution)/shard_map/ppermute | solution.py:49
  54.0 0.7 add.7
  54.6 3.2 %collective-permute-start.1 = (f32[1,1,128]{2,1,0:T(1,128)S(1)}, f32[1,1,128]{2,1,0:T(1,128)S(1)}, u32[]{:S(2)}, u32[]{:S(2)}) collective-permute-start(f32[1,1,128]{2,1,0:T(1,128)S(1)} %add.7), channel_id=1, source_target_pairs={{0,3},{1,2},{2,1},{3,0},{4,7},{5,6},{6,5},{7,4},{8,11},{9,10},{10,... | collective-permute-start | bytes 1544 | tf_op jit(solution)/shard_map/ppermute | solution.py:49
  57.8 0.0 collective-permute-done.4.refs_1_
  57.8 1.9 %collective-permute-start.7 = (bf16[1,2048,128]{2,1,0:T(8,128)(2,1)}, bf16[1,2048,128]{2,1,0:T(8,128)(2,1)}, u32[]{:S(2)}, u32[]{:S(2)}) collective-permute-start(bf16[1,2048,128]{2,1,0:T(8,128)(2,1)} %collective-permute-done.4.refs_1_), channel_id=1, source_target_pairs={{0,4},{4,0},{8,12},{12,8},{1,5},{5,1},{9,13},{13,9},{2,6},{6,2},{1... | collective-permute-start | bytes 1572872 | tf_op jit(solution)/shard_map/ppermute | solution.py:49
  59.7 0.0 collective-permute-done.1
  59.7 1.8 %collective-permute-start.10 = (bf16[1,2048,128]{2,1,0:T(8,128)(2,1)S(1)}, bf16[1,2048,128]{2,1,0:T(8,128)(2,1)}, u32[]{:S(2)}, u32[]{:S(2)}) collective-permute-start(bf16[1,2048,128]{2,1,0:T(8,128)(2,1)S(1)} %constant_dynamic-update-slice_fusion.refs_0_), channel_id=1, source_target_pairs={{0,4},{4,0},{8,12},{12,8},{1,5},{5,1},{9,13},{13,9},{2,6},{6,2},{1... | collective-permute-start | bytes 1572872 | tf_op jit(solution)/shard_map/ppermute | solution.py:49
  61.5 0.6 broadcast_in_dim.8
  62.1 7.7 %all-to-all-start = ((f32[32,1,128]{2,1,0:T(1,128)}), f32[32,1,128]{2,1,0:T(1,128)S(1)}, u32[]{:S(2)}, u32[]{:S(2)}) async-start(f32[32,1,128]{2,1,0:T(1,128)} %broadcast_in_dim.8), calls=%async_computation | async-start | bytes 32768 | tf_op jit(solution)/shard_map/all_to_all | solution.py:56
  69.8 0.0 collective-permute-done.3.refs_0_
  69.8 3.1 %collective-permute-start.5 = (bf16[1,2048,128]{2,1,0:T(8,128)(2,1)}, bf16[1,2048,128]{2,1,0:T(8,128)(2,1)}, u32[]{:S(2)}, u32[]{:S(2)}) collective-permute-start(bf16[1,2048,128]{2,1,0:T(8,128)(2,1)} %collective-permute-done.4.refs_1_), channel_id=1, source_target_pairs={{0,12},{4,8},{8,4},{12,0},{1,13},{5,9},{9,5},{13,1},{2,14},{6,10},... | collective-permute-start | bytes 1572872 | tf_op jit(solution)/shard_map/ppermute | solution.py:49
  72.9 0.3 collective-permute-start.6
  73.2 3.9 %shard_map.86.refs_4_ = bf16[1024,512]{1,0:T(8,128)(2,1)} custom-call(bf16[1,1024,512]{2,1,0:T(8,128)(2,1)} %get-tuple-element.18.own_ref, bf16[1,1024,512]{2,1,0:T(8,128)(2,1)} %collective-permute-done.11.other_ref, bf16[1,1024,512]{2,1,0:T(8,128)(2,1)} %right_ref.7), custom_call_target="tpu_custom_call" | custom-call | flops 1073741824 | bytes 4194304 | tf_op jit(solution)/shard_map/pallas_call | solution.py:169
  77.1 1.2 collective-permute-start.8
  78.4 9.3 %all-to-all-done.sums_ref = f32[32,1,128]{2,1,0:T(1,128)S(1)} async-done(((f32[32,1,128]{2,1,0:T(1,128)}), f32[32,1,128]{2,1,0:T(1,128)S(1)}, u32[]{:S(2)}, u32[]{:S(2)}) %all-to-all-start) | async-done | bytes 16416 | tf_op jit(solution)/shard_map/all_to_all | solution.py:56
  87.7 0.6 copy-done.7
  88.3 9.7 %shard_map.87 = (f32[1,2048,512]{2,1,0:T(8,128)}, f32[1,2048,512]{2,1,0:T(8,128)}, bf16[1024,512]{1,0:T(8,128)(2,1)}, bf16[1024,512]{1,0:T(8,128)(2,1)}) custom-call(s32[1]{0:T(128)} %bitcast.1.block_ref, f32[32,1,128]{2,1,0:T(1,128)} %copy-done.7, bf16[1,2048,128]{2,1,0:T(8,128)(2,1)} %copy-done.5, bf16[1,2048,128]{2,1,0:T(8,128)(2,1)} %collective-permute-done.4.refs_1_, ...), custom_call_target="tpu_custom_call" | custom-call | flops 2684354560 | bytes 10485760 | tf_op jit(solution)/shard_map/pallas_call | solution.py:299
  98.0 0.4 collective-permute-start.15
  98.4 0.0 collective-permute-done.9.other_ref
  98.4 3.9 %shard_map.85.refs_4_ = bf16[1024,512]{1,0:T(8,128)(2,1)} custom-call(bf16[1,1024,512]{2,1,0:T(8,128)(2,1)} %get-tuple-element.17.own_ref, bf16[1,1024,512]{2,1,0:T(8,128)(2,1)} %collective-permute-done.9.other_ref, bf16[1,1024,512]{2,1,0:T(8,128)(2,1)} %right_ref.7), custom_call_target="tpu_custom_call" | custom-call | flops 1073741824 | bytes 4194304 | tf_op jit(solution)/shard_map/pallas_call | solution.py:169
  102.4 0.0 collective-permute-done.5.refs_1_
  102.4 9.8 %shard_map.88 = (f32[1,2048,512]{2,1,0:T(8,128)}, f32[1,2048,512]{2,1,0:T(8,128)}, bf16[1024,512]{1,0:T(8,128)(2,1)}, bf16[512,512]{1,0:T(8,128)(2,1)}, bf16[384...) custom-call(s32[1]{0:T(128)} %bitcast.block_ref, ...), custom_call_target="tpu_custom_call", output_to_operand_aliasing={{0}: (10, {}), {1}: (11, {})} | custom-call | flops 2684354560 | bytes 10485760 | tf_op jit(solution)/shard_map/pallas_call | solution.py:299
  112.2 2.0 %collective-permute-start.14 = (bf16[512,512]{1,0:T(8,128)(2,1)}, bf16[512,512]{1,0:T(8,128)(2,1)S(1)}, u32[]{:S(2)}, u32[]{:S(2)}) collective-permute-start(bf16[512,512]{1,0:T(8,128)(2,1)} %get-tuple-element.24), channel_id=1, source_target_pairs={{0,1},{1,0},{2,3},{3,2},{4,5},{5,4},{6,7},{7,6},{8,9},{9,8},{10,11... | collective-permute-start | bytes 1572872 | tf_op jit(solution)/shard_map/ppermute | solution.py:49
  114.2 0.1 collective-permute-start.13
  114.3 1.9 %collective-permute-start.12 = (bf16[128,512]{1,0:T(8,128)(2,1)}, bf16[128,512]{1,0:T(8,128)(2,1)S(1)}, u32[]{:S(2)}, u32[]{:S(2)}) collective-permute-start(bf16[128,512]{1,0:T(8,128)(2,1)} %get-tuple-element.22), channel_id=1, source_target_pairs={{0,1},{1,0},{2,3},{3,2},{4,5},{5,4},{6,7},{7,6},{8,9},{9,8},{10,11... | collective-permute-start | bytes 393224 | tf_op jit(solution)/shard_map/ppermute | solution.py:49
  116.2 1.2 copy-done
  117.4 1.6 %copy-done.2 = bf16[1,2048,512]{2,1,0:T(8,128)(2,1)S(1)} copy-done((bf16[1,2048,512]{2,1,0:T(8,128)(2,1)S(1)}, bf16[1,2048,512]{2,1,0:T(8,128)(2,1)}, u32[]{:S(2)}) %copy-start.2) | copy-done | bytes 2097176
  119.0 1.2 copy-done.3
  120.2 1.5 shard_map.90.base_ref
  121.7 0.1 copy-done.4
  121.8 1.5 shard_map.89.base_ref
  123.2 1.4 collective-permute-done.15.received_ref
  124.6 5.3 %shard_map.91.refs_0_ = bf16[1,2048,512]{2,1,0:T(8,128)(2,1)} custom-call(s32[1]{0:T(128)} %bitcast.1.block_ref, f32[1024,512]{1,0:T(8,128)S(1)} %shard_map.90.base_ref, bf16[1024,512]{1,0:T(8,128)(2,1)} %collective-permute-done.15.received_ref), custom_call_target="tpu_custom_call" | custom-call | flops 1048576 | bytes 4194304 | tf_op jit(solution)/shard_map/pallas_call | solution.py:372
  129.9 5.9 %collective-permute-done.14.received_ref = bf16[512,512]{1,0:T(8,128)(2,1)S(1)} collective-permute-done((bf16[512,512]{1,0:T(8,128)(2,1)}, bf16[512,512]{1,0:T(8,128)(2,1)S(1)}, u32[]{:S(2)}, u32[]{:S(2)}) %collective-permute-start.14) | collective-permute-done | bytes 524320 | tf_op jit(solution)/shard_map/ppermute | solution.py:49
  135.8 1.4 shard_map.92.refs_0_
  137.2 7.0 %collective-permute-done.13.received_ref = bf16[384,512]{1,0:T(8,128)(2,1)S(1)} collective-permute-done((bf16[384,512]{1,0:T(8,128)(2,1)}, bf16[384,512]{1,0:T(8,128)(2,1)S(1)}, u32[]{:S(2)}, u32[]{:S(2)}) %collective-permute-start.13) | collective-permute-done | bytes 393248 | tf_op jit(solution)/shard_map/ppermute | solution.py:49
  144.2 1.4 shard_map.93.refs_0_
  145.6 0.3 collective-permute-done.12.received_ref
  145.9 0.7 shard_map.94
  (18 shorter events, 0.1 us)
Async XLA Ops:
  0.6 9.4 %collective-permute-start.2 = (bf16[1,1024,128]{2,1,0:T(8,128)(2,1)}, bf16[1,1024,128]{2,1,0:T(8,128)(2,1)}, u32[]{:S(2)}, u32[]{:S(2)}) collective-permute-start(bf16[1,1024,128]{2,1,0:T(8,128)(2,1)} %param.10), channel_id=1, source_target_pairs={{0,1},{1,0},{2,3},{3,2},{4,5},{5,4},{6,7},{7,6},{8,9},{9,8},{10,11... | collective-permute-start | bytes 786440 | tf_op jit(solution)/shard_map/ppermute | solution.py:49
  2.4 3.5 %copy-start.6 = (bf16[1,1024,128]{2,1,0:T(8,128)(2,1)S(1)}, bf16[1,1024,128]{2,1,0:T(8,128)(2,1)}, u32[]{:S(2)}) copy-start(bf16[1,1024,128]{2,1,0:T(8,128)(2,1)} %param.10) | copy-start | bytes 786436
  5.5 67.4 %collective-permute-start.11 = (bf16[1,1024,512]{2,1,0:T(8,128)(2,1)}, bf16[1,1024,512]{2,1,0:T(8,128)(2,1)}, u32[]{:S(2)}, u32[]{:S(2)}) collective-permute-start(bf16[1,1024,512]{2,1,0:T(8,128)(2,1)} %get-tuple-element.18.own_ref), channel_id=1, source_target_pairs={{0,1},{1,0},{2,3},{3,2},{4,5},{5,4},{6,7},{7,6},{8,9},{9,8},{10,11... | collective-permute-start | bytes 3145736 | tf_op jit(solution)/shard_map/ppermute | solution.py:49
  11.0 66.0 %copy-start.5 = (bf16[1,2048,128]{2,1,0:T(8,128)(2,1)}, bf16[1,2048,128]{2,1,0:T(8,128)(2,1)S(1)}, u32[]{:S(2)}) copy-start(bf16[1,2048,128]{2,1,0:T(8,128)(2,1)S(1)} %constant_dynamic-update-slice_fusion.refs_0_) | copy-start | bytes 1572868
  11.1 46.8 %collective-permute-start.4 = (bf16[1,2048,128]{2,1,0:T(8,128)(2,1)S(1)}, bf16[1,2048,128]{2,1,0:T(8,128)(2,1)}, u32[]{:S(2)}, u32[]{:S(2)}) collective-permute-start(bf16[1,2048,128]{2,1,0:T(8,128)(2,1)S(1)} %constant_dynamic-update-slice_fusion.refs_0_), channel_id=1, source_target_pairs={{0,3},{1,2},{2,1},{3,0},{4,7},{5,6},{6,5},{7,4},{8,11},{9,10},{10,... | collective-permute-start | bytes 1572872 | tf_op jit(solution)/shard_map/ppermute | solution.py:49
  14.4 55.4 %collective-permute-start.3 = (bf16[1,2048,128]{2,1,0:T(8,128)(2,1)S(1)}, bf16[1,2048,128]{2,1,0:T(8,128)(2,1)}, u32[]{:S(2)}, u32[]{:S(2)}) collective-permute-start(bf16[1,2048,128]{2,1,0:T(8,128)(2,1)S(1)} %constant_dynamic-update-slice_fusion.refs_0_), channel_id=1, source_target_pairs={{0,12},{4,8},{8,4},{12,0},{1,13},{5,9},{9,5},{13,1},{2,14},{6,10},... | collective-permute-start | bytes 1572872 | tf_op jit(solution)/shard_map/ppermute | solution.py:49
  18.4 80.0 %collective-permute-start.9 = (bf16[1,1024,512]{2,1,0:T(8,128)(2,1)}, bf16[1,1024,512]{2,1,0:T(8,128)(2,1)}, u32[]{:S(2)}, u32[]{:S(2)}) collective-permute-start(bf16[1,1024,512]{2,1,0:T(8,128)(2,1)} %get-tuple-element.17.own_ref), channel_id=1, source_target_pairs={{0,1},{1,0},{2,3},{3,2},{4,5},{5,4},{6,7},{7,6},{8,9},{9,8},{10,11... | collective-permute-start | bytes 3145736 | tf_op jit(solution)/shard_map/ppermute | solution.py:49
  18.6 35.4 %collective-permute-start = (f32[1,1,128]{2,1,0:T(1,128)}, f32[1,1,128]{2,1,0:T(1,128)S(1)}, u32[]{:S(2)}, u32[]{:S(2)}) collective-permute-start(f32[1,1,128]{2,1,0:T(1,128)} %get-tuple-element.16), channel_id=1, source_target_pairs={{0,1},{1,0},{2,3},{3,2},{4,5},{5,4},{6,7},{7,6},{8,9},{9,8},{10,11... | collective-permute-start | bytes 1544 | tf_op jit(solution)/shard_map/ppermute | solution.py:49
  54.6 5.1 %collective-permute-start.1 = (f32[1,1,128]{2,1,0:T(1,128)S(1)}, f32[1,1,128]{2,1,0:T(1,128)S(1)}, u32[]{:S(2)}, u32[]{:S(2)}) collective-permute-start(f32[1,1,128]{2,1,0:T(1,128)S(1)} %add.7), channel_id=1, source_target_pairs={{0,3},{1,2},{2,1},{3,0},{4,7},{5,6},{6,5},{7,4},{8,11},{9,10},{10,... | collective-permute-start | bytes 1544 | tf_op jit(solution)/shard_map/ppermute | solution.py:49
  57.8 19.3 %collective-permute-start.7 = (bf16[1,2048,128]{2,1,0:T(8,128)(2,1)}, bf16[1,2048,128]{2,1,0:T(8,128)(2,1)}, u32[]{:S(2)}, u32[]{:S(2)}) collective-permute-start(bf16[1,2048,128]{2,1,0:T(8,128)(2,1)} %collective-permute-done.4.refs_1_), channel_id=1, source_target_pairs={{0,4},{4,0},{8,12},{12,8},{1,5},{5,1},{9,13},{13,9},{2,6},{6,2},{1... | collective-permute-start | bytes 1572872 | tf_op jit(solution)/shard_map/ppermute | solution.py:49
  59.7 28.0 %collective-permute-start.10 = (bf16[1,2048,128]{2,1,0:T(8,128)(2,1)S(1)}, bf16[1,2048,128]{2,1,0:T(8,128)(2,1)}, u32[]{:S(2)}, u32[]{:S(2)}) collective-permute-start(bf16[1,2048,128]{2,1,0:T(8,128)(2,1)S(1)} %constant_dynamic-update-slice_fusion.refs_0_), channel_id=1, source_target_pairs={{0,4},{4,0},{8,12},{12,8},{1,5},{5,1},{9,13},{13,9},{2,6},{6,2},{1... | collective-permute-start | bytes 1572872 | tf_op jit(solution)/shard_map/ppermute | solution.py:49
  62.1 25.6 %all-to-all-start = ((f32[32,1,128]{2,1,0:T(1,128)}), f32[32,1,128]{2,1,0:T(1,128)S(1)}, u32[]{:S(2)}, u32[]{:S(2)}) async-start(f32[32,1,128]{2,1,0:T(1,128)} %broadcast_in_dim.8), calls=%async_computation | async-start | bytes 32768 | tf_op jit(solution)/shard_map/all_to_all | solution.py:56
  69.8 32.5 %collective-permute-start.5 = (bf16[1,2048,128]{2,1,0:T(8,128)(2,1)}, bf16[1,2048,128]{2,1,0:T(8,128)(2,1)}, u32[]{:S(2)}, u32[]{:S(2)}) collective-permute-start(bf16[1,2048,128]{2,1,0:T(8,128)(2,1)} %collective-permute-done.4.refs_1_), channel_id=1, source_target_pairs={{0,12},{4,8},{8,4},{12,0},{1,13},{5,9},{9,5},{13,1},{2,14},{6,10},... | collective-permute-start | bytes 1572872 | tf_op jit(solution)/shard_map/ppermute | solution.py:49
  72.9 29.4 %collective-permute-start.6 = (bf16[1,2048,128]{2,1,0:T(8,128)(2,1)}, bf16[1,2048,128]{2,1,0:T(8,128)(2,1)}, u32[]{:S(2)}, u32[]{:S(2)}) collective-permute-start(bf16[1,2048,128]{2,1,0:T(8,128)(2,1)} %collective-permute-done.3.refs_0_), channel_id=1, source_target_pairs={{0,4},{4,0},{8,12},{12,8},{1,5},{5,1},{9,13},{13,9},{2,6},{6,2},{1... | collective-permute-start | bytes 1572872 | tf_op jit(solution)/shard_map/ppermute | solution.py:49
  77.1 25.3 %collective-permute-start.8 = (bf16[1,2048,128]{2,1,0:T(8,128)(2,1)}, bf16[1,2048,128]{2,1,0:T(8,128)(2,1)}, u32[]{:S(2)}, u32[]{:S(2)}) collective-permute-start(bf16[1,2048,128]{2,1,0:T(8,128)(2,1)} %collective-permute-done.7.refs_3_), channel_id=1, source_target_pairs={{0,12},{4,8},{8,4},{12,0},{1,13},{5,9},{9,5},{13,1},{2,14},{6,10},... | collective-permute-start | bytes 1572872 | tf_op jit(solution)/shard_map/ppermute | solution.py:49
  87.7 0.6 copy-start.7
  98.0 26.6 %collective-permute-start.15 = (bf16[1024,512]{1,0:T(8,128)(2,1)}, bf16[1024,512]{1,0:T(8,128)(2,1)}, u32[]{:S(2)}, u32[]{:S(2)}) collective-permute-start(bf16[1024,512]{1,0:T(8,128)(2,1)} %get-tuple-element.26), channel_id=1, source_target_pairs={{0,1},{1,0},{2,3},{3,2},{4,5},{5,4},{6,7},{7,6},{8,9},{9,8},{10,11... | collective-permute-start | bytes 3145736 | tf_op jit(solution)/shard_map/ppermute | solution.py:49
  112.2 23.6 %collective-permute-start.14 = (bf16[512,512]{1,0:T(8,128)(2,1)}, bf16[512,512]{1,0:T(8,128)(2,1)S(1)}, u32[]{:S(2)}, u32[]{:S(2)}) collective-permute-start(bf16[512,512]{1,0:T(8,128)(2,1)} %get-tuple-element.24), channel_id=1, source_target_pairs={{0,1},{1,0},{2,3},{3,2},{4,5},{5,4},{6,7},{7,6},{8,9},{9,8},{10,11... | collective-permute-start | bytes 1572872 | tf_op jit(solution)/shard_map/ppermute | solution.py:49
  114.2 30.0 %collective-permute-start.13 = (bf16[384,512]{1,0:T(8,128)(2,1)}, bf16[384,512]{1,0:T(8,128)(2,1)S(1)}, u32[]{:S(2)}, u32[]{:S(2)}) collective-permute-start(bf16[384,512]{1,0:T(8,128)(2,1)} %get-tuple-element.23), channel_id=1, source_target_pairs={{0,1},{1,0},{2,3},{3,2},{4,5},{5,4},{6,7},{7,6},{8,9},{9,8},{10,11... | collective-permute-start | bytes 1179656 | tf_op jit(solution)/shard_map/ppermute | solution.py:49
  114.3 31.6 %collective-permute-start.12 = (bf16[128,512]{1,0:T(8,128)(2,1)}, bf16[128,512]{1,0:T(8,128)(2,1)S(1)}, u32[]{:S(2)}, u32[]{:S(2)}) collective-permute-start(bf16[128,512]{1,0:T(8,128)(2,1)} %get-tuple-element.22), channel_id=1, source_target_pairs={{0,1},{1,0},{2,3},{3,2},{4,5},{5,4},{6,7},{7,6},{8,9},{9,8},{10,11... | collective-permute-start | bytes 393224 | tf_op jit(solution)/shard_map/ppermute | solution.py:49
  116.2 1.2 copy-start
  117.4 1.6 %copy-start.2 = (bf16[1,2048,512]{2,1,0:T(8,128)(2,1)S(1)}, bf16[1,2048,512]{2,1,0:T(8,128)(2,1)}, u32[]{:S(2)}) copy-start(bf16[1,2048,512]{2,1,0:T(8,128)(2,1)} %weight_ref.3) | copy-start | bytes 6291460
  119.0 1.2 copy-start.3
  120.2 1.5 %copy-start.1 = (bf16[1,1024,512]{2,1,0:T(8,128)(2,1)S(1)}, bf16[1,1024,512]{2,1,0:T(8,128)(2,1)}, u32[]{:S(2)}) copy-start(bf16[1,1024,512]{2,1,0:T(8,128)(2,1)} %right_ref.7) | copy-start | bytes 3145732
  120.2 1.5 %copy-start.4 = (bf16[1024,512]{1,0:T(8,128)(2,1)S(1)}, bf16[1024,512]{1,0:T(8,128)(2,1)}, u32[]{:S(2)}) copy-start(bf16[1024,512]{1,0:T(8,128)(2,1)} %get-tuple-element.21.turned_ref) | copy-start | bytes 3145732

commit v5 on v4

--- a/solution.py
+++ b/solution.py
@@ -25,7 +25,7 @@
 ANY = pl.BlockSpec(memory_space=pl.ANY)
 HBM = pl.BlockSpec(memory_space=pltpu.HBM)
 MIB = 1024 * 1024
-PIECES = ((0, 512), (512, 384), (896, 128))
+PIECES = ((0, 768), (768, 128), (896, 128))
 
 
 def cost(flops, bytes_accessed):
@@ -79,7 +79,7 @@
 
 def split(which, grad, block):
     _, _, width = grad.shape
-    rows = 512
+    rows = block
     steps = block // rows
     half = jax.ShapeDtypeStruct((1, block, width), bf16)
     chunk = pl.BlockSpec((1, rows, width), lambda s, b: (0, s, 0))
@@ -358,7 +358,7 @@
 def finish(which, base_term, received, start, total_rows, previous):
     block = base_term.shape[0]
     count, width = received.shape
-    rows = 128
+    rows = 256 if count % 256 == 0 else 128
     in_specs = [
         pl.BlockSpec((rows, width), lambda s, b: (start // rows + s, 0)),
         pl.BlockSpec((rows, width), lambda s, b: (s, 0)),

time: 147 us -> 146 us (level)
  Pallas kernels: 42.1 us -> 39.7 us
  waiting for transfers between devices: 61.6 us -> 63.6 us
    pallas_call x4, Pallas kernels: 8.75 us -> 6.35 us  [finish(): pl.pallas_call(finish_kernel, grid_spec=pltpu.PrefetchScalarGridSpec(num_...]
    ppermute x16, waiting for transfers between devices: 52.3 us -> 54.4 us  [permute(): return lax.ppermute(value, axis, pairs)]
  transfers between devices with their start and end apart: 17 -> 17, of which waited for: 7 -> 9; matrix products, arithmetic and copies ran while one was open for 2% -> 2% of each run, Pallas kernels for 28% -> 27%
where the time goes in v5:
time: 146 us; the launch traced here: 145 us
  waiting for transfers between devices  63.6 us (44%)
  Pallas kernels  39.7 us (27%)
  starting transfers between devices  33.9 us (23%)
  local copies, waits for them, and re-layouts  6.32 us (4%)
    ppermute x16, waiting for transfers between devices, permute(): return lax.ppermute(value, axis, pairs)  54.4 us
    ppermute x16, starting transfers between devices, permute(): return lax.ppermute(value, axis, pairs)  27.3 us
    pallas_call x2, Pallas kernels, moments(): pl.pallas_call(functools.partial(moments_kernel, is_near, count, pieces),...  19.5 us
    all_to_all x1, waiting for transfers between devices, every_sum(): lax.all_to_all(jnp.broadcast_to(value, (lax.axis_size(axes), 1, 128)), ax...  9.2 us
    pallas_call x2, Pallas kernels, rotate_right(): pl.pallas_call(rotate_right_kernel, out_shape=jax.ShapeDtypeStruct((block...  7.83 us
    all_to_all x1, starting transfers between devices, every_sum(): lax.all_to_all(jnp.broadcast_to(value, (lax.axis_size(axes), 1, 128)), ax...  6.67 us
    pallas_call x4, Pallas kernels, finish(): pl.pallas_call(finish_kernel, grid_spec=pltpu.PrefetchScalarGridSpec(num_...  6.35 us
    unnamed x17, local copies, waits for them, and re-layouts  4.72 us
  transfers between devices with their start and end apart: 17, of which 9 were waited for; matrix products, arithmetic and copies ran while one was open for 2% of the time, Pallas kernels for 27%

profile of v5, /device:TPU:0, one launch (start us, length us, event | category | flops | bytes accessed | tf_op | source)
XLA Modules:
  0.0 145.0 jit_solution(13311663683159511513)
XLA Ops:
  0.6 1.8 %collective-permute-start.2 = (bf16[1,1024,128]{2,1,0:T(8,128)(2,1)}, bf16[1,1024,128]{2,1,0:T(8,128)(2,1)}, u32[]{:S(2)}, u32[]{:S(2)}) collective-permute-start(bf16[1,1024,128]{2,1,0:T(8,128)(2,1)} %param.10), channel_id=1, source_target_pairs={{0,1},{1,0},{2,3},{3,2},{4,5},{5,4},{6,7},{7,6},{8,9},{9,8},{10,11... | collective-permute-start | bytes 786440 | tf_op jit(solution)/shard_map/ppermute | solution.py:49
  2.4 3.1 %split.1 = (bf16[1,1024,512]{2,1,0:T(8,128)(2,1)}, bf16[1,1024,512]{2,1,0:T(8,128)(2,1)}, f32[1,1,128]{2,1,0:T(1,128)}) custom-call(s32[1]{0:T(128)} %bitcast.1.block_ref, bf16[1,2048,512]{2,1,0:T(8,128)(2,1)} %second_ref.1, bf16[1,2048,512]{2,1,0:T(8,128)(2,1)} %second_ref.1), custom_call_target="tpu_custom_call" | custom-call | flops 2097152 | bytes 4194304 | tf_op jit(solution)/shard_map/split/pallas_call | solution.py:86
  5.5 0.3 collective-permute-start.11
  5.8 4.3 %collective-permute-done.2 = bf16[1,1024,128]{2,1,0:T(8,128)(2,1)} collective-permute-done((bf16[1,1024,128]{2,1,0:T(8,128)(2,1)}, bf16[1,1024,128]{2,1,0:T(8,128)(2,1)}, u32[]{:S(2)}, u32[]{:S(2)}) %collective-permute-start.2) | collective-permute-done | bytes 262176 | tf_op jit(solution)/shard_map/ppermute | solution.py:49
  10.1 1.0 constant_dynamic-update-slice_fusion.refs_0_
  11.1 3.3 %collective-permute-start.4 = (bf16[1,2048,128]{2,1,0:T(8,128)(2,1)S(1)}, bf16[1,2048,128]{2,1,0:T(8,128)(2,1)}, u32[]{:S(2)}, u32[]{:S(2)}) collective-permute-start(bf16[1,2048,128]{2,1,0:T(8,128)(2,1)S(1)} %constant_dynamic-update-slice_fusion.refs_0_), channel_id=1, source_target_pairs={{0,3},{1,2},{2,1},{3,0},{4,7},{5,6},{6,5},{7,4},{8,11},{9,10},{10,... | collective-permute-start | bytes 1572872 | tf_op jit(solution)/shard_map/ppermute | solution.py:49
  14.4 4.0 %collective-permute-start.3 = (bf16[1,2048,128]{2,1,0:T(8,128)(2,1)S(1)}, bf16[1,2048,128]{2,1,0:T(8,128)(2,1)}, u32[]{:S(2)}, u32[]{:S(2)}) collective-permute-start(bf16[1,2048,128]{2,1,0:T(8,128)(2,1)S(1)} %constant_dynamic-update-slice_fusion.refs_0_), channel_id=1, source_target_pairs={{0,12},{4,8},{8,4},{12,0},{1,13},{5,9},{9,5},{13,1},{2,14},{6,10},... | collective-permute-start | bytes 1572872 | tf_op jit(solution)/shard_map/ppermute | solution.py:49
  18.4 6.0 %collective-permute-done.4.refs_1_ = bf16[1,2048,128]{2,1,0:T(8,128)(2,1)} collective-permute-done((bf16[1,2048,128]{2,1,0:T(8,128)(2,1)S(1)}, bf16[1,2048,128]{2,1,0:T(8,128)(2,1)}, u32[]{:S(2)}, u32[]{:S(2)}) %collective-permute-start.4) | collective-permute-done | bytes 524320 | tf_op jit(solution)/shard_map/ppermute | solution.py:49
  24.4 1.9 %collective-permute-start.7 = (bf16[1,2048,128]{2,1,0:T(8,128)(2,1)}, bf16[1,2048,128]{2,1,0:T(8,128)(2,1)}, u32[]{:S(2)}, u32[]{:S(2)}) collective-permute-start(bf16[1,2048,128]{2,1,0:T(8,128)(2,1)} %collective-permute-done.4.refs_1_), channel_id=1, source_target_pairs={{0,4},{4,0},{8,12},{12,8},{1,5},{5,1},{9,13},{13,9},{2,6},{6,2},{1... | collective-permute-start | bytes 1572872 | tf_op jit(solution)/shard_map/ppermute | solution.py:49
  26.4 0.3 collective-permute-start.9
  26.7 1.7 %collective-permute-start = (f32[1,1,128]{2,1,0:T(1,128)}, f32[1,1,128]{2,1,0:T(1,128)S(1)}, u32[]{:S(2)}, u32[]{:S(2)}) collective-permute-start(f32[1,1,128]{2,1,0:T(1,128)} %get-tuple-element.16), channel_id=1, source_target_pairs={{0,1},{1,0},{2,3},{3,2},{4,5},{5,4},{6,7},{7,6},{8,9},{9,8},{10,11... | collective-permute-start | bytes 1544 | tf_op jit(solution)/shard_map/ppermute | solution.py:49
  28.4 25.6 %collective-permute-done = f32[1,1,128]{2,1,0:T(1,128)S(1)} collective-permute-done((f32[1,1,128]{2,1,0:T(1,128)}, f32[1,1,128]{2,1,0:T(1,128)S(1)}, u32[]{:S(2)}, u32[]{:S(2)}) %collective-permute-start) | collective-permute-done | bytes 544 | tf_op jit(solution)/shard_map/ppermute | solution.py:49
  54.0 0.7 add.7
  54.6 3.2 %collective-permute-start.1 = (f32[1,1,128]{2,1,0:T(1,128)S(1)}, f32[1,1,128]{2,1,0:T(1,128)S(1)}, u32[]{:S(2)}, u32[]{:S(2)}) collective-permute-start(f32[1,1,128]{2,1,0:T(1,128)S(1)} %add.7), channel_id=1, source_target_pairs={{0,3},{1,2},{2,1},{3,0},{4,7},{5,6},{6,5},{7,4},{8,11},{9,10},{10,... | collective-permute-start | bytes 1544 | tf_op jit(solution)/shard_map/ppermute | solution.py:49
  57.8 1.6 %collective-permute-done.1 = f32[1,1,128]{2,1,0:T(1,128)S(1)} collective-permute-done((f32[1,1,128]{2,1,0:T(1,128)S(1)}, f32[1,1,128]{2,1,0:T(1,128)S(1)}, u32[]{:S(2)}, u32[]{:S(2)}) %collective-permute-start.1) | collective-permute-done | bytes 544 | tf_op jit(solution)/shard_map/ppermute | solution.py:49
  59.4 2.1 %collective-permute-start.10 = (bf16[1,2048,128]{2,1,0:T(8,128)(2,1)S(1)}, bf16[1,2048,128]{2,1,0:T(8,128)(2,1)}, u32[]{:S(2)}, u32[]{:S(2)}) collective-permute-start(bf16[1,2048,128]{2,1,0:T(8,128)(2,1)S(1)} %constant_dynamic-update-slice_fusion.refs_0_), channel_id=1, source_target_pairs={{0,4},{4,0},{8,12},{12,8},{1,5},{5,1},{9,13},{13,9},{2,6},{6,2},{1... | collective-permute-start | bytes 1572872 | tf_op jit(solution)/shard_map/ppermute | solution.py:49
  61.5 2.5 %collective-permute-start.5 = (bf16[1,2048,128]{2,1,0:T(8,128)(2,1)}, bf16[1,2048,128]{2,1,0:T(8,128)(2,1)}, u32[]{:S(2)}, u32[]{:S(2)}) collective-permute-start(bf16[1,2048,128]{2,1,0:T(8,128)(2,1)} %collective-permute-done.4.refs_1_), channel_id=1, source_target_pairs={{0,12},{4,8},{8,4},{12,0},{1,13},{5,9},{9,5},{13,1},{2,14},{6,10},... | collective-permute-start | bytes 1572872 | tf_op jit(solution)/shard_map/ppermute | solution.py:49
  64.0 1.0 collective-permute-start.6
  65.0 0.0 collective-permute-done.7.refs_3_
  65.0 0.7 collective-permute-start.8
  65.7 0.6 broadcast_in_dim.8
  66.3 6.7 %all-to-all-start = ((f32[32,1,128]{2,1,0:T(1,128)}), f32[32,1,128]{2,1,0:T(1,128)S(1)}, u32[]{:S(2)}, u32[]{:S(2)}) async-start(f32[32,1,128]{2,1,0:T(1,128)} %broadcast_in_dim.8), calls=%async_computation | async-start | bytes 32768 | tf_op jit(solution)/shard_map/all_to_all | solution.py:56
  73.0 3.9 %shard_map.86.refs_4_ = bf16[1024,512]{1,0:T(8,128)(2,1)} custom-call(bf16[1,1024,512]{2,1,0:T(8,128)(2,1)} %get-tuple-element.18.own_ref, bf16[1,1024,512]{2,1,0:T(8,128)(2,1)} %collective-permute-done.11.other_ref, bf16[1,1024,512]{2,1,0:T(8,128)(2,1)} %right_ref.7), custom_call_target="tpu_custom_call" | custom-call | flops 1073741824 | bytes 4194304 | tf_op jit(solution)/shard_map/pallas_call | solution.py:169
  77.0 9.2 %all-to-all-done.sums_ref = f32[32,1,128]{2,1,0:T(1,128)S(1)} async-done(((f32[32,1,128]{2,1,0:T(1,128)}), f32[32,1,128]{2,1,0:T(1,128)S(1)}, u32[]{:S(2)}, u32[]{:S(2)}) %all-to-all-start) | async-done | bytes 16416 | tf_op jit(solution)/shard_map/all_to_all | solution.py:56
  86.2 0.0 collective-permute-done.10.refs_2_
  86.2 0.6 copy-done.7
  86.8 9.7 %shard_map.87 = (f32[1,2048,512]{2,1,0:T(8,128)}, f32[1,2048,512]{2,1,0:T(8,128)}, bf16[1024,512]{1,0:T(8,128)(2,1)}, bf16[1024,512]{1,0:T(8,128)(2,1)}) custom-call(s32[1]{0:T(128)} %bitcast.1.block_ref, f32[32,1,128]{2,1,0:T(1,128)} %copy-done.7, bf16[1,2048,128]{2,1,0:T(8,128)(2,1)} %copy-done.5, bf16[1,2048,128]{2,1,0:T(8,128)(2,1)} %collective-permute-done.4.refs_1_, ...), custom_call_target="tpu_custom_call" | custom-call | flops 2684354560 | bytes 10485760 | tf_op jit(solution)/shard_map/pallas_call | solution.py:299
  96.5 0.6 collective-permute-start.15
  97.1 0.0 collective-permute-done.9.other_ref
  97.1 3.9 %shard_map.85.refs_4_ = bf16[1024,512]{1,0:T(8,128)(2,1)} custom-call(bf16[1,1024,512]{2,1,0:T(8,128)(2,1)} %get-tuple-element.17.own_ref, bf16[1,1024,512]{2,1,0:T(8,128)(2,1)} %collective-permute-done.9.other_ref, bf16[1,1024,512]{2,1,0:T(8,128)(2,1)} %right_ref.7), custom_call_target="tpu_custom_call" | custom-call | flops 1073741824 | bytes 4194304 | tf_op jit(solution)/shard_map/pallas_call | solution.py:169
  101.0 9.8 %shard_map.88 = (f32[1,2048,512]{2,1,0:T(8,128)}, f32[1,2048,512]{2,1,0:T(8,128)}, bf16[1024,512]{1,0:T(8,128)(2,1)}, bf16[768,512]{1,0:T(8,128)(2,1)}, bf16[128...) custom-call(s32[1]{0:T(128)} %bitcast.block_ref, ...), custom_call_target="tpu_custom_call", output_to_operand_aliasing={{0}: (10, {}), {1}: (11, {})} | custom-call | flops 2684354560 | bytes 10485760 | tf_op jit(solution)/shard_map/pallas_call | solution.py:299
  110.8 1.8 %collective-permute-start.14 = (bf16[768,512]{1,0:T(8,128)(2,1)}, bf16[768,512]{1,0:T(8,128)(2,1)S(1)}, u32[]{:S(2)}, u32[]{:S(2)}) collective-permute-start(bf16[768,512]{1,0:T(8,128)(2,1)} %get-tuple-element.24), channel_id=1, source_target_pairs={{0,1},{1,0},{2,3},{3,2},{4,5},{5,4},{6,7},{7,6},{8,9},{9,8},{10,11... | collective-permute-start | bytes 2359304 | tf_op jit(solution)/shard_map/ppermute | solution.py:49
  112.6 0.3 collective-permute-start.13
  112.9 1.7 %collective-permute-start.12 = (bf16[128,512]{1,0:T(8,128)(2,1)}, bf16[128,512]{1,0:T(8,128)(2,1)S(1)}, u32[]{:S(2)}, u32[]{:S(2)}) collective-permute-start(bf16[128,512]{1,0:T(8,128)(2,1)} %get-tuple-element.22), channel_id=1, source_target_pairs={{0,1},{1,0},{2,3},{3,2},{4,5},{5,4},{6,7},{7,6},{8,9},{9,8},{10,11... | collective-permute-start | bytes 393224 | tf_op jit(solution)/shard_map/ppermute | solution.py:49
  114.7 1.2 copy-done
  115.9 1.6 %copy-done.2 = bf16[1,2048,512]{2,1,0:T(8,128)(2,1)S(1)} copy-done((bf16[1,2048,512]{2,1,0:T(8,128)(2,1)S(1)}, bf16[1,2048,512]{2,1,0:T(8,128)(2,1)}, u32[]{:S(2)}) %copy-start.2) | copy-done | bytes 2097176
  117.5 1.2 copy-done.3
  118.7 1.5 %shard_map.90.base_ref = f32[1024,512]{1,0:T(8,128)S(1)} custom-call(s32[1]{0:T(128)} %bitcast.1.block_ref, bf16[1024,512]{1,0:T(8,128)(2,1)S(1)} %copy-done.3, bf16[1,1024,512]{2,1,0:T(8,128)(2,1)S(1)} %copy-done, bf16[1,2048,512]{2,1,0:T(8,128)(2,1)S(1)} %copy-done.2), custom_call_target="tpu_custom_call" | custom-call | flops 536870912 | bytes 5242880 | tf_op jit(solution)/shard_map/pallas_call | solution.py:336
  120.2 0.1 copy-done.4
  120.2 1.5 %shard_map.89.base_ref = f32[1024,512]{1,0:T(8,128)S(1)} custom-call(s32[1]{0:T(128)} %bitcast.block_ref, bf16[1024,512]{1,0:T(8,128)(2,1)S(1)} %copy-done.4, bf16[1,1024,512]{2,1,0:T(8,128)(2,1)S(1)} %copy-done.1, bf16[1,2048,512]{2,1,0:T(8,128)(2,1)S(1)} %copy-done.2), custom_call_target="tpu_custom_call" | custom-call | flops 536870912 | bytes 5242880 | tf_op jit(solution)/shard_map/pallas_call | solution.py:336
  121.7 1.4 collective-permute-done.15.received_ref
  123.1 3.4 %shard_map.91.refs_0_ = bf16[1,2048,512]{2,1,0:T(8,128)(2,1)} custom-call(s32[1]{0:T(128)} %bitcast.1.block_ref, f32[1024,512]{1,0:T(8,128)S(1)} %shard_map.90.base_ref, bf16[1024,512]{1,0:T(8,128)(2,1)} %collective-permute-done.15.received_ref), custom_call_target="tpu_custom_call" | custom-call | flops 1048576 | bytes 4194304 | tf_op jit(solution)/shard_map/pallas_call | solution.py:372
  126.6 13.3 %collective-permute-done.14.received_ref = bf16[768,512]{1,0:T(8,128)(2,1)S(1)} collective-permute-done((bf16[768,512]{1,0:T(8,128)(2,1)}, bf16[768,512]{1,0:T(8,128)(2,1)S(1)}, u32[]{:S(2)}, u32[]{:S(2)}) %collective-permute-start.14) | collective-permute-done | bytes 786464 | tf_op jit(solution)/shard_map/ppermute | solution.py:49
  139.9 1.5 %shard_map.92.refs_0_ = bf16[1,2048,512]{2,1,0:T(8,128)(2,1)} custom-call(s32[1]{0:T(128)} %bitcast.block_ref, f32[1024,512]{1,0:T(8,128)S(1)} %shard_map.89.base_ref, bf16[768,512]{1,0:T(8,128)(2,1)S(1)} %collective-permute-done.14.received_ref, bf16[1,2048,512]{2,1,0:T(8,128)(2,1)} %shard_map.91.refs_0_), custom_call_target="tpu_custom_call", output_to_operand_aliasing={{}: (3, {})} | custom-call | flops 786432 | bytes 3145728 | tf_op jit(solution)/shard_map/pallas_call | solution.py:372
  141.4 1.3 collective-permute-done.13.received_ref
  142.7 0.7 shard_map.93.refs_0_
  143.4 1.0 collective-permute-done.12.received_ref
  144.3 0.7 shard_map.94
  (18 shorter events, 0.1 us)
Async XLA Ops:
  0.6 9.5 %collective-permute-start.2 = (bf16[1,1024,128]{2,1,0:T(8,128)(2,1)}, bf16[1,1024,128]{2,1,0:T(8,128)(2,1)}, u32[]{:S(2)}, u32[]{:S(2)}) collective-permute-start(bf16[1,1024,128]{2,1,0:T(8,128)(2,1)} %param.10), channel_id=1, source_target_pairs={{0,1},{1,0},{2,3},{3,2},{4,5},{5,4},{6,7},{7,6},{8,9},{9,8},{10,11... | collective-permute-start | bytes 786440 | tf_op jit(solution)/shard_map/ppermute | solution.py:49
  2.4 3.4 %copy-start.6 = (bf16[1,1024,128]{2,1,0:T(8,128)(2,1)S(1)}, bf16[1,1024,128]{2,1,0:T(8,128)(2,1)}, u32[]{:S(2)}) copy-start(bf16[1,1024,128]{2,1,0:T(8,128)(2,1)} %param.10) | copy-start | bytes 786436
  5.5 58.5 %collective-permute-start.11 = (bf16[1,1024,512]{2,1,0:T(8,128)(2,1)}, bf16[1,1024,512]{2,1,0:T(8,128)(2,1)}, u32[]{:S(2)}, u32[]{:S(2)}) collective-permute-start(bf16[1,1024,512]{2,1,0:T(8,128)(2,1)} %get-tuple-element.18.own_ref), channel_id=1, source_target_pairs={{0,1},{1,0},{2,3},{3,2},{4,5},{5,4},{6,7},{7,6},{8,9},{9,8},{10,11... | collective-permute-start | bytes 3145736 | tf_op jit(solution)/shard_map/ppermute | solution.py:49
  11.1 65.9 %copy-start.5 = (bf16[1,2048,128]{2,1,0:T(8,128)(2,1)}, bf16[1,2048,128]{2,1,0:T(8,128)(2,1)S(1)}, u32[]{:S(2)}) copy-start(bf16[1,2048,128]{2,1,0:T(8,128)(2,1)S(1)} %constant_dynamic-update-slice_fusion.refs_0_) | copy-start | bytes 1572868
  11.1 13.3 %collective-permute-start.4 = (bf16[1,2048,128]{2,1,0:T(8,128)(2,1)S(1)}, bf16[1,2048,128]{2,1,0:T(8,128)(2,1)}, u32[]{:S(2)}, u32[]{:S(2)}) collective-permute-start(bf16[1,2048,128]{2,1,0:T(8,128)(2,1)S(1)} %constant_dynamic-update-slice_fusion.refs_0_), channel_id=1, source_target_pairs={{0,3},{1,2},{2,1},{3,0},{4,7},{5,6},{6,5},{7,4},{8,11},{9,10},{10,... | collective-permute-start | bytes 1572872 | tf_op jit(solution)/shard_map/ppermute | solution.py:49
  14.4 47.1 %collective-permute-start.3 = (bf16[1,2048,128]{2,1,0:T(8,128)(2,1)S(1)}, bf16[1,2048,128]{2,1,0:T(8,128)(2,1)}, u32[]{:S(2)}, u32[]{:S(2)}) collective-permute-start(bf16[1,2048,128]{2,1,0:T(8,128)(2,1)S(1)} %constant_dynamic-update-slice_fusion.refs_0_), channel_id=1, source_target_pairs={{0,12},{4,8},{8,4},{12,0},{1,13},{5,9},{9,5},{13,1},{2,14},{6,10},... | collective-permute-start | bytes 1572872 | tf_op jit(solution)/shard_map/ppermute | solution.py:49
  24.4 40.6 %collective-permute-start.7 = (bf16[1,2048,128]{2,1,0:T(8,128)(2,1)}, bf16[1,2048,128]{2,1,0:T(8,128)(2,1)}, u32[]{:S(2)}, u32[]{:S(2)}) collective-permute-start(bf16[1,2048,128]{2,1,0:T(8,128)(2,1)} %collective-permute-done.4.refs_1_), channel_id=1, source_target_pairs={{0,4},{4,0},{8,12},{12,8},{1,5},{5,1},{9,13},{13,9},{2,6},{6,2},{1... | collective-permute-start | bytes 1572872 | tf_op jit(solution)/shard_map/ppermute | solution.py:49
  26.4 70.7 %collective-permute-start.9 = (bf16[1,1024,512]{2,1,0:T(8,128)(2,1)}, bf16[1,1024,512]{2,1,0:T(8,128)(2,1)}, u32[]{:S(2)}, u32[]{:S(2)}) collective-permute-start(bf16[1,1024,512]{2,1,0:T(8,128)(2,1)} %get-tuple-element.17.own_ref), channel_id=1, source_target_pairs={{0,1},{1,0},{2,3},{3,2},{4,5},{5,4},{6,7},{7,6},{8,9},{9,8},{10,11... | collective-permute-start | bytes 3145736 | tf_op jit(solution)/shard_map/ppermute | solution.py:49
  26.7 27.3 %collective-permute-start = (f32[1,1,128]{2,1,0:T(1,128)}, f32[1,1,128]{2,1,0:T(1,128)S(1)}, u32[]{:S(2)}, u32[]{:S(2)}) collective-permute-start(f32[1,1,128]{2,1,0:T(1,128)} %get-tuple-element.16), channel_id=1, source_target_pairs={{0,1},{1,0},{2,3},{3,2},{4,5},{5,4},{6,7},{7,6},{8,9},{9,8},{10,11... | collective-permute-start | bytes 1544 | tf_op jit(solution)/shard_map/ppermute | solution.py:49
  54.6 4.8 %collective-permute-start.1 = (f32[1,1,128]{2,1,0:T(1,128)S(1)}, f32[1,1,128]{2,1,0:T(1,128)S(1)}, u32[]{:S(2)}, u32[]{:S(2)}) collective-permute-start(f32[1,1,128]{2,1,0:T(1,128)S(1)} %add.7), channel_id=1, source_target_pairs={{0,3},{1,2},{2,1},{3,0},{4,7},{5,6},{6,5},{7,4},{8,11},{9,10},{10,... | collective-permute-start | bytes 1544 | tf_op jit(solution)/shard_map/ppermute | solution.py:49
  59.4 26.8 %collective-permute-start.10 = (bf16[1,2048,128]{2,1,0:T(8,128)(2,1)S(1)}, bf16[1,2048,128]{2,1,0:T(8,128)(2,1)}, u32[]{:S(2)}, u32[]{:S(2)}) collective-permute-start(bf16[1,2048,128]{2,1,0:T(8,128)(2,1)S(1)} %constant_dynamic-update-slice_fusion.refs_0_), channel_id=1, source_target_pairs={{0,4},{4,0},{8,12},{12,8},{1,5},{5,1},{9,13},{13,9},{2,6},{6,2},{1... | collective-permute-start | bytes 1572872 | tf_op jit(solution)/shard_map/ppermute | solution.py:49
  61.5 39.5 %collective-permute-start.5 = (bf16[1,2048,128]{2,1,0:T(8,128)(2,1)}, bf16[1,2048,128]{2,1,0:T(8,128)(2,1)}, u32[]{:S(2)}, u32[]{:S(2)}) collective-permute-start(bf16[1,2048,128]{2,1,0:T(8,128)(2,1)} %collective-permute-done.4.refs_1_), channel_id=1, source_target_pairs={{0,12},{4,8},{8,4},{12,0},{1,13},{5,9},{9,5},{13,1},{2,14},{6,10},... | collective-permute-start | bytes 1572872 | tf_op jit(solution)/shard_map/ppermute | solution.py:49
  64.0 37.0 %collective-permute-start.6 = (bf16[1,2048,128]{2,1,0:T(8,128)(2,1)}, bf16[1,2048,128]{2,1,0:T(8,128)(2,1)}, u32[]{:S(2)}, u32[]{:S(2)}) collective-permute-start(bf16[1,2048,128]{2,1,0:T(8,128)(2,1)} %collective-permute-done.3.refs_0_), channel_id=1, source_target_pairs={{0,4},{4,0},{8,12},{12,8},{1,5},{5,1},{9,13},{13,9},{2,6},{6,2},{1... | collective-permute-start | bytes 1572872 | tf_op jit(solution)/shard_map/ppermute | solution.py:49
  65.0 36.0 %collective-permute-start.8 = (bf16[1,2048,128]{2,1,0:T(8,128)(2,1)}, bf16[1,2048,128]{2,1,0:T(8,128)(2,1)}, u32[]{:S(2)}, u32[]{:S(2)}) collective-permute-start(bf16[1,2048,128]{2,1,0:T(8,128)(2,1)} %collective-permute-done.7.refs_3_), channel_id=1, source_target_pairs={{0,12},{4,8},{8,4},{12,0},{1,13},{5,9},{9,5},{13,1},{2,14},{6,10},... | collective-permute-start | bytes 1572872 | tf_op jit(solution)/shard_map/ppermute | solution.py:49
  66.3 19.8 %all-to-all-start = ((f32[32,1,128]{2,1,0:T(1,128)}), f32[32,1,128]{2,1,0:T(1,128)S(1)}, u32[]{:S(2)}, u32[]{:S(2)}) async-start(f32[32,1,128]{2,1,0:T(1,128)} %broadcast_in_dim.8), calls=%async_computation | async-start | bytes 32768 | tf_op jit(solution)/shard_map/all_to_all | solution.py:56
  86.2 0.6 copy-start.7
  96.5 26.6 %collective-permute-start.15 = (bf16[1024,512]{1,0:T(8,128)(2,1)}, bf16[1024,512]{1,0:T(8,128)(2,1)}, u32[]{:S(2)}, u32[]{:S(2)}) collective-permute-start(bf16[1024,512]{1,0:T(8,128)(2,1)} %get-tuple-element.26), channel_id=1, source_target_pairs={{0,1},{1,0},{2,3},{3,2},{4,5},{5,4},{6,7},{7,6},{8,9},{9,8},{10,11... | collective-permute-start | bytes 3145736 | tf_op jit(solution)/shard_map/ppermute | solution.py:49
  110.8 29.0 %collective-permute-start.14 = (bf16[768,512]{1,0:T(8,128)(2,1)}, bf16[768,512]{1,0:T(8,128)(2,1)S(1)}, u32[]{:S(2)}, u32[]{:S(2)}) collective-permute-start(bf16[768,512]{1,0:T(8,128)(2,1)} %get-tuple-element.24), channel_id=1, source_target_pairs={{0,1},{1,0},{2,3},{3,2},{4,5},{5,4},{6,7},{7,6},{8,9},{9,8},{10,11... | collective-permute-start | bytes 2359304 | tf_op jit(solution)/shard_map/ppermute | solution.py:49
  112.6 30.0 %collective-permute-start.13 = (bf16[128,512]{1,0:T(8,128)(2,1)}, bf16[128,512]{1,0:T(8,128)(2,1)S(1)}, u32[]{:S(2)}, u32[]{:S(2)}) collective-permute-start(bf16[128,512]{1,0:T(8,128)(2,1)} %get-tuple-element.23), channel_id=1, source_target_pairs={{0,1},{1,0},{2,3},{3,2},{4,5},{5,4},{6,7},{7,6},{8,9},{9,8},{10,11... | collective-permute-start | bytes 393224 | tf_op jit(solution)/shard_map/ppermute | solution.py:49
  112.9 31.4 %collective-permute-start.12 = (bf16[128,512]{1,0:T(8,128)(2,1)}, bf16[128,512]{1,0:T(8,128)(2,1)S(1)}, u32[]{:S(2)}, u32[]{:S(2)}) collective-permute-start(bf16[128,512]{1,0:T(8,128)(2,1)} %get-tuple-element.22), channel_id=1, source_target_pairs={{0,1},{1,0},{2,3},{3,2},{4,5},{5,4},{6,7},{7,6},{8,9},{9,8},{10,11... | collective-permute-start | bytes 393224 | tf_op jit(solution)/shard_map/ppermute | solution.py:49
  114.7 1.2 copy-start
  115.9 1.6 %copy-start.2 = (bf16[1,2048,512]{2,1,0:T(8,128)(2,1)S(1)}, bf16[1,2048,512]{2,1,0:T(8,128)(2,1)}, u32[]{:S(2)}) copy-start(bf16[1,2048,512]{2,1,0:T(8,128)(2,1)} %weight_ref.3) | copy-start | bytes 6291460
  117.5 1.2 copy-start.3
  118.7 1.5 %copy-start.1 = (bf16[1,1024,512]{2,1,0:T(8,128)(2,1)S(1)}, bf16[1,1024,512]{2,1,0:T(8,128)(2,1)}, u32[]{:S(2)}) copy-start(bf16[1,1024,512]{2,1,0:T(8,128)(2,1)} %right_ref.7) | copy-start | bytes 3145732
  118.7 1.5 %copy-start.4 = (bf16[1024,512]{1,0:T(8,128)(2,1)S(1)}, bf16[1024,512]{1,0:T(8,128)(2,1)}, u32[]{:S(2)}) copy-start(bf16[1024,512]{1,0:T(8,128)(2,1)} %get-tuple-element.21.turned_ref) | copy-start | bytes 3145732
